TPU v7x, 32 devices: a 4x4x1 block of a 4x4x8 slice. The times are simulated.
32 devices in a mesh: dp: 1 (over z), cp: 4 (over y), tp: 8 (over x, core).
Axes of the slice: x: 4, y: 4, z: 1, core: 2. Of those that a mesh axis runs over, the one named last changes fastest.
The devices are a block of a 4x4x8 slice.
Arguments:
- x_tok: bfloat16 [16384, 2048], P(('dp', 'cp', 'tp'))
- w_q: bfloat16 [2048, 16, 128], P(None, 'tp')
- w_k: bfloat16 [2048, 16, 128], P(None, 'tp')
- w_v: bfloat16 [2048, 16, 128], P(None, 'tp')
- w_o: bfloat16 [16, 128, 2048], P('tp')
- expert_ids: int32 [16384, 8], P(('dp', 'cp', 'tp'))
- gate_wts: float32 [16384, 8], P(('dp', 'cp', 'tp'))
- w_gate: bfloat16 [128, 2048, 512], P(('cp', 'tp'))
- w_up: bfloat16 [128, 2048, 512], P(('cp', 'tp'))
- w_down: bfloat16 [128, 512, 2048], P(('cp', 'tp'))
Outputs:
- output: bfloat16 [16384, 2048], P(('dp', 'cp', 'tp'))
All inputs are finite; a program needn't handle non-finite values.
Results may differ from a plain program's by a relative error of at most 0.0115601.
Values are sent between devices in bfloat16 or wider.
A program may use at most 768 MiB of HBM per device.

v0:
```python
import jax
import jax.numpy as jnp
from jax import lax
from jax.sharding import PartitionSpec as P


def seq_positions(cp_index, n_cp, half_len):
    chunk_len = half_len // 2
    in_half = jnp.arange(half_len)
    return jnp.where(in_half < chunk_len, cp_index * chunk_len + in_half, (2 * n_cp - 1 - cp_index) * chunk_len + in_half - chunk_len)


def attend_block(q_loc, k_blk, v_blk, q_pos, k_pos, run_max, run_sum, run_acc):
    head_dim = q_loc.shape[-1]
    scores = jnp.einsum("qgrd,kgd->grqk", q_loc, k_blk, preferred_element_type=jnp.float32) * (head_dim ** -0.5)
    allowed = q_pos[:, None] >= k_pos[None, :]
    scores = jnp.where(allowed, scores, -1e30)
    new_max = jnp.maximum(run_max, jnp.max(scores, axis=-1))
    prob_vals = jnp.exp(scores - new_max[..., None])
    rescale = jnp.exp(run_max - new_max)
    new_sum = run_sum * rescale + jnp.sum(prob_vals, axis=-1)
    new_acc = run_acc * rescale[..., None] + jnp.einsum("grqk,kgd->grqd", prob_vals.astype(jnp.bfloat16), v_blk, preferred_element_type=jnp.float32)
    return new_max, new_sum, new_acc


def solution(mesh):
    n_cp = mesh.shape["cp"]
    n_tp = mesh.shape["tp"]
    row_spec = P(("dp", "cp", "tp"), None)
    head_spec = P(None, "tp", None)
    expert_spec = P(("cp", "tp"), None, None)

    def device_step(x_loc, w_q, w_k, w_v, w_o, ids_loc, gates_loc, w_gate, w_up, w_down):
        tok_dev, hid_dim = x_loc.shape
        top_k = ids_loc.shape[1]
        kv_loc = w_k.shape[1]
        head_dim = w_q.shape[2]
        grp_size = w_q.shape[1] // kv_loc
        local_exp = w_gate.shape[0]
        n_experts = local_exp * n_cp * n_tp // 2
        capacity = top_k * tok_dev // n_experts
        half_hid = hid_dim // 2
        cp_index = lax.axis_index("cp")
        tp_index = lax.axis_index("tp")

        x_half = lax.all_gather(x_loc, "tp", axis=0, tiled=True)
        half_len = x_half.shape[0]
        q_loc = jnp.einsum("sh,hnd->snd", x_half, w_q, preferred_element_type=jnp.float32).astype(jnp.bfloat16).reshape(half_len, kv_loc, grp_size, head_dim)
        k_cur = jnp.einsum("sh,hnd->snd", x_half, w_k, preferred_element_type=jnp.float32).astype(jnp.bfloat16)
        v_cur = jnp.einsum("sh,hnd->snd", x_half, w_v, preferred_element_type=jnp.float32).astype(jnp.bfloat16)
        q_pos = seq_positions(cp_index, n_cp, half_len)
        init_max = jnp.full((kv_loc, grp_size, half_len), -1e30, jnp.float32)
        init_sum = jnp.zeros((kv_loc, grp_size, half_len), jnp.float32)
        init_acc = jnp.zeros((kv_loc, grp_size, half_len, head_dim), jnp.float32)
        first_state = attend_block(q_loc, k_cur, v_cur, q_pos, q_pos, init_max, init_sum, init_acc)
        shift_perm = [(src_dev, (src_dev + 1) % n_cp) for src_dev in range(n_cp)]

        def kv_step(step_idx, kv_state):
            k_blk, v_blk, cur_max, cur_sum, cur_acc = kv_state
            k_blk = lax.ppermute(k_blk, "cp", shift_perm)
            v_blk = lax.ppermute(v_blk, "cp", shift_perm)
            k_pos = seq_positions((cp_index - step_idx) % n_cp, n_cp, half_len)
            cur_max, cur_sum, cur_acc = attend_block(q_loc, k_blk, v_blk, q_pos, k_pos, cur_max, cur_sum, cur_acc)
            return k_blk, v_blk, cur_max, cur_sum, cur_acc

        kv_state = lax.fori_loop(1, n_cp, kv_step, (k_cur, v_cur) + first_state)
        attn_out = (kv_state[4] / kv_state[3][..., None]).astype(jnp.bfloat16)
        w_o_view = w_o.reshape(kv_loc, grp_size, head_dim, hid_dim)
        attn_part = jnp.einsum("grqd,grdh->qh", attn_out, w_o_view, preferred_element_type=jnp.float32)
        attn_rows = lax.psum_scatter(attn_part, "tp", scatter_dimension=0, tiled=True)
        h_loc = (x_loc.astype(jnp.float32) + attn_rows).astype(jnp.bfloat16)

        flat_ids = ids_loc.reshape(-1)
        one_hot = (flat_ids[:, None] == jnp.arange(n_experts)[None, :]).astype(jnp.int32)
        slot_ids = jnp.sum(jnp.cumsum(one_hot, axis=0) * one_hot, axis=1) - 1
        dest_idx = flat_ids * capacity + slot_ids
        choice_rows = jnp.arange(tok_dev * top_k, dtype=jnp.int32) // top_k
        slot_rows = jax.ops.segment_sum(choice_rows, dest_idx, num_segments=n_experts * capacity)
        send_buf = jnp.take(h_loc, slot_rows, axis=0).reshape(n_cp, n_tp // 2, 1, local_exp, capacity, hid_dim)
        send_buf = jnp.broadcast_to(send_buf, (n_cp, n_tp // 2, 2, local_exp, capacity, hid_dim)).reshape(n_cp, n_tp, local_exp, capacity, hid_dim)
        recv_buf = lax.all_to_all(send_buf, "tp", 1, 1, tiled=True)
        recv_buf = lax.all_to_all(recv_buf, "cp", 0, 0, tiled=True)

        gate_pre = jnp.einsum("uvech,ehf->uvecf", recv_buf, w_gate, preferred_element_type=jnp.float32)
        up_pre = jnp.einsum("uvech,ehf->uvecf", recv_buf, w_up, preferred_element_type=jnp.float32)
        hidden = (jax.nn.silu(gate_pre) * up_pre).astype(jnp.bfloat16)
        z_part = jnp.einsum("uvecf,efh->uvech", hidden, w_down, preferred_element_type=jnp.float32)

        my_half = tp_index % 2
        keep_part = lax.dynamic_slice_in_dim(z_part, my_half * half_hid, half_hid, axis=4)
        send_part = lax.dynamic_slice_in_dim(z_part, (1 - my_half) * half_hid, half_hid, axis=4)
        pair_perm = [(dev_idx, dev_idx ^ 1) for dev_idx in range(n_tp)]
        z_half = (keep_part + lax.ppermute(send_part, "tp", pair_perm)).astype(jnp.bfloat16)

        back_buf = lax.all_to_all(z_half, "cp", 0, 0, tiled=True)
        back_buf = lax.all_to_all(back_buf, "tp", 1, 1, tiled=True)
        z_full = back_buf.reshape(n_cp, n_tp // 2, 2, local_exp, capacity, half_hid).transpose(0, 1, 3, 4, 2, 5).reshape(n_experts * capacity, hid_dim)
        picked = jnp.take(z_full, dest_idx, axis=0).reshape(tok_dev, top_k, hid_dim)
        y_loc = h_loc.astype(jnp.float32) + jnp.sum(gates_loc[:, :, None] * picked, axis=1)
        return y_loc.astype(jnp.bfloat16)

    return jax.shard_map(device_step, mesh=mesh, in_specs=(row_spec, head_spec, head_spec, head_spec, P("tp", None, None), row_spec, row_spec, expert_spec, expert_spec, expert_spec), out_specs=row_spec, check_vma=False)
```

profile of v0, /device:TPU:99, one launch (start us, length us, event | category | flops | bytes accessed | tf_op | source)
XLA Modules:
  0.0 2616.0 jit_solution(6385694230750317726)
XLA Ops:
  6.6 0.7 all-gather.2.cloned.1.call-update
  7.4 12.4 broadcast_compare_fusion.1
  19.8 74.8 %all-gather.2.cloned.1.call-done = bf16[4096,2048]{1,0:T(8,128)(2,1)} async-done(((bf16[512,2048]{1,0:T(8,128)(2,1)}), bf16[4096,2048]{1,0:T(8,128)(2,1)}) %all-gather.2.cloned.1.call-update) | async-done | bytes 16777232 | tf_op jit(solution)/shard_map/all_gather | solution.py:46
  94.6 10.7 fusion.59
  105.6 5.7 fusion.65
  111.4 54.0 %fusion.23 = (f32[2,4096]{1,0:T(2,128)S(1)}, f32[2,4096,4096]{2,1,0:T(8,128)}) fusion(pred[4096,4096]{0,1:T(8,128)(4,1)} %broadcast_compare_fusion.1, bf16[4096,2,128]{2,0,1:T(8,128)(2,1)S(1)} %fusion.59, bf16[4096,2,128]{2,0,1:T(8,128)(2,1)} %fusion.65), kind=kOutput, calls=%fused_computation.30 | convolution fusion | flops 8690589696 | bytes 155222016 | tf_op jit(solution)/shard_map/qgrd,kgd->grqk/dot_general | solution.py:15
  165.4 46.5 %fusion.22 = f32[2,4096]{1,0:T(2,128)S(1)} fusion(f32[2,4096,4096]{2,1,0:T(8,128)} %get-tuple-element.286, f32[2,4096]{1,0:T(2,128)S(1)} %get-tuple-element.284, pred[4096,4096]{0,1:T(8,128)(4,1)} %broadcast_compare_fusion.1), kind=kLoop, calls=%fused_computation.29 | loop fusion | flops 134209536 | bytes 151060480 | tf_op jit(solution)/shard_map/reduce_sum | solution.py:21
  212.0 9.9 fusion.62
  221.9 57.0 %fusion.56 = f32[2,1,4096,128]{3,2,0,1:T(8,128)} fusion(bf16[4096,2,128]{2,0,1:T(8,128)(2,1)} %fusion.62, f32[2,4096,4096]{2,1,0:T(8,128)} %get-tuple-element.286, f32[2,4096]{1,0:T(2,128)S(1)} %get-tuple-element.284, pred[4096,4096]{0,1:T(8,128)(4,1)} %broadcast_compare_fusion.1, f32[2,4096]{1,0:T(2,128)S(1)} %get-tuple-element.282), kind=kOutput, calls=%fused_computation.65 | convolution fusion | flops 8725200896 | bytes 157351936 | tf_op jit(solution)/shard_map/grqk,kgd->grqd/dot_general | solution.py:22
  278.8 635.7 %while.24 = (s32[]{:T(128)}, bf16[4096,2,128]{2,0,1:T(8,128)(2,1)}, bf16[4096,2,128]{2,0,1:T(8,128)(2,1)}, f32[2,1,4096]{2,0,1:T(2,128)S(1)}, f32[2,1,4096]{2,0,...) while((s32[]{:T(128)}, bf16[4096,2,128]{2,0,1:T(8,128)(2,1)}, ...), condition=%wide.region_5.6_spmd.clone, body=%wide.region_2.5_spmd.clone.sunk | while | flops 17567903744 | bytes 510198144 | solution.py:66
  279.2 1.3 collective-permute-start
  280.5 1.2 collective-permute-start.1
  281.7 12.3 broadcast_compare_fusion.3
  294.1 33.5 %collective-permute-done = bf16[4096,2,128]{2,0,1:T(8,128)(2,1)} collective-permute-done((bf16[4096,2,128]{2,0,1:T(8,128)(2,1)}, bf16[4096,2,128]{2,0,1:T(8,128)(2,1)}, u32[]{:S(2)}, u32[]{:S(2)}) %collective-permute-start) | collective-permute-done | bytes 2097184 | tf_op jit(solution)/shard_map/while/body/eval_jaxpr/ppermute | solution.py:60
  327.6 54.7 %fusion.106 = (f32[2,4096]{1,0:T(2,128)S(1)}, f32[2,4096,4096]{2,1,0:T(8,128)}) fusion(pred[4096,4096]{0,1:T(8,128)(4,1)} %broadcast_compare_fusion.3, bf16[4096,2,128]{2,0,1:T(8,128)(2,1)} %collective-permute-done, bf16[4096,2,1,128]{3,0,1,2:T(8,128)(2,1)} %get-tuple-element.399), kind=kOutput, calls=%fused_computation.8.clone.1 | convolution fusion | flops 8690589696 | bytes 155222016 | tf_op jit(solution)/shard_map/while/body/eval_jaxpr/qgrd,kgd->grqk/dot_general | solution.py:15
  382.3 46.2 %fusion.108 = f32[2,4096]{1,0:T(2,128)S(1)} fusion(f32[2,4096,4096]{2,1,0:T(8,128)} %get-tuple-element.358, f32[2,4096]{1,0:T(2,128)S(1)} %bitcast.204, pred[4096,4096]{0,1:T(8,128)(4,1)} %broadcast_compare_fusion.3), kind=kLoop, calls=%fused_computation.7.clone.1 | loop fusion | flops 134209536 | bytes 151060480 | tf_op jit(solution)/shard_map/while/body/eval_jaxpr/reduce_sum | solution.py:21
  428.6 3.0 copy.109
  431.6 1.3 copy.110
  432.9 60.1 %fusion.109 = f32[2,1,4096,128]{3,2,0,1:T(8,128)} fusion(bf16[4096,2,128]{2,0,1:T(8,128)(2,1)S(1)} %collective-permute-done.1, f32[2,4096,4096]{2,1,0:T(8,128)} %get-tuple-element.358, f32[2,4096]{1,0:T(2,128)S(1)} %bitcast.205, pred[4096,4096]{0,1:T(8,128)(4,1)} %broadcast_compare_fusion.3, f32[2,1,4096,128]{3,2,0,1:T(8,128)} %get-tuple-element.381, ...), kind=kOutput, calls=%fused_computation.14.clone.1 | convolution fusion | flops 8726249472 | bytes 161546240 | tf_op jit(solution)/shard_map/while/body/eval_jaxpr/grqk,kgd->grqd/dot_general | solution.py:22
  493.0 1.2 collective-permute-start.1
  494.2 12.3 broadcast_compare_fusion.3
  506.6 33.2 %collective-permute-done = bf16[4096,2,128]{2,0,1:T(8,128)(2,1)} collective-permute-done((bf16[4096,2,128]{2,0,1:T(8,128)(2,1)}, bf16[4096,2,128]{2,0,1:T(8,128)(2,1)}, u32[]{:S(2)}, u32[]{:S(2)}) %collective-permute-start) | collective-permute-done | bytes 2097184 | tf_op jit(solution)/shard_map/while/body/eval_jaxpr/ppermute | solution.py:60
  539.8 54.7 %fusion.106 = (f32[2,4096]{1,0:T(2,128)S(1)}, f32[2,4096,4096]{2,1,0:T(8,128)}) fusion(pred[4096,4096]{0,1:T(8,128)(4,1)} %broadcast_compare_fusion.3, bf16[4096,2,128]{2,0,1:T(8,128)(2,1)} %collective-permute-done, bf16[4096,2,1,128]{3,0,1,2:T(8,128)(2,1)} %get-tuple-element.399), kind=kOutput, calls=%fused_computation.8.clone.1 | convolution fusion | flops 8690589696 | bytes 155222016 | tf_op jit(solution)/shard_map/while/body/eval_jaxpr/qgrd,kgd->grqk/dot_general | solution.py:15
  594.5 46.2 %fusion.108 = f32[2,4096]{1,0:T(2,128)S(1)} fusion(f32[2,4096,4096]{2,1,0:T(8,128)} %get-tuple-element.358, f32[2,4096]{1,0:T(2,128)S(1)} %bitcast.204, pred[4096,4096]{0,1:T(8,128)(4,1)} %broadcast_compare_fusion.3), kind=kLoop, calls=%fused_computation.7.clone.1 | loop fusion | flops 134209536 | bytes 151060480 | tf_op jit(solution)/shard_map/while/body/eval_jaxpr/reduce_sum | solution.py:21
  640.8 3.0 copy.109
  643.9 1.3 copy.110
  645.2 60.1 %fusion.109 = f32[2,1,4096,128]{3,2,0,1:T(8,128)} fusion(bf16[4096,2,128]{2,0,1:T(8,128)(2,1)S(1)} %collective-permute-done.1, f32[2,4096,4096]{2,1,0:T(8,128)} %get-tuple-element.358, f32[2,4096]{1,0:T(2,128)S(1)} %bitcast.205, pred[4096,4096]{0,1:T(8,128)(4,1)} %broadcast_compare_fusion.3, f32[2,1,4096,128]{3,2,0,1:T(8,128)} %get-tuple-element.381, ...), kind=kOutput, calls=%fused_computation.14.clone.1 | convolution fusion | flops 8726249472 | bytes 161546240 | tf_op jit(solution)/shard_map/while/body/eval_jaxpr/grqk,kgd->grqd/dot_general | solution.py:22
  705.3 12.4 broadcast_compare_fusion.3
  717.7 31.5 %collective-permute-done = bf16[4096,2,128]{2,0,1:T(8,128)(2,1)} collective-permute-done((bf16[4096,2,128]{2,0,1:T(8,128)(2,1)}, bf16[4096,2,128]{2,0,1:T(8,128)(2,1)}, u32[]{:S(2)}, u32[]{:S(2)}) %collective-permute-start) | collective-permute-done | bytes 2097184 | tf_op jit(solution)/shard_map/while/body/eval_jaxpr/ppermute | solution.py:60
  749.1 54.7 %fusion.106 = (f32[2,4096]{1,0:T(2,128)S(1)}, f32[2,4096,4096]{2,1,0:T(8,128)}) fusion(pred[4096,4096]{0,1:T(8,128)(4,1)} %broadcast_compare_fusion.3, bf16[4096,2,128]{2,0,1:T(8,128)(2,1)} %collective-permute-done, bf16[4096,2,1,128]{3,0,1,2:T(8,128)(2,1)} %get-tuple-element.399), kind=kOutput, calls=%fused_computation.8.clone.1 | convolution fusion | flops 8690589696 | bytes 155222016 | tf_op jit(solution)/shard_map/while/body/eval_jaxpr/qgrd,kgd->grqk/dot_general | solution.py:15
  803.9 46.2 %fusion.108 = f32[2,4096]{1,0:T(2,128)S(1)} fusion(f32[2,4096,4096]{2,1,0:T(8,128)} %get-tuple-element.358, f32[2,4096]{1,0:T(2,128)S(1)} %bitcast.204, pred[4096,4096]{0,1:T(8,128)(4,1)} %broadcast_compare_fusion.3), kind=kLoop, calls=%fused_computation.7.clone.1 | loop fusion | flops 134209536 | bytes 151060480 | tf_op jit(solution)/shard_map/while/body/eval_jaxpr/reduce_sum | solution.py:21
  850.1 3.0 copy.109
  853.2 1.3 copy.110
  854.5 60.1 %fusion.109 = f32[2,1,4096,128]{3,2,0,1:T(8,128)} fusion(bf16[4096,2,128]{2,0,1:T(8,128)(2,1)S(1)} %collective-permute-done.1, f32[2,4096,4096]{2,1,0:T(8,128)} %get-tuple-element.358, f32[2,4096]{1,0:T(2,128)S(1)} %bitcast.205, pred[4096,4096]{0,1:T(8,128)(4,1)} %broadcast_compare_fusion.3, f32[2,1,4096,128]{3,2,0,1:T(8,128)} %get-tuple-element.381, ...), kind=kOutput, calls=%fused_computation.14.clone.1 | convolution fusion | flops 8726249472 | bytes 161546240 | tf_op jit(solution)/shard_map/while/body/eval_jaxpr/grqk,kgd->grqd/dot_general | solution.py:22
  914.6 15.5 convolution_bitcast_fusion
  931.7 18.4 reduce-window.6
  951.4 0.8 fusion.70
  952.9 21.9 scatter_custom_fusion
  974.9 130.9 %reduce-scatter.2.cloned.1.call-done = f32[512,2048]{1,0:T(8,128)} async-done(((f32[4096,2048]{1,0:T(8,128)}), f32[512,2048]{1,0:T(8,128)}) %reduce-scatter.2.cloned.1.call-update) | async-done | bytes 4194320 | tf_op jit(solution)/shard_map/reduce_scatter | solution.py:70
  1105.8 3.5 add_convert_fusion.1
  1109.4 20.9 gather_fusion
  1130.3 8.5 broadcast_select_fusion
  1138.8 6.6 copy.64
  1145.3 15.9 broadcast_in_dim.100
  1161.2 374.8 %all_to_all.20 = bf16[4,8,4,64,2048]{4,3,0,2,1:T(8,128)(2,1)} all-to-all(bf16[4,8,4,64,2048]{4,3,0,2,1:T(8,128)(2,1)} %bitcast.201), channel_id=1, replica_groups=mesh['dp'=1,'cp'=4,'tp'=8] {'tp'}, dimensions={1} | all-to-all | bytes 67108864 | tf_op jit(solution)/shard_map/all_to_all | solution.py:81
  1535.9 22.9 copy.65
  1558.8 10.0 all-to-all-start.1
  1568.9 362.2 %all-to-all-done.1 = bf16[4,8,4,64,2048]{4,3,1,2,0:T(8,128)(2,1)} async-done(((bf16[4,8,4,64,2048]{4,3,1,2,0:T(8,128)(2,1)}), bf16[4,8,4,64,2048]{4,3,1,2,0:T(8,128)(2,1)}, u32[]{:S(2)}, u32[]{:S(2)}) %all-to-all-start.1) | async-done | bytes 33554464 | tf_op jit(solution)/shard_map/all_to_all | solution.py:82
  1931.1 26.2 %fusion.29 = f32[4,4,8,64,512]{4,3,2,1,0:T(8,128)} fusion(bf16[4,8,4,64,2048]{4,3,1,2,0:T(8,128)(2,1)} %all-to-all-done.1, bf16[4,2048,512]{2,1,0:T(8,128)(2,1)} %param.20), kind=kOutput, calls=%fused_computation.39 | convolution fusion | flops 17179869184 | bytes 58720256 | tf_op jit(solution)/shard_map/uvech,ehf->uvecf/dot_general | solution.py:85
  1957.3 61.1 %fusion.45 = f32[4,4,8,64,2048]{4,3,2,1,0:T(8,128)} fusion(bf16[4,512,2048]{2,1,0:T(8,128)(2,1)} %param.21, f32[4,4,8,64,512]{4,3,2,1,0:T(8,128)} %fusion.29, bf16[4,8,4,64,2048]{4,3,1,2,0:T(8,128)(2,1)} %all-to-all-done.1, bf16[4,2048,512]{2,1,0:T(8,128)(2,1)} %param.19), kind=kOutput, calls=%fused_computation.59 | convolution fusion | flops 34384904192 | bytes 134217728 | tf_op jit(solution)/shard_map/uvecf,efh->uvech/dot_general | solution.py:87
  2018.4 23.3 dynamic-slice_bitcast_fusion
  2041.7 2.0 collective-permute-start.2
  2043.7 48.8 %collective-permute-done.2 = f32[4,8,4,64,1024]{4,3,1,0,2:T(8,128)} collective-permute-done((f32[4,8,4,64,1024]{4,3,1,0,2:T(8,128)}, f32[4,8,4,64,1024]{4,3,1,0,2:T(8,128)}, u32[]{:S(2)}, u32[]{:S(2)}) %collective-permute-start.2) | collective-permute-done | bytes 33554464 | tf_op jit(solution)/shard_map/ppermute | solution.py:93
  2092.5 27.6 %fusion.28 = bf16[4,8,4,64,1024]{4,3,1,0,2:T(8,128)(2,1)} fusion(f32[4,8,4,64,1024]{4,3,1,0,2:T(8,128)} %collective-permute-done.2, f32[4,4,8,64,2048]{4,3,2,1,0:T(8,128)} %fusion.45, s32[]{:T(128)S(6)} %select_n.114), kind=kLoop, calls=%fused_computation.35 | loop fusion | flops 16777216 | bytes 83886080 | tf_op jit(solution)/shard_map/convert_element_type | solution.py:93
  2120.0 8.2 copy.68
  2128.2 186.4 %all_to_all.21 = bf16[4,8,4,64,1024]{4,3,1,2,0:T(8,128)(2,1)S(1)} all-to-all(bf16[4,8,4,64,1024]{4,3,1,2,0:T(8,128)(2,1)S(1)} %copy.68), channel_id=1, replica_groups=mesh['dp'=1,'cp'=4,'tp'=8] {'cp'}, dimensions={0} | all-to-all | bytes 33554432 | tf_op jit(solution)/shard_map/all_to_all | solution.py:95
  2314.6 6.6 copy.69
  2321.2 8.6 all-to-all-start.3
  2330.5 181.7 %all-to-all-done.3 = bf16[4,8,4,64,1024]{4,3,0,2,1:T(8,128)(2,1)} async-done(((bf16[4,8,4,64,1024]{4,3,0,2,1:T(8,128)(2,1)}), bf16[4,8,4,64,1024]{4,3,0,2,1:T(8,128)(2,1)}, u32[]{:S(2)}, u32[]{:S(2)}) %all-to-all-start.3) | async-done | bytes 16777248 | tf_op jit(solution)/shard_map/all_to_all | solution.py:96
  2512.2 28.3 %copy.70 = bf16[4,4,2,4,64,1024]{5,2,4,3,1,0:T(2,128)(2,1)S(1)} copy(bf16[4,4,2,4,64,1024]{5,4,0,3,2,1:T(8,128)(2,1)} %bitcast.28) | data formatting | bytes 33554432 | tf_op jit(solution)/shard_map/reshape | solution.py:97
  2540.5 9.2 copy.78
  2549.7 39.2 %gather_fusion.1 = bf16[4096,2048]{1,0:T(8,128)(2,1)} fusion(bf16[4096,2048]{1,0:T(8,128)(2,1)} %bitcast.200, s32[4096]{0:T(1024)S(1)} %broadcast_clamp_fusion), kind=kCustom, calls=%fused_computation.1 | custom fusion | bytes 33570816 | tf_op jit(solution)/shard_map/jit(_take)/gather | solution.py:98
  2588.9 17.7 multiply_reduce_fusion
  2606.7 2.1 add_convert_fusion
  (73 shorter events, 5.0 us)
Async XLA Ops:
  6.5 908.0 %copy-start = (bf16[2,128,2048]{2,1,0:T(8,128)(2,1)S(1)}, bf16[2,128,2048]{2,1,0:T(8,128)(2,1)}, u32[]{:S(2)}) copy-start(bf16[2,128,2048]{2,1,0:T(8,128)(2,1)} %param.16) | copy-start | bytes 3145732
  6.6 88.0 %all-gather.2.cloned.1.call-start = ((), (), s32[]{:S(2)}) async-start(), calls=%async_computation.5 | async-start | bytes 18874368 | tf_op jit(solution)/shard_map/all_gather | solution.py:46
  7.3 1098.5 %reduce-scatter.2.cloned.1.call-start = ((), (), s32[]{:S(2)}) async-start(), calls=%async_computation.6 | async-start | bytes 37748736 | tf_op jit(solution)/shard_map/reduce_scatter | solution.py:70
  94.6 10.8 copy-start.9
  94.6 11.1 copy-start.11
  105.6 5.7 copy-start.10
  165.4 46.5 %copy-start.12 = (bf16[2048,2,128]{2,1,0:T(2,128)(2,1)S(1)}, bf16[2048,2,128]{2,1,0:T(2,128)(2,1)}, u32[]{:S(2)}) copy-start(bf16[2048,2,128]{2,1,0:T(2,128)(2,1)} %param.15) | copy-start | bytes 3145732
  279.2 48.3 %collective-permute-start = (bf16[4096,2,128]{2,0,1:T(8,128)(2,1)}, bf16[4096,2,128]{2,0,1:T(8,128)(2,1)}, u32[]{:S(2)}, u32[]{:S(2)}) collective-permute-start(bf16[4096,2,128]{2,0,1:T(8,128)(2,1)} %get-tuple-element.377), channel_id=1, source_target_pairs={{0,8},{8,16},{16,24},{24,0},{1,9},{9,17},{17,25},{25,1},{2,10},{10... | collective-permute-start | bytes 6291464 | tf_op jit(solution)/shard_map/while/body/eval_jaxpr/ppermute | solution.py:60
  280.5 151.1 %collective-permute-start.1 = (bf16[4096,2,128]{2,0,1:T(8,128)(2,1)}, bf16[4096,2,128]{2,0,1:T(8,128)(2,1)S(1)}, u32[]{:S(2)}, u32[]{:S(2)}) collective-permute-start(bf16[4096,2,128]{2,0,1:T(8,128)(2,1)} %get-tuple-element.378), channel_id=1, source_target_pairs={{0,8},{8,16},{16,24},{24,0},{1,9},{9,17},{17,25},{25,1},{2,10},{10... | collective-permute-start | bytes 6291464 | tf_op jit(solution)/shard_map/while/body/eval_jaxpr/ppermute | solution.py:61
  493.0 46.8 %collective-permute-start = (bf16[4096,2,128]{2,0,1:T(8,128)(2,1)}, bf16[4096,2,128]{2,0,1:T(8,128)(2,1)}, u32[]{:S(2)}, u32[]{:S(2)}) collective-permute-start(bf16[4096,2,128]{2,0,1:T(8,128)(2,1)} %get-tuple-element.377), channel_id=1, source_target_pairs={{0,8},{8,16},{16,24},{24,0},{1,9},{9,17},{17,25},{25,1},{2,10},{10... | collective-permute-start | bytes 6291464 | tf_op jit(solution)/shard_map/while/body/eval_jaxpr/ppermute | solution.py:60
  493.0 150.8 %collective-permute-start.1 = (bf16[4096,2,128]{2,0,1:T(8,128)(2,1)}, bf16[4096,2,128]{2,0,1:T(8,128)(2,1)S(1)}, u32[]{:S(2)}, u32[]{:S(2)}) collective-permute-start(bf16[4096,2,128]{2,0,1:T(8,128)(2,1)} %get-tuple-element.378), channel_id=1, source_target_pairs={{0,8},{8,16},{16,24},{24,0},{1,9},{9,17},{17,25},{25,1},{2,10},{10... | collective-permute-start | bytes 6291464 | tf_op jit(solution)/shard_map/while/body/eval_jaxpr/ppermute | solution.py:61
  705.3 43.9 %collective-permute-start = (bf16[4096,2,128]{2,0,1:T(8,128)(2,1)}, bf16[4096,2,128]{2,0,1:T(8,128)(2,1)}, u32[]{:S(2)}, u32[]{:S(2)}) collective-permute-start(bf16[4096,2,128]{2,0,1:T(8,128)(2,1)} %get-tuple-element.377), channel_id=1, source_target_pairs={{0,8},{8,16},{16,24},{24,0},{1,9},{9,17},{17,25},{25,1},{2,10},{10... | collective-permute-start | bytes 6291464 | tf_op jit(solution)/shard_map/while/body/eval_jaxpr/ppermute | solution.py:60
  705.3 147.9 %collective-permute-start.1 = (bf16[4096,2,128]{2,0,1:T(8,128)(2,1)}, bf16[4096,2,128]{2,0,1:T(8,128)(2,1)S(1)}, u32[]{:S(2)}, u32[]{:S(2)}) collective-permute-start(bf16[4096,2,128]{2,0,1:T(8,128)(2,1)} %get-tuple-element.378), channel_id=1, source_target_pairs={{0,8},{8,16},{16,24},{24,0},{1,9},{9,17},{17,25},{25,1},{2,10},{10... | collective-permute-start | bytes 6291464 | tf_op jit(solution)/shard_map/while/body/eval_jaxpr/ppermute | solution.py:61
  930.1 0.7 copy-start.3
  952.3 0.6 copy-start.5
  1109.4 20.9 copy-start.1
  1558.8 372.2 %all-to-all-start.1 = ((bf16[4,8,4,64,2048]{4,3,1,2,0:T(8,128)(2,1)}), bf16[4,8,4,64,2048]{4,3,1,2,0:T(8,128)(2,1)}, u32[]{:S(2)}, u32[]{:S(2)}) async-start(bf16[4,8,4,64,2048]{4,3,1,2,0:T(8,128)(2,1)} %copy.65), calls=%async_computation.2 | async-start | bytes 67108864 | tf_op jit(solution)/shard_map/all_to_all | solution.py:82
  2041.7 50.8 %collective-permute-start.2 = (f32[4,8,4,64,1024]{4,3,1,0,2:T(8,128)}, f32[4,8,4,64,1024]{4,3,1,0,2:T(8,128)}, u32[]{:S(2)}, u32[]{:S(2)}) collective-permute-start(f32[4,8,4,64,1024]{4,3,1,0,2:T(8,128)} %dynamic-slice_bitcast_fusion), channel_id=1, source_target_pairs={{0,1},{1,0},{2,3},{3,2},{4,5},{5,4},{6,7},{7,6},{8,9},{9,8},{10,11... | collective-permute-start | bytes 100663304 | tf_op jit(solution)/shard_map/ppermute | solution.py:93
  2321.2 8.6 copy-start.6
  2321.2 8.8 copy-start.8
  2321.2 9.1 copy-start.4
  2321.2 9.3 copy-start.7
  2321.2 190.9 %all-to-all-start.3 = ((bf16[4,8,4,64,1024]{4,3,0,2,1:T(8,128)(2,1)}), bf16[4,8,4,64,1024]{4,3,0,2,1:T(8,128)(2,1)}, u32[]{:S(2)}, u32[]{:S(2)}) async-start(bf16[4,8,4,64,1024]{4,3,0,2,1:T(8,128)(2,1)} %copy.69), calls=%async_computation.4 | async-start | bytes 33554432 | tf_op jit(solution)/shard_map/all_to_all | solution.py:96
  2588.9 17.7 copy-start.2
Sparse Core Ops, SparseCore 0:
  9.0 85.5 all-gather.1
  930.2 175.5 reduce-scatter.1
where the time goes:
time: 2630 us; the launch traced here: 2620 us
  waiting for transfers between devices  897 us (34%)
  matrix products  584 us (22%)
  blocking collectives  561 us (21%)
  other arithmetic  337 us (13%)
  local copies, waits for them, and re-layouts  197 us (7%)
    all_to_all x1, blocking collectives, device_step(): recv_buf = lax.all_to_all(send_buf, 'tp', 1, 1, tiled=True)  375 us
    all_to_all x1, waiting for transfers between devices, device_step(): recv_buf = lax.all_to_all(recv_buf, 'cp', 0, 0, tiled=True)  362 us
    dot_general x4, matrix products, attend_block(): jnp.einsum('grqk,kgd->grqd', prob_vals.astype(jnp.bfloat16), v_blk, prefe...  237 us
    dot_general x4, matrix products, attend_block(): jnp.einsum('qgrd,kgd->grqk', q_loc, k_blk, preferred_element_type=jnp.flo...  218 us
    all_to_all x1, blocking collectives, device_step(): back_buf = lax.all_to_all(z_half, 'cp', 0, 0, tiled=True)  186 us
    reduce_sum x4, other arithmetic, attend_block(): new_sum = run_sum * rescale + jnp.sum(prob_vals, axis=-1)  185 us
    all_to_all x1, waiting for transfers between devices, device_step(): back_buf = lax.all_to_all(back_buf, 'tp', 1, 1, tiled=True)  182 us
    reduce_scatter x1, waiting for transfers between devices, device_step(): lax.psum_scatter(attn_part, 'tp', scatter_dimension=0, tiled=True)  131 us
  transfers between devices with their start and end apart: 11, of which 8 were waited for; matrix products, arithmetic and copies ran while one was open for 16% of the time, Pallas kernels for 0%

commit v1 on v0

--- a/solution.py
+++ b/solution.py
@@ -1,7 +1,241 @@
+import functools
+
 import jax
 import jax.numpy as jnp
 from jax import lax
+from jax.experimental import pallas as pl
+from jax.experimental.pallas import tpu as pltpu
 from jax.sharding import PartitionSpec as P
+
+MESH = pl.DeviceIdType.MESH
+VMEM_LIMIT = 66_000_000
+
+
+def peer_of(step, cp_pos, tp_pos, n_cp, n_tp, sign):
+    n_x = n_tp // 2
+    flip = step % 2
+    off_x = (step // 2) % n_x
+    off_y = (off_x + step // n_tp) % n_cp
+    if sign < 0:
+        off_x = n_x - off_x
+        off_y = n_cp - off_y
+    to_cp = (cp_pos + off_y) % n_cp
+    to_tp = ((tp_pos // 2 + off_x) % n_x) * 2 + (tp_pos % 2 + flip) % 2
+    return to_cp, to_tp
+
+
+def mesh_id(cp_pos, tp_pos):
+    return {"cp": cp_pos, "tp": tp_pos}
+
+
+def moe_kernel(n_cp, n_tp, group, h_hbm, rank_ref, gate_ref, wg_hbm, wu_hbm, wd_hbm, wgx_hbm, wux_hbm, wdx_hbm,
+               y_ref, rx_hbm, rz_hbm,
+               h_buf, wg_buf, wu_buf, wd_buf, stage, x_buf, z_buf, acc, parts,
+               w_sem, in_sem, x_sem, z_sem, sx_sem, rx_sem, sz_sem, rz_sem):
+    n_dev = n_cp * n_tp
+    tok_dev, hid = h_buf.shape
+    cap = stage.shape[1] // 2
+    half_f = wg_buf.shape[3]
+    cp_pos, tp_pos = lax.axis_index("cp"), lax.axis_index("tp")
+    core = tp_pos % 2
+
+    def signal_peer(step, carry):
+        to_cp, to_tp = peer_of(step, cp_pos, tp_pos, n_cp, n_tp, 1)
+        pl.semaphore_signal(pltpu.get_barrier_semaphore(), inc=1, device_id=mesh_id(to_cp, to_tp), device_id_type=MESH)
+        return carry
+
+    h_copy = pltpu.make_async_copy(h_hbm, h_buf, in_sem)
+    h_copy.start()
+    w_copies = []
+    for slot, (own, other, buf) in enumerate(((wg_hbm, wgx_hbm, wg_buf), (wu_hbm, wux_hbm, wu_buf), (wd_hbm, wdx_hbm, wd_buf))):
+        w_copies.append(pltpu.make_async_copy(own.at[pl.ds(2 * core, 2)], buf.at[0], w_sem.at[2 * slot]))
+        w_copies.append(pltpu.make_async_copy(other, buf.at[1], w_sem.at[2 * slot + 1]))
+    for one in w_copies:
+        one.start()
+    lax.fori_loop(1, n_dev, signal_peer, 0)
+    pl.semaphore_wait(pltpu.get_barrier_semaphore(), n_dev - 1)
+    h_copy.wait()
+
+    slots = lax.broadcasted_iota(jnp.int32, (cap, tok_dev), 0).astype(jnp.float32)
+
+    def gather_rows(step):
+        to_cp, to_tp = peer_of(step, cp_pos, tp_pos, n_cp, n_tp, 1)
+        first = 2 * (to_cp * n_tp + to_tp)
+        picks = [jnp.where(rank_ref[pl.ds(first + i, 1), :] == slots, 1.0, 0.0) for i in range(2)]
+        pick = jnp.concatenate(picks, axis=0).astype(jnp.bfloat16)
+        stage[step] = jnp.dot(pick, h_buf[...], preferred_element_type=jnp.float32).astype(jnp.bfloat16)
+
+    def x_send(step):
+        to_cp, to_tp = peer_of(step, cp_pos, tp_pos, n_cp, n_tp, 1)
+        return pltpu.make_async_remote_copy(stage.at[step], rx_hbm.at[step], sx_sem.at[step], rx_sem.at[step],
+                                            device_id=mesh_id(to_cp, to_tp), device_id_type=MESH)
+
+    def z_send(step):
+        to_cp, to_tp = peer_of(step, cp_pos, tp_pos, n_cp, n_tp, -1)
+        return pltpu.make_async_remote_copy(stage.at[step], rz_hbm.at[step], sz_sem.at[step], rz_sem.at[step],
+                                            device_id=mesh_id(to_cp, to_tp), device_id_type=MESH)
+
+    self_x = pltpu.make_async_copy(stage.at[0], rx_hbm.at[0], rx_sem.at[0])
+    self_z = pltpu.make_async_copy(stage.at[0], rz_hbm.at[0], rz_sem.at[0])
+
+    gather_rows(0)
+    gather_rows(1)
+    self_x.start()
+
+    def gather_step(step, carry):
+        gather_rows(step)
+        x_send(step - 1).start()
+        return carry
+
+    lax.fori_loop(2, n_dev, gather_step, 0)
+
+    gate_all = gate_ref[...]
+    high = gate_all.astype(jnp.bfloat16).astype(jnp.float32)
+    rest = gate_all - high
+    mid = rest.astype(jnp.bfloat16).astype(jnp.float32)
+    parts[0] = high
+    parts[1] = mid
+    parts[2] = rest - mid
+    x_send(n_dev - 1).start()
+    acc[...] = h_buf[...].astype(jnp.float32)
+    for one in w_copies:
+        one.wait()
+
+    rows = group * cap
+    n_cols = min(512, hid)
+
+    def expert_rows(place, i):
+        x_rows = x_buf[:, pl.ds(i * cap, cap), :].reshape(rows, hid)
+        hidden = []
+        for half in range(2):
+            gate_pre = jnp.dot(x_rows, wg_buf[half, i], preferred_element_type=jnp.float32)
+            up_pre = jnp.dot(x_rows, wu_buf[half, i], preferred_element_type=jnp.float32)
+            hidden.append((gate_pre * (1.0 / (1.0 + jnp.exp(-gate_pre))) * up_pre).astype(jnp.bfloat16))
+        for col in range(0, hid, n_cols):
+            z_rows = (jnp.dot(hidden[0], wd_buf[0, i, :, pl.ds(col, n_cols)], preferred_element_type=jnp.float32)
+                      + jnp.dot(hidden[1], wd_buf[1, i, :, pl.ds(col, n_cols)], preferred_element_type=jnp.float32))
+            stage[pl.ds(place, group), pl.ds(i * cap, cap), pl.ds(col, n_cols)] = z_rows.astype(jnp.bfloat16).reshape(group, cap, n_cols)
+
+    def expert_group(g, carry):
+        place = g * group
+        for q in range(group):
+            @pl.when(place + q == 0)
+            def _():
+                self_x.wait()
+
+            @pl.when(place + q > 0)
+            def _():
+                x_send(place + q).wait_recv()
+        for q in range(group):
+            pltpu.make_async_copy(rx_hbm.at[place + q], x_buf.at[q], x_sem.at[q]).start()
+        for q in range(group):
+            pltpu.make_async_copy(rx_hbm.at[place + q], x_buf.at[q], x_sem.at[q]).wait()
+        for q in range(group):
+            @pl.when(place + q > 0)
+            def _():
+                x_send(place + q).wait_send()
+        for i in range(2):
+            expert_rows(place, i)
+        for q in range(group):
+            @pl.when(place + q == 0)
+            def _():
+                self_z.start()
+
+            @pl.when(place + q > 0)
+            def _():
+                z_send(place + q).start()
+        return carry
+
+    lax.fori_loop(0, n_dev // group, expert_group, 0)
+
+    def combine_pair(j, carry):
+        @pl.when(j == 0)
+        def _():
+            self_z.wait()
+
+        @pl.when(j > 0)
+        def _():
+            z_send(2 * j).wait_recv()
+        z_send(2 * j + 1).wait_recv()
+        z_copy = pltpu.make_async_copy(rz_hbm.at[pl.ds(2 * j, 2)], z_buf, z_sem)
+        z_copy.start()
+        weights = [[], [], []]
+        for q in range(2):
+            to_cp, to_tp = peer_of(2 * j + q, cp_pos, tp_pos, n_cp, n_tp, 1)
+            first = 2 * (to_cp * n_tp + to_tp)
+            for i in range(2):
+                chosen = rank_ref[pl.ds(first + i, 1), :] == slots
+                for part in range(3):
+                    weights[part].append(jnp.where(chosen, parts[part, pl.ds(first + i, 1), :], 0.0))
+        weights = [jnp.concatenate(w, axis=0).astype(jnp.bfloat16) for w in weights]
+        z_copy.wait()
+        for col in range(0, hid, n_cols):
+            z_rows = z_buf[:, :, pl.ds(col, n_cols)].reshape(4 * cap, n_cols)
+            total = None
+            for part in range(3):
+                term = lax.dot_general(weights[part], z_rows, (((0,), (0,)), ((), ())), preferred_element_type=jnp.float32)
+                total = term if total is None else total + term
+            acc[:, pl.ds(col, n_cols)] += total
+        return carry
+
+    lax.fori_loop(0, n_dev // 2, combine_pair, 0)
+    y_ref[...] = acc[...].astype(jnp.bfloat16)
+
+    def drain(step, carry):
+        z_send(step).wait_send()
+        return carry
+
+    lax.fori_loop(1, n_dev, drain, 0)
+
+
+def moe_call(n_cp, n_tp, cap, h_loc, rank_rows, gate_rows, w_gate, w_up, w_down, wg_other, wu_other, wd_other):
+    n_dev = n_cp * n_tp
+    tok_dev, hid = h_loc.shape
+    half_f = w_gate.shape[2]
+    group = 4
+    any_spec = pl.BlockSpec(memory_space=pl.ANY)
+    vmem_spec = pl.BlockSpec(memory_space=pltpu.VMEM)
+    slab = jax.ShapeDtypeStruct((n_dev, 2 * cap, hid), jnp.bfloat16)
+    flops = 2 * n_dev * 2 * cap * hid * 2 * half_f * 3
+    y_loc, _, _ = pl.pallas_call(
+        functools.partial(moe_kernel, n_cp, n_tp, group),
+        name="routed_experts",
+        out_shape=(jax.ShapeDtypeStruct((tok_dev, hid), jnp.bfloat16), slab, slab),
+        in_specs=[any_spec, vmem_spec, vmem_spec] + [any_spec] * 6,
+        out_specs=(vmem_spec, any_spec, any_spec),
+        scratch_shapes=[
+            pltpu.VMEM((tok_dev, hid), jnp.bfloat16),
+            pltpu.VMEM((2, 2, hid, half_f), jnp.bfloat16),
+            pltpu.VMEM((2, 2, hid, half_f), jnp.bfloat16),
+            pltpu.VMEM((2, 2, half_f, hid), jnp.bfloat16),
+            pltpu.VMEM((n_dev, 2 * cap, hid), jnp.bfloat16),
+            pltpu.VMEM((group, 2 * cap, hid), jnp.bfloat16),
+            pltpu.VMEM((2, 2 * cap, hid), jnp.bfloat16),
+            pltpu.VMEM((tok_dev, hid), jnp.float32),
+            pltpu.VMEM((3,) + rank_rows.shape, jnp.float32),
+            pltpu.SemaphoreType.DMA((6,)),
+            pltpu.SemaphoreType.DMA,
+            pltpu.SemaphoreType.DMA((group,)),
+            pltpu.SemaphoreType.DMA,
+            pltpu.SemaphoreType.DMA((n_dev,)),
+            pltpu.SemaphoreType.DMA((n_dev,)),
+            pltpu.SemaphoreType.DMA((n_dev,)),
+            pltpu.SemaphoreType.DMA((n_dev,)),
+        ],
+        compiler_params=pltpu.CompilerParams(collective_id=2, has_side_effects=True, vmem_limit_bytes=VMEM_LIMIT),
+        cost_estimate=pl.CostEstimate(flops=flops, bytes_accessed=2**27, transcendentals=0),
+    )(h_loc, rank_rows, gate_rows, w_gate, w_up, w_down, wg_other, wu_other, wd_other)
+    return y_loc
+
+
+def routing_rows(ids_loc, gates_loc, n_experts):
+    tok_dev = ids_loc.shape[0]
+    chosen = ids_loc.T[None, :, :] == jnp.arange(n_experts, dtype=ids_loc.dtype)[:, None, None]
+    mask = jnp.any(chosen, axis=1)
+    gate_rows = jnp.sum(jnp.where(chosen, gates_loc.T[None, :, :], 0.0), axis=1)
+    before = jnp.triu(jnp.ones((tok_dev, tok_dev), jnp.bfloat16), 1)
+    rank = jnp.dot(mask.astype(jnp.bfloat16), before, preferred_element_type=jnp.float32)
+    return jnp.where(mask, rank, -1.0), gate_rows
 
 
 def seq_positions(cp_index, n_cp, half_len):
@@ -39,7 +273,6 @@
         local_exp = w_gate.shape[0]
         n_experts = local_exp * n_cp * n_tp // 2
         capacity = top_k * tok_dev // n_experts
-        half_hid = hid_dim // 2
         cp_index = lax.axis_index("cp")
         tp_index = lax.axis_index("tp")
 
@@ -70,33 +303,11 @@
         attn_rows = lax.psum_scatter(attn_part, "tp", scatter_dimension=0, tiled=True)
         h_loc = (x_loc.astype(jnp.float32) + attn_rows).astype(jnp.bfloat16)
 
-        flat_ids = ids_loc.reshape(-1)
-        one_hot = (flat_ids[:, None] == jnp.arange(n_experts)[None, :]).astype(jnp.int32)
-        slot_ids = jnp.sum(jnp.cumsum(one_hot, axis=0) * one_hot, axis=1) - 1
-        dest_idx = flat_ids * capacity + slot_ids
-        choice_rows = jnp.arange(tok_dev * top_k, dtype=jnp.int32) // top_k
-        slot_rows = jax.ops.segment_sum(choice_rows, dest_idx, num_segments=n_experts * capacity)
-        send_buf = jnp.take(h_loc, slot_rows, axis=0).reshape(n_cp, n_tp // 2, 1, local_exp, capacity, hid_dim)
-        send_buf = jnp.broadcast_to(send_buf, (n_cp, n_tp // 2, 2, local_exp, capacity, hid_dim)).reshape(n_cp, n_tp, local_exp, capacity, hid_dim)
-        recv_buf = lax.all_to_all(send_buf, "tp", 1, 1, tiled=True)
-        recv_buf = lax.all_to_all(recv_buf, "cp", 0, 0, tiled=True)
-
-        gate_pre = jnp.einsum("uvech,ehf->uvecf", recv_buf, w_gate, preferred_element_type=jnp.float32)
-        up_pre = jnp.einsum("uvech,ehf->uvecf", recv_buf, w_up, preferred_element_type=jnp.float32)
-        hidden = (jax.nn.silu(gate_pre) * up_pre).astype(jnp.bfloat16)
-        z_part = jnp.einsum("uvecf,efh->uvech", hidden, w_down, preferred_element_type=jnp.float32)
-
-        my_half = tp_index % 2
-        keep_part = lax.dynamic_slice_in_dim(z_part, my_half * half_hid, half_hid, axis=4)
-        send_part = lax.dynamic_slice_in_dim(z_part, (1 - my_half) * half_hid, half_hid, axis=4)
+        rank_rows, gate_rows = routing_rows(ids_loc, gates_loc, n_experts)
+        keep = local_exp // 2
+        give = (1 - tp_index % 2) * keep
         pair_perm = [(dev_idx, dev_idx ^ 1) for dev_idx in range(n_tp)]
-        z_half = (keep_part + lax.ppermute(send_part, "tp", pair_perm)).astype(jnp.bfloat16)
-
-        back_buf = lax.all_to_all(z_half, "cp", 0, 0, tiled=True)
-        back_buf = lax.all_to_all(back_buf, "tp", 1, 1, tiled=True)
-        z_full = back_buf.reshape(n_cp, n_tp // 2, 2, local_exp, capacity, half_hid).transpose(0, 1, 3, 4, 2, 5).reshape(n_experts * capacity, hid_dim)
-        picked = jnp.take(z_full, dest_idx, axis=0).reshape(tok_dev, top_k, hid_dim)
-        y_loc = h_loc.astype(jnp.float32) + jnp.sum(gates_loc[:, :, None] * picked, axis=1)
-        return y_loc.astype(jnp.bfloat16)
+        others = [lax.ppermute(lax.dynamic_slice_in_dim(w, give, keep, axis=0), "tp", pair_perm) for w in (w_gate, w_up, w_down)]
+        return moe_call(n_cp, n_tp, capacity, h_loc, rank_rows, gate_rows, w_gate, w_up, w_down, *others)
 
     return jax.shard_map(device_step, mesh=mesh, in_specs=(row_spec, head_spec, head_spec, head_spec, P("tp", None, None), row_spec, row_spec, expert_spec, expert_spec, expert_spec), out_specs=row_spec, check_vma=False)

time: 2630 us -> 1710 us (0.65)
  the two profiles are of different devices: /device:TPU:99 before, /device:TPU:103 now
where the time goes in v1:
time: 1710 us; the launch traced here: 1700 us
  Pallas kernels  580 us (34%)
  matrix products  497 us (29%)
  waiting for transfers between devices  321 us (19%)
  other arithmetic  240 us (14%)
  local copies, waits for them, and re-layouts  32.1 us (2%)
    pallas_call x1, Pallas kernels, moe_call(): pl.pallas_call(functools.partial(moe_kernel, n_cp, n_tp, group), name='ro...  580 us
    dot_general x4, matrix products, attend_block(): jnp.einsum('grqk,kgd->grqd', prob_vals.astype(jnp.bfloat16), v_blk, prefe...  237 us
    dot_general x4, matrix products, attend_block(): jnp.einsum('qgrd,kgd->grqk', q_loc, k_blk, preferred_element_type=jnp.flo...  218 us
    reduce_sum x4, other arithmetic, attend_block(): new_sum = run_sum * rescale + jnp.sum(prob_vals, axis=-1)  185 us
    reduce_scatter x1, waiting for transfers between devices, device_step(): lax.psum_scatter(attn_part, 'tp', scatter_dimension=0, tiled=True)  149 us
    ppermute x3, waiting for transfers between devices, kv_step(): k_blk = lax.ppermute(k_blk, 'cp', shift_perm)  98.1 us
    all_gather x1, waiting for transfers between devices, device_step(): x_half = lax.all_gather(x_loc, 'tp', axis=0, tiled=True)  73.4 us
    ge x4, other arithmetic, attend_block(): allowed = q_pos[:, None] >= k_pos[None, :]  49.4 us
  transfers between devices with their start and end apart: 11, of which 5 were waited for; matrix products, arithmetic and copies ran while one was open for 22% of the time, Pallas kernels for 0%

profile of v1, /device:TPU:103, one launch (start us, length us, event | category | flops | bytes accessed | tf_op | source)
XLA Modules:
  0.0 1699.1 jit_solution(16909621065235421194)
XLA Ops:
  6.6 0.7 all-gather.2.cloned.1.call-update
  7.3 0.1 reduce-scatter.2.cloned.1.call-start
  7.4 12.4 broadcast_compare_fusion.1
  19.8 73.4 %all-gather.2.cloned.1.call-done = bf16[4096,2048]{1,0:T(8,128)(2,1)} async-done(((bf16[512,2048]{1,0:T(8,128)(2,1)}), bf16[4096,2048]{1,0:T(8,128)(2,1)}) %all-gather.2.cloned.1.call-update) | async-done | bytes 16777232 | tf_op jit(solution)/shard_map/all_gather | solution.py:279
  93.1 8.7 fusion.40
  101.9 1.8 copy-done.4
  103.7 0.2 copy-done.7
  103.9 5.7 fusion.46
  109.6 54.0 %fusion.23 = (f32[2,4096]{1,0:T(2,128)S(1)}, f32[2,4096,4096]{2,1,0:T(8,128)}) fusion(pred[4096,4096]{0,1:T(8,128)(4,1)} %broadcast_compare_fusion.1, bf16[4096,2,128]{2,0,1:T(8,128)(2,1)S(1)} %fusion.40, bf16[4096,2,128]{2,0,1:T(8,128)(2,1)} %fusion.46), kind=kOutput, calls=%fused_computation.27 | convolution fusion | flops 8690589696 | bytes 155222016 | tf_op jit(solution)/shard_map/qgrd,kgd->grqk/dot_general | solution.py:249
  163.7 0.0 copy-start.8
  163.7 46.3 %fusion.22 = f32[2,4096]{1,0:T(2,128)S(1)} fusion(f32[2,4096,4096]{2,1,0:T(8,128)} %get-tuple-element.286, f32[2,4096]{1,0:T(2,128)S(1)} %get-tuple-element.284, pred[4096,4096]{0,1:T(8,128)(4,1)} %broadcast_compare_fusion.1), kind=kLoop, calls=%fused_computation.26 | loop fusion | flops 134209536 | bytes 151060480 | tf_op jit(solution)/shard_map/reduce_sum | solution.py:255
  210.1 10.4 fusion.43
  220.4 57.0 %fusion.37 = f32[2,1,4096,128]{3,2,0,1:T(8,128)} fusion(bf16[4096,2,128]{2,0,1:T(8,128)(2,1)} %fusion.43, f32[2,4096,4096]{2,1,0:T(8,128)} %get-tuple-element.286, f32[2,4096]{1,0:T(2,128)S(1)} %get-tuple-element.284, pred[4096,4096]{0,1:T(8,128)(4,1)} %broadcast_compare_fusion.1, f32[2,4096]{1,0:T(2,128)S(1)} %get-tuple-element.282), kind=kOutput, calls=%fused_computation.40 | convolution fusion | flops 8725200896 | bytes 157351936 | tf_op jit(solution)/shard_map/grqk,kgd->grqd/dot_general | solution.py:256
  277.4 635.9 %while.24 = (s32[]{:T(128)}, bf16[4096,2,128]{2,0,1:T(8,128)(2,1)}, bf16[4096,2,128]{2,0,1:T(8,128)(2,1)}, f32[2,1,4096]{2,0,1:T(2,128)S(1)}, f32[2,1,4096]{2,0,...) while((s32[]{:T(128)}, bf16[4096,2,128]{2,0,1:T(8,128)(2,1)}, ...), condition=%wide.region_5.6_spmd.clone, body=%wide.region_2.5_spmd.clone.sunk | while | flops 17567903744 | bytes 510198144 | solution.py:299
  277.6 1.5 collective-permute-start
  279.1 1.2 collective-permute-start.1
  280.3 12.3 broadcast_compare_fusion.3
  292.7 33.3 %collective-permute-done = bf16[4096,2,128]{2,0,1:T(8,128)(2,1)} collective-permute-done((bf16[4096,2,128]{2,0,1:T(8,128)(2,1)}, bf16[4096,2,128]{2,0,1:T(8,128)(2,1)}, u32[]{:S(2)}, u32[]{:S(2)}) %collective-permute-start) | collective-permute-done | bytes 2097184 | tf_op jit(solution)/shard_map/while/body/eval_jaxpr/ppermute | solution.py:293
  326.0 54.7 %fusion.80 = (f32[2,4096]{1,0:T(2,128)S(1)}, f32[2,4096,4096]{2,1,0:T(8,128)}) fusion(pred[4096,4096]{0,1:T(8,128)(4,1)} %broadcast_compare_fusion.3, bf16[4096,2,128]{2,0,1:T(8,128)(2,1)} %collective-permute-done, bf16[4096,2,1,128]{3,0,1,2:T(8,128)(2,1)} %get-tuple-element.399), kind=kOutput, calls=%fused_computation.5.clone.1 | convolution fusion | flops 8690589696 | bytes 155222016 | tf_op jit(solution)/shard_map/while/body/eval_jaxpr/qgrd,kgd->grqk/dot_general | solution.py:249
  380.7 46.2 %fusion.82 = f32[2,4096]{1,0:T(2,128)S(1)} fusion(f32[2,4096,4096]{2,1,0:T(8,128)} %get-tuple-element.358, f32[2,4096]{1,0:T(2,128)S(1)} %bitcast.123, pred[4096,4096]{0,1:T(8,128)(4,1)} %broadcast_compare_fusion.3), kind=kLoop, calls=%fused_computation.4.clone.1 | loop fusion | flops 134209536 | bytes 151060480 | tf_op jit(solution)/shard_map/while/body/eval_jaxpr/reduce_sum | solution.py:255
  426.9 0.1 bitcast_add_fusion.3
  427.0 3.0 copy.42
  430.1 1.3 copy.43
  431.4 60.1 %fusion.83 = f32[2,1,4096,128]{3,2,0,1:T(8,128)} fusion(bf16[4096,2,128]{2,0,1:T(8,128)(2,1)S(1)} %collective-permute-done.1, f32[2,4096,4096]{2,1,0:T(8,128)} %get-tuple-element.358, f32[2,4096]{1,0:T(2,128)S(1)} %bitcast.124, pred[4096,4096]{0,1:T(8,128)(4,1)} %broadcast_compare_fusion.3, f32[2,1,4096,128]{3,2,0,1:T(8,128)} %get-tuple-element.381, ...), kind=kOutput, calls=%fused_computation.11.clone.1 | convolution fusion | flops 8726249472 | bytes 161546240 | tf_op jit(solution)/shard_map/while/body/eval_jaxpr/grqk,kgd->grqd/dot_general | solution.py:256
  491.5 0.1 collective-permute-start
  491.6 1.2 collective-permute-start.1
  492.8 12.3 broadcast_compare_fusion.3
  505.2 33.1 %collective-permute-done = bf16[4096,2,128]{2,0,1:T(8,128)(2,1)} collective-permute-done((bf16[4096,2,128]{2,0,1:T(8,128)(2,1)}, bf16[4096,2,128]{2,0,1:T(8,128)(2,1)}, u32[]{:S(2)}, u32[]{:S(2)}) %collective-permute-start) | collective-permute-done | bytes 2097184 | tf_op jit(solution)/shard_map/while/body/eval_jaxpr/ppermute | solution.py:293
  538.3 54.7 %fusion.80 = (f32[2,4096]{1,0:T(2,128)S(1)}, f32[2,4096,4096]{2,1,0:T(8,128)}) fusion(pred[4096,4096]{0,1:T(8,128)(4,1)} %broadcast_compare_fusion.3, bf16[4096,2,128]{2,0,1:T(8,128)(2,1)} %collective-permute-done, bf16[4096,2,1,128]{3,0,1,2:T(8,128)(2,1)} %get-tuple-element.399), kind=kOutput, calls=%fused_computation.5.clone.1 | convolution fusion | flops 8690589696 | bytes 155222016 | tf_op jit(solution)/shard_map/while/body/eval_jaxpr/qgrd,kgd->grqk/dot_general | solution.py:249
  593.1 46.2 %fusion.82 = f32[2,4096]{1,0:T(2,128)S(1)} fusion(f32[2,4096,4096]{2,1,0:T(8,128)} %get-tuple-element.358, f32[2,4096]{1,0:T(2,128)S(1)} %bitcast.123, pred[4096,4096]{0,1:T(8,128)(4,1)} %broadcast_compare_fusion.3), kind=kLoop, calls=%fused_computation.4.clone.1 | loop fusion | flops 134209536 | bytes 151060480 | tf_op jit(solution)/shard_map/while/body/eval_jaxpr/reduce_sum | solution.py:255
  639.3 0.1 bitcast_add_fusion.3
  639.3 3.0 copy.42
  642.4 1.3 copy.43
  643.7 60.1 %fusion.83 = f32[2,1,4096,128]{3,2,0,1:T(8,128)} fusion(bf16[4096,2,128]{2,0,1:T(8,128)(2,1)S(1)} %collective-permute-done.1, f32[2,4096,4096]{2,1,0:T(8,128)} %get-tuple-element.358, f32[2,4096]{1,0:T(2,128)S(1)} %bitcast.124, pred[4096,4096]{0,1:T(8,128)(4,1)} %broadcast_compare_fusion.3, f32[2,1,4096,128]{3,2,0,1:T(8,128)} %get-tuple-element.381, ...), kind=kOutput, calls=%fused_computation.11.clone.1 | convolution fusion | flops 8726249472 | bytes 161546240 | tf_op jit(solution)/shard_map/while/body/eval_jaxpr/grqk,kgd->grqd/dot_general | solution.py:256
  703.8 0.0 collective-permute-start.1
  703.9 12.3 broadcast_compare_fusion.3
  716.2 31.6 %collective-permute-done = bf16[4096,2,128]{2,0,1:T(8,128)(2,1)} collective-permute-done((bf16[4096,2,128]{2,0,1:T(8,128)(2,1)}, bf16[4096,2,128]{2,0,1:T(8,128)(2,1)}, u32[]{:S(2)}, u32[]{:S(2)}) %collective-permute-start) | collective-permute-done | bytes 2097184 | tf_op jit(solution)/shard_map/while/body/eval_jaxpr/ppermute | solution.py:293
  747.8 54.7 %fusion.80 = (f32[2,4096]{1,0:T(2,128)S(1)}, f32[2,4096,4096]{2,1,0:T(8,128)}) fusion(pred[4096,4096]{0,1:T(8,128)(4,1)} %broadcast_compare_fusion.3, bf16[4096,2,128]{2,0,1:T(8,128)(2,1)} %collective-permute-done, bf16[4096,2,1,128]{3,0,1,2:T(8,128)(2,1)} %get-tuple-element.399), kind=kOutput, calls=%fused_computation.5.clone.1 | convolution fusion | flops 8690589696 | bytes 155222016 | tf_op jit(solution)/shard_map/while/body/eval_jaxpr/qgrd,kgd->grqk/dot_general | solution.py:249
  802.6 46.2 %fusion.82 = f32[2,4096]{1,0:T(2,128)S(1)} fusion(f32[2,4096,4096]{2,1,0:T(8,128)} %get-tuple-element.358, f32[2,4096]{1,0:T(2,128)S(1)} %bitcast.123, pred[4096,4096]{0,1:T(8,128)(4,1)} %broadcast_compare_fusion.3), kind=kLoop, calls=%fused_computation.4.clone.1 | loop fusion | flops 134209536 | bytes 151060480 | tf_op jit(solution)/shard_map/while/body/eval_jaxpr/reduce_sum | solution.py:255
  848.8 0.1 bitcast_add_fusion.3
  848.8 3.0 copy.42
  851.9 0.0 collective-permute-done.1
  851.9 1.3 copy.43
  853.2 60.1 %fusion.83 = f32[2,1,4096,128]{3,2,0,1:T(8,128)} fusion(bf16[4096,2,128]{2,0,1:T(8,128)(2,1)S(1)} %collective-permute-done.1, f32[2,4096,4096]{2,1,0:T(8,128)} %get-tuple-element.358, f32[2,4096]{1,0:T(2,128)S(1)} %bitcast.124, pred[4096,4096]{0,1:T(8,128)(4,1)} %broadcast_compare_fusion.3, f32[2,1,4096,128]{3,2,0,1:T(8,128)} %get-tuple-element.381, ...), kind=kOutput, calls=%fused_computation.11.clone.1 | convolution fusion | flops 8726249472 | bytes 161546240 | tf_op jit(solution)/shard_map/while/body/eval_jaxpr/grqk,kgd->grqd/dot_general | solution.py:256
  913.3 15.6 convolution_bitcast_fusion
  928.9 0.1 reduce-scatter.2.cloned.1.call-update
  929.0 0.0 copy-start.2
  929.0 0.0 copy-start.3
  929.0 0.0 copy-start
  929.0 4.6 constant_dynamic-slice_fusion.2
  933.7 10.2 collective-permute-start.2
  943.9 4.4 constant_dynamic-slice_fusion.1
  948.4 0.0 collective-permute-start.3
  948.4 4.7 constant_dynamic-slice_fusion
  953.1 0.5 collective-permute-start.4
  953.6 0.3 fusion.53
  954.0 1.0 select_reduce_fusion.gate_ref
  954.9 0.9 convolution_select_fusion.rank_ref
  955.8 149.0 %reduce-scatter.2.cloned.1.call-done = f32[512,2048]{1,0:T(8,128)} async-done(((f32[4096,2048]{1,0:T(8,128)}), f32[512,2048]{1,0:T(8,128)}) %reduce-scatter.2.cloned.1.call-update) | async-done | bytes 4194320 | tf_op jit(solution)/shard_map/reduce_scatter | solution.py:303
  1104.8 4.2 add_convert_fusion.h_hbm
  1109.0 0.0 collective-permute-done.3.wux_hbm
  1109.0 0.0 collective-permute-done.4.wdx_hbm
  1109.0 579.7 %routed_experts.1 = (bf16[512,2048]{1,0:T(8,128)(2,1)}, bf16[32,128,2048]{2,1,0:T(8,128)(2,1)}, bf16[32,128,2048]{2,1,0:T(8,128)(2,1)}) custom-call(bf16[512,2048]{1,0:T(8,128)(2,1)} %add_convert_fusion.h_hbm, f32[64,512]{1,0:T(8,128)} %convolution_select_fusion.rank_ref, f32[64,512]{1,0:T(8,128)} %select_reduce_fusion.gate_ref, ...), custom_call_target="tpu_custom_call" | custom-call | flops 51539607552 | bytes 134217728 | tf_op jit(solution)/shard_map/routed_experts/pallas_call | solution.py:200
  1688.7 3.2 copy.48
  (29 shorter events, 0.3 us)
Async XLA Ops:
  6.5 86.6 %copy-start.6 = (bf16[2048,2,128]{2,1,0:T(2,128)(2,1)S(1)}, bf16[2048,2,128]{2,1,0:T(2,128)(2,1)}, u32[]{:S(2)}) copy-start(bf16[2048,2,128]{2,1,0:T(2,128)(2,1)} %param.14) | copy-start | bytes 3145732
  6.5 86.6 %all-gather.2.cloned.1.call-start = ((), (), s32[]{:S(2)}) async-start(), calls=%async_computation.1 | async-start | bytes 18874368 | tf_op jit(solution)/shard_map/all_gather | solution.py:279
  7.3 1097.5 %reduce-scatter.2.cloned.1.call-start = ((), (), s32[]{:S(2)}) async-start(), calls=%async_computation.2 | async-start | bytes 37748736 | tf_op jit(solution)/shard_map/reduce_scatter | solution.py:303
  93.1 10.5 copy-start.4
  93.1 10.8 copy-start.7
  103.9 5.7 copy-start.5
  163.7 46.4 %copy-start.8 = (bf16[2048,2,128]{2,1,0:T(2,128)(2,1)S(1)}, bf16[2048,2,128]{2,1,0:T(2,128)(2,1)}, u32[]{:S(2)}) copy-start(bf16[2048,2,128]{2,1,0:T(2,128)(2,1)} %param.15) | copy-start | bytes 3145732
  277.4 635.9 %copy-start.1 = (bf16[2,128,2048]{2,1,0:T(8,128)(2,1)S(1)}, bf16[2,128,2048]{2,1,0:T(8,128)(2,1)}, u32[]{:S(2)}) copy-start(bf16[2,128,2048]{2,1,0:T(8,128)(2,1)} %param.16) | copy-start | bytes 3145732
  277.6 48.4 %collective-permute-start = (bf16[4096,2,128]{2,0,1:T(8,128)(2,1)}, bf16[4096,2,128]{2,0,1:T(8,128)(2,1)}, u32[]{:S(2)}, u32[]{:S(2)}) collective-permute-start(bf16[4096,2,128]{2,0,1:T(8,128)(2,1)} %get-tuple-element.377), channel_id=1, source_target_pairs={{0,8},{8,16},{16,24},{24,0},{1,9},{9,17},{17,25},{25,1},{2,10},{10... | collective-permute-start | bytes 6291464 | tf_op jit(solution)/shard_map/while/body/eval_jaxpr/ppermute | solution.py:293
  279.1 151.0 %collective-permute-start.1 = (bf16[4096,2,128]{2,0,1:T(8,128)(2,1)}, bf16[4096,2,128]{2,0,1:T(8,128)(2,1)S(1)}, u32[]{:S(2)}, u32[]{:S(2)}) collective-permute-start(bf16[4096,2,128]{2,0,1:T(8,128)(2,1)} %get-tuple-element.378), channel_id=1, source_target_pairs={{0,8},{8,16},{16,24},{24,0},{1,9},{9,17},{17,25},{25,1},{2,10},{10... | collective-permute-start | bytes 6291464 | tf_op jit(solution)/shard_map/while/body/eval_jaxpr/ppermute | solution.py:294
  491.5 46.9 %collective-permute-start = (bf16[4096,2,128]{2,0,1:T(8,128)(2,1)}, bf16[4096,2,128]{2,0,1:T(8,128)(2,1)}, u32[]{:S(2)}, u32[]{:S(2)}) collective-permute-start(bf16[4096,2,128]{2,0,1:T(8,128)(2,1)} %get-tuple-element.377), channel_id=1, source_target_pairs={{0,8},{8,16},{16,24},{24,0},{1,9},{9,17},{17,25},{25,1},{2,10},{10... | collective-permute-start | bytes 6291464 | tf_op jit(solution)/shard_map/while/body/eval_jaxpr/ppermute | solution.py:293
  491.6 150.8 %collective-permute-start.1 = (bf16[4096,2,128]{2,0,1:T(8,128)(2,1)}, bf16[4096,2,128]{2,0,1:T(8,128)(2,1)S(1)}, u32[]{:S(2)}, u32[]{:S(2)}) collective-permute-start(bf16[4096,2,128]{2,0,1:T(8,128)(2,1)} %get-tuple-element.378), channel_id=1, source_target_pairs={{0,8},{8,16},{16,24},{24,0},{1,9},{9,17},{17,25},{25,1},{2,10},{10... | collective-permute-start | bytes 6291464 | tf_op jit(solution)/shard_map/while/body/eval_jaxpr/ppermute | solution.py:294
  703.8 44.0 %collective-permute-start = (bf16[4096,2,128]{2,0,1:T(8,128)(2,1)}, bf16[4096,2,128]{2,0,1:T(8,128)(2,1)}, u32[]{:S(2)}, u32[]{:S(2)}) collective-permute-start(bf16[4096,2,128]{2,0,1:T(8,128)(2,1)} %get-tuple-element.377), channel_id=1, source_target_pairs={{0,8},{8,16},{16,24},{24,0},{1,9},{9,17},{17,25},{25,1},{2,10},{10... | collective-permute-start | bytes 6291464 | tf_op jit(solution)/shard_map/while/body/eval_jaxpr/ppermute | solution.py:293
  703.8 148.0 %collective-permute-start.1 = (bf16[4096,2,128]{2,0,1:T(8,128)(2,1)}, bf16[4096,2,128]{2,0,1:T(8,128)(2,1)S(1)}, u32[]{:S(2)}, u32[]{:S(2)}) collective-permute-start(bf16[4096,2,128]{2,0,1:T(8,128)(2,1)} %get-tuple-element.378), channel_id=1, source_target_pairs={{0,8},{8,16},{16,24},{24,0},{1,9},{9,17},{17,25},{25,1},{2,10},{10... | collective-permute-start | bytes 6291464 | tf_op jit(solution)/shard_map/while/body/eval_jaxpr/ppermute | solution.py:294
  929.0 24.6 %copy-start.2 = (s32[512,8]{0,1:T(8,128)S(1)}, s32[512,8]{0,1:T(8,128)}, u32[]{:S(2)}) copy-start(s32[512,8]{0,1:T(8,128)} %param.17) | copy-start | bytes 49156
  929.0 24.9 %copy-start.3 = (f32[512,8]{0,1:T(8,128)S(1)}, f32[512,8]{0,1:T(8,128)}, u32[]{:S(2)}) copy-start(f32[512,8]{0,1:T(8,128)} %param.18) | copy-start | bytes 49156
  929.0 175.8 %copy-start = (bf16[512,2048]{1,0:T(8,128)(2,1)S(1)}, bf16[512,2048]{1,0:T(8,128)(2,1)}, u32[]{:S(2)}) copy-start(bf16[512,2048]{1,0:T(8,128)(2,1)} %param.12) | copy-start | bytes 6291460
  933.7 175.3 %collective-permute-start.2 = (bf16[2,2048,512]{2,1,0:T(8,128)(2,1)}, bf16[2,2048,512]{2,1,0:T(8,128)(2,1)}, u32[]{:S(2)}, u32[]{:S(2)}) collective-permute-start(bf16[2,2048,512]{2,1,0:T(8,128)(2,1)} %constant_dynamic-slice_fusion.2), channel_id=1, source_target_pairs={{0,1},{1,0},{2,3},{3,2},{4,5},{5,4},{6,7},{7,6},{8,9},{9,8},{10,11... | collective-permute-start | bytes 12582920 | tf_op jit(solution)/shard_map/ppermute | solution.py:310
  948.4 160.7 %collective-permute-start.3 = (bf16[2,2048,512]{2,1,0:T(8,128)(2,1)}, bf16[2,2048,512]{2,1,0:T(8,128)(2,1)}, u32[]{:S(2)}, u32[]{:S(2)}) collective-permute-start(bf16[2,2048,512]{2,1,0:T(8,128)(2,1)} %constant_dynamic-slice_fusion.1), channel_id=1, source_target_pairs={{0,1},{1,0},{2,3},{3,2},{4,5},{5,4},{6,7},{7,6},{8,9},{9,8},{10,11... | collective-permute-start | bytes 12582920 | tf_op jit(solution)/shard_map/ppermute | solution.py:310
  953.1 155.9 %collective-permute-start.4 = (bf16[2,512,2048]{2,1,0:T(8,128)(2,1)}, bf16[2,512,2048]{2,1,0:T(8,128)(2,1)}, u32[]{:S(2)}, u32[]{:S(2)}) collective-permute-start(bf16[2,512,2048]{2,1,0:T(8,128)(2,1)} %constant_dynamic-slice_fusion), channel_id=1, source_target_pairs={{0,1},{1,0},{2,3},{3,2},{4,5},{5,4},{6,7},{7,6},{8,9},{9,8},{10,11... | collective-permute-start | bytes 12582920 | tf_op jit(solution)/shard_map/ppermute | solution.py:310
Sparse Core Ops, SparseCore 0:
  9.0 84.1 all-gather.1
  929.1 175.6 reduce-scatter.1

commit v2 on v1

--- a/solution.py
+++ b/solution.py
@@ -192,6 +192,7 @@
     n_dev = n_cp * n_tp
     tok_dev, hid = h_loc.shape
     half_f = w_gate.shape[2]
+    cap = 8 * tok_dev // rank_rows.shape[0]
     group = 4
     any_spec = pl.BlockSpec(memory_space=pl.ANY)
     vmem_spec = pl.BlockSpec(memory_space=pltpu.VMEM)
@@ -238,23 +239,401 @@
     return jnp.where(mask, rank, -1.0), gate_rows
 
 
-def seq_positions(cp_index, n_cp, half_len):
-    chunk_len = half_len // 2
-    in_half = jnp.arange(half_len)
-    return jnp.where(in_half < chunk_len, cp_index * chunk_len + in_half, (2 * n_cp - 1 - cp_index) * chunk_len + in_half - chunk_len)
-
-
-def attend_block(q_loc, k_blk, v_blk, q_pos, k_pos, run_max, run_sum, run_acc):
-    head_dim = q_loc.shape[-1]
-    scores = jnp.einsum("qgrd,kgd->grqk", q_loc, k_blk, preferred_element_type=jnp.float32) * (head_dim ** -0.5)
-    allowed = q_pos[:, None] >= k_pos[None, :]
-    scores = jnp.where(allowed, scores, -1e30)
-    new_max = jnp.maximum(run_max, jnp.max(scores, axis=-1))
-    prob_vals = jnp.exp(scores - new_max[..., None])
-    rescale = jnp.exp(run_max - new_max)
-    new_sum = run_sum * rescale + jnp.sum(prob_vals, axis=-1)
-    new_acc = run_acc * rescale[..., None] + jnp.einsum("grqk,kgd->grqd", prob_vals.astype(jnp.bfloat16), v_blk, preferred_element_type=jnp.float32)
-    return new_max, new_sum, new_acc
+def block_of(cp_pos, tp_pos, n_cp, n_tp):
+    per_chunk = n_tp // 2
+    late = tp_pos // per_chunk
+    chunk = late * (2 * n_cp - 1 - cp_pos) + (1 - late) * cp_pos
+    return chunk * per_chunk + tp_pos % per_chunk
+
+
+def owner_of(block, n_cp, n_tp):
+    per_chunk = n_tp // 2
+    chunk = block // per_chunk
+    late = chunk // n_cp
+    return late * (2 * n_cp - 1 - chunk) + (1 - late) * chunk, late * per_chunk + block % per_chunk
+
+
+def front_kernel(n_cp, n_tp, x_hbm, w_ref, k_hbm, vt_hbm, q_hbm, x_buf, q_st, k_st, vt_st,
+                 own_sem, ring_sem, pair_sem, rx_sem, sk_sem, sv_sem, sq_sem, kv_sem, rq_sem, sf_sem, rf_sem):
+    n_x = n_tp // 2
+    tok_dev, hid = x_hbm.shape
+    half = tok_dev // 2
+    head_dim = k_hbm.shape[1]
+    n_loc = q_st.shape[1]
+    chunk_len = tok_dev * n_x
+    cp_pos, tp_pos = lax.axis_index("cp"), lax.axis_index("tp")
+    x_pos, core = tp_pos // 2, tp_pos % 2
+    sibling = 2 * x_pos + 1 - core
+    barrier = pltpu.get_barrier_semaphore()
+
+    def slot_at(off, flip):
+        return 2 * ((x_pos + off + n_x) % n_x) + (core + flip) % 2
+
+    own_copy = pltpu.make_async_copy(x_hbm, x_buf.at[tp_pos], own_sem)
+    own_copy.start()
+    for step in (1, n_x - 1):
+        pl.semaphore_signal(barrier, inc=1, device_id=mesh_id(cp_pos, slot_at(step, 0)), device_id_type=MESH)
+    for step in range(1, 2 * n_cp):
+        pl.semaphore_signal(barrier, inc=1, device_id=mesh_id((cp_pos + step // 2) % n_cp, 2 * x_pos + (core + step) % 2), device_id_type=MESH)
+    pl.semaphore_wait(barrier, 2 * n_cp + 1)
+
+    def own_send(part, to_tp, sem):
+        rows = pl.ds(part * half, half)
+        return pltpu.make_async_remote_copy(x_hbm.at[rows], x_buf.at[tp_pos, rows], sem, rx_sem.at[tp_pos, part],
+                                            device_id=mesh_id(cp_pos, to_tp), device_id_type=MESH)
+
+    def pass_on(slot, part, to_tp, sem):
+        rows = pl.ds(pl.multiple_of(part * half, half), half)
+        return pltpu.make_async_remote_copy(x_buf.at[slot, rows], x_buf.at[slot, rows], sem, rx_sem.at[slot, part],
+                                            device_id=mesh_id(cp_pos, to_tp), device_id_type=MESH)
+
+    for i, (part, off) in enumerate(((0, 1), (1, -1), (1, 1), (0, -1))):
+        own_send(part, slot_at(off, 0), ring_sem.at[i]).start()
+    for part in range(2):
+        own_send(part, sibling, pair_sem.at[part]).start()
+
+    def place_of(step):
+        wave, other, side = step // 4, (step // 2) % 2, step % 2
+        near = ((wave + 1) // 2) % 2
+        swap = (wave // 2) * (1 - wave // 3)
+        off = near * (2 * side - 1) + 2 * (wave // 3)
+        return slot_at(off, other), side + swap * (1 - 2 * side), off
+
+    def outputs_of(step):
+        slot, part, _ = place_of(step)
+        block = block_of(cp_pos, slot, n_cp, n_tp)
+        pos = block * tok_dev + part * half
+        q_core = ((block % 4 + 1) // 2) % 2
+        q_pos = (2 * (block // 4) + (block % 4) // 2) * tok_dev + part * half
+        pos, q_pos = pl.multiple_of(pos, half), pl.multiple_of(q_pos, half)
+        for i in range(n_loc):
+            to_cp = n_loc * core + i
+            for src, dst, s_sem, r_sem, to_core in (
+                (k_st.at[step, i], k_hbm.at[pl.ds(pos, half)], sk_sem.at[i], kv_sem.at[cp_pos], 0),
+                (vt_st.at[step, i], vt_hbm.at[:, pl.ds(pos, half)], sv_sem.at[i], kv_sem.at[cp_pos], 1),
+                (q_st.at[step, i], q_hbm.at[pl.ds(q_pos, half)], sq_sem.at[i, q_core], rq_sem.at[cp_pos], q_core),
+            ):
+                here = jnp.logical_and(to_cp == cp_pos, to_core == core)
+
+                @pl.when(here)
+                def _():
+                    pltpu.make_async_copy(src, dst, r_sem).start()
+
+                @pl.when(jnp.logical_not(here))
+                def _():
+                    pltpu.make_async_remote_copy(src, dst, s_sem, r_sem, device_id=mesh_id(to_cp, 2 * x_pos + to_core),
+                                                 device_id_type=MESH).start()
+
+    def project(step, carry):
+        slot, part, off = place_of(step)
+        wave, other, side = step // 4, (step // 2) % 2, step % 2
+
+        @pl.when(step == 0)
+        def _():
+            own_copy.wait()
+
+        @pl.when(step > 1)
+        def _():
+            pass_on(slot, part, sibling, pair_sem.at[0]).wait_recv()
+
+        @pl.when(jnp.logical_and(wave > 0, other == 0))
+        def _():
+            @pl.when(wave == 1)
+            def _():
+                pass_on(slot, part, slot_at(-off, 0), ring_sem.at[4 + side]).start()
+            pass_on(slot, part, sibling, pair_sem.at[2 * wave + side]).start()
+
+        x_rows = x_buf[slot, pl.ds(pl.multiple_of(part * half, half), half), :]
+        qkv = jnp.dot(x_rows, w_ref[...], preferred_element_type=jnp.float32)
+        for i in range(n_loc):
+            q_st[step, i] = qkv[:, i * head_dim:(i + 1) * head_dim].astype(jnp.bfloat16)
+            k_st[step, i] = qkv[:, (n_loc + i) * head_dim:(n_loc + i + 1) * head_dim].astype(jnp.bfloat16)
+            vt_st[step, i] = qkv[:, (2 * n_loc + i) * head_dim:(2 * n_loc + i + 1) * head_dim].T.astype(jnp.bfloat16)
+
+        @pl.when(step > 0)
+        def _():
+            outputs_of(step - 1)
+        return carry
+
+    n_steps = 2 * n_tp
+    lax.fori_loop(0, n_steps, project, 0)
+    outputs_of(n_steps - 1)
+
+    def whole(ref, count, sem):
+        return pltpu.make_async_copy(ref.at[pl.ds(0, count)], ref.at[pl.ds(0, count)], sem)
+
+    def forward(y, place, core_id):
+        chunk = y if place == 0 else 2 * n_cp - 1 - y
+        cols = pl.ds(chunk * chunk_len, chunk_len)
+        ref = k_hbm.at[cols] if core_id == 0 else vt_hbm.at[:, cols]
+        return pltpu.make_async_remote_copy(ref, ref, sf_sem.at[2 * y + place], rf_sem.at[2 * y + place],
+                                            device_id=mesh_id(cp_pos, sibling), device_id_type=MESH)
+
+    for y in range(n_cp):
+        whole(k_hbm, 2 * chunk_len, kv_sem.at[y]).wait()
+        for core_id in range(2):
+            @pl.when(core == core_id)
+            def _():
+                for place in range(2):
+                    forward(y, place, core_id).start()
+    for y in range(n_cp):
+        whole(q_hbm, chunk_len, rq_sem.at[y]).wait()
+    for i in range(4):
+        own_send(0, sibling, ring_sem.at[i]).wait_send()
+    for i in range(2):
+        own_send(0, sibling, ring_sem.at[4 + i]).wait_send()
+    for i in range(8):
+        own_send(0, sibling, pair_sem.at[i]).wait_send()
+    for i in range(n_loc):
+        to_cp = n_loc * core + i
+        for sem, to_core, count in ((sk_sem.at[i], 0, 2 * chunk_len), (sv_sem.at[i], 1, 2 * chunk_len),
+                                    (sq_sem.at[i, 0], 0, chunk_len), (sq_sem.at[i, 1], 1, chunk_len)):
+            @pl.when(jnp.logical_not(jnp.logical_and(to_cp == cp_pos, to_core == core)))
+            def _():
+                whole(k_hbm, count, sem).wait()
+    for core_id in range(2):
+        @pl.when(core == core_id)
+        def _():
+            for y in range(n_cp):
+                for place in range(2):
+                    forward(y, place, core_id).wait_send()
+                    forward(y, place, 1 - core_id).wait_recv()
+
+
+def front_call(n_cp, n_tp, x_loc, w_qkv, head_dim, n_loc):
+    tok_dev, hid = x_loc.shape
+    half = tok_dev // 2
+    seq = tok_dev * n_cp * n_tp
+    any_spec = pl.BlockSpec(memory_space=pl.ANY)
+    n_steps = 2 * n_tp
+    return pl.pallas_call(
+        functools.partial(front_kernel, n_cp, n_tp),
+        name="gather_project",
+        out_shape=(jax.ShapeDtypeStruct((seq, head_dim), jnp.bfloat16), jax.ShapeDtypeStruct((head_dim, seq), jnp.bfloat16),
+                   jax.ShapeDtypeStruct((seq // 2, head_dim), jnp.bfloat16)),
+        in_specs=[any_spec, pl.BlockSpec(memory_space=pltpu.VMEM)],
+        out_specs=(any_spec, any_spec, any_spec),
+        scratch_shapes=[
+            pltpu.VMEM((n_tp, tok_dev, hid), jnp.bfloat16),
+            pltpu.VMEM((n_steps, n_loc, half, head_dim), jnp.bfloat16),
+            pltpu.VMEM((n_steps, n_loc, half, head_dim), jnp.bfloat16),
+            pltpu.VMEM((n_steps, n_loc, head_dim, half), jnp.bfloat16),
+            pltpu.SemaphoreType.DMA,
+            pltpu.SemaphoreType.DMA((6,)),
+            pltpu.SemaphoreType.DMA((8,)),
+            pltpu.SemaphoreType.DMA((n_tp, 2)),
+            pltpu.SemaphoreType.DMA((n_loc,)),
+            pltpu.SemaphoreType.DMA((n_loc,)),
+            pltpu.SemaphoreType.DMA((n_loc, 2)),
+            pltpu.SemaphoreType.DMA((n_cp,)),
+            pltpu.SemaphoreType.DMA((n_cp,)),
+            pltpu.SemaphoreType.DMA((2 * n_cp,)),
+            pltpu.SemaphoreType.DMA((2 * n_cp,)),
+        ],
+        compiler_params=pltpu.CompilerParams(collective_id=0, has_side_effects=True, vmem_limit_bytes=VMEM_LIMIT),
+        cost_estimate=pl.CostEstimate(flops=2 * n_tp * tok_dev * hid * w_qkv.shape[1], bytes_accessed=2**26, transcendentals=0),
+    )(x_loc, w_qkv)
+
+
+def attend_kernel(n_cp, n_tp, k_hbm, vt_hbm, q_hbm, x_hbm, wo_hbm, wg_hbm, wu_hbm, wd_hbm,
+                  h_ref, o_hbm, wgx_hbm, wux_hbm, wdx_hbm,
+                  k_buf, vt_buf, q_buf, qt_buf, o_st, o_buf, wo_buf, x_buf, s_even, s_odd, acc, m_ref, l_ref,
+                  in_sem, so_sem, ro_sem, swo_sem, rwo_sem, sw_sem, rw_sem, o_sem):
+    n_dev = n_cp * n_tp
+    n_x = n_tp // 2
+    tok_dev, hid = x_buf.shape
+    head_dim = k_buf.shape[1]
+    n_heads = o_buf.shape[0]
+    cp_pos, tp_pos = lax.axis_index("cp"), lax.axis_index("tp")
+    x_pos, core = tp_pos // 2, tp_pos % 2
+    head = n_cp * x_pos + cp_pos
+    scale = (head_dim ** -0.5) * 1.4426950408889634
+    barrier = pltpu.get_barrier_semaphore()
+
+    loads = [pltpu.make_async_copy(src, dst, in_sem.at[i]) for i, (src, dst) in enumerate(
+        ((q_hbm, q_buf), (k_hbm, k_buf), (vt_hbm, vt_buf), (x_hbm, x_buf), (wo_hbm, wo_buf.at[tp_pos])))]
+    for one in loads:
+        one.start()
+
+    def signal_peer(step, carry):
+        to_cp, to_tp = peer_of(step, cp_pos, tp_pos, n_cp, n_tp, 1)
+        pl.semaphore_signal(pltpu.get_barrier_semaphore(), inc=1, device_id=mesh_id(to_cp, to_tp), device_id_type=MESH)
+        return carry
+
+    lax.fori_loop(1, n_dev, signal_peer, 0)
+    pl.semaphore_wait(barrier, n_dev - 1)
+
+    def wo_send(step):
+        return pltpu.make_async_remote_copy(wo_hbm, wo_buf.at[tp_pos], swo_sem.at[step], rwo_sem.at[step],
+                                            device_id=mesh_id(cp_pos, (tp_pos + step) % n_tp), device_id_type=MESH)
+
+    def wo_arrival(step):
+        return pltpu.make_async_remote_copy(wo_hbm, wo_buf.at[(tp_pos + n_tp - step) % n_tp], swo_sem.at[step], rwo_sem.at[step],
+                                            device_id=mesh_id(cp_pos, tp_pos), device_id_type=MESH)
+
+    keep = wgx_hbm.shape[0]
+    swaps = [pltpu.make_async_remote_copy(src.at[pl.ds((1 - core) * keep, keep)], dst, sw_sem.at[i], rw_sem.at[i],
+                                          device_id=mesh_id(cp_pos, 2 * x_pos + 1 - core), device_id_type=MESH)
+             for i, (src, dst) in enumerate(((wg_hbm, wgx_hbm), (wu_hbm, wux_hbm), (wd_hbm, wdx_hbm)))]
+    for step in range(1, n_tp):
+        wo_send(step).start()
+    for one in swaps:
+        one.start()
+    for one in loads[:3]:
+        one.wait()
+
+    def update(s_vals, s_top, v_cols, lo, width):
+        cols = pl.ds(lo, width)
+        m_old = m_ref[:, cols]
+        m_new = jnp.maximum(m_old, s_top)
+        prob = jnp.exp2((s_vals - m_new) * scale)
+        shrink = jnp.exp2((m_old - m_new) * scale)
+        m_ref[:, cols] = m_new
+        l_ref[:, cols] = l_ref[:, cols] * shrink + jnp.sum(prob, axis=0, keepdims=True)
+        acc[:, cols] = acc[:, cols] * shrink + jnp.dot(v_cols, prob.astype(jnp.bfloat16), preferred_element_type=jnp.float32)
+
+    def keys_at(block):
+        return k_buf[pl.ds(pl.multiple_of(block * tok_dev, tok_dev), tok_dev), :]
+
+    def values_at(block):
+        return vt_buf[:, pl.ds(pl.multiple_of(block * tok_dev, tok_dev), tok_dev)]
+
+    def query_pair(g, carry):
+        q_rows = q_buf[pl.ds(pl.multiple_of(g * 2 * tok_dev, 2 * tok_dev), 2 * tok_dev), :]
+        qt_buf[...] = q_rows.astype(jnp.float32).T.astype(jnp.bfloat16)
+        m_ref[...] = jnp.full_like(m_ref, -1e30)
+        l_ref[...] = jnp.zeros_like(l_ref)
+        acc[...] = jnp.zeros_like(acc)
+        for r in range(2):
+            lo = r * tok_dev
+            inner = (1 - core) * 3 * r + core * (1 + r)
+
+            def near_scores(block):
+                return jnp.dot(keys_at(block), qt_buf[:, pl.ds(lo, tok_dev)], preferred_element_type=jnp.float32)
+
+            s_vals = near_scores(4 * g + inner)
+            key_id = lax.broadcasted_iota(jnp.int32, s_vals.shape, 0)
+            query_id = lax.broadcasted_iota(jnp.int32, s_vals.shape, 1)
+            s_vals = jnp.where(key_id <= query_id, s_vals, -1e30)
+            update(s_vals, jnp.max(s_vals, axis=0, keepdims=True), values_at(4 * g + inner), lo, tok_dev)
+
+            def near_block(j, inner_carry):
+                s_near = near_scores(4 * g + j)
+                update(s_near, jnp.max(s_near, axis=0, keepdims=True), values_at(4 * g + j), lo, tok_dev)
+                return inner_carry
+
+            lax.fori_loop(0, inner, near_block, 0)
+
+        def far_scores(block, s_ref):
+            s_vals = jnp.dot(keys_at(block), qt_buf[...], preferred_element_type=jnp.float32)
+            s_ref[...] = s_vals
+            return jnp.max(s_vals, axis=0, keepdims=True)
+
+        def far_pair(n, top_even):
+            top_odd = far_scores(2 * n + 1, s_odd)
+            update(s_even[...], top_even, values_at(2 * n), 0, 2 * tok_dev)
+            top_next = far_scores(2 * n + 2, s_even)
+            update(s_odd[...], top_odd, values_at(2 * n + 1), 0, 2 * tok_dev)
+            return top_next
+
+        lax.fori_loop(0, 2 * g, far_pair, far_scores(0, s_even))
+        out = (acc[...] / l_ref[...]).T.astype(jnp.bfloat16)
+        for r in range(2):
+            o_st[2 * g + r] = out[r * tok_dev:(r + 1) * tok_dev]
+            o_push(2 * g + r, "start")
+        return carry
+
+    def o_push(index, what):
+        block = 4 * (index // 2) + (1 - core) * 3 * (index % 2) + core * (1 + index % 2)
+        to_cp, to_tp = owner_of(block, n_cp, n_tp)
+        here = jnp.logical_and(to_cp == cp_pos, to_tp == tp_pos)
+        if what == "start":
+            @pl.when(here)
+            def _():
+                pltpu.make_async_copy(o_st.at[index], o_hbm.at[head], ro_sem.at[head]).start()
+
+        @pl.when(jnp.logical_not(here))
+        def _():
+            copy = pltpu.make_async_remote_copy(o_st.at[index], o_hbm.at[head], so_sem.at[index], ro_sem.at[head],
+                                                device_id=mesh_id(to_cp, to_tp), device_id_type=MESH)
+            if what == "start":
+                copy.start()
+            else:
+                copy.wait_send()
+
+    lax.fori_loop(0, n_dev // 4, query_pair, 0)
+
+    for step in range(1, n_tp):
+        wo_arrival(step).wait_recv()
+    for one in loads[3:]:
+        one.wait()
+    for j in range(n_heads):
+        pltpu.make_async_copy(o_hbm.at[j], o_hbm.at[j], ro_sem.at[j]).wait()
+    o_load = pltpu.make_async_copy(o_hbm, o_buf, o_sem)
+    o_load.start()
+    o_load.wait()
+    o_rows = jnp.concatenate([o_buf[j] for j in range(n_heads)], axis=1)
+    n_cols = min(512, hid)
+
+    for col in range(0, hid, n_cols):
+        cols = pl.ds(col, n_cols)
+        w_cols = wo_buf[:, :, cols].reshape(n_heads * head_dim, n_cols)
+        h_ref[:, cols] = (x_buf[:, cols].astype(jnp.float32) + jnp.dot(o_rows, w_cols, preferred_element_type=jnp.float32)).astype(jnp.bfloat16)
+
+    for step in range(1, n_tp):
+        wo_send(step).wait_send()
+    for one in swaps:
+        one.wait()
+
+    def drain(index, carry):
+        o_push(index, "wait")
+        return carry
+
+    lax.fori_loop(0, n_dev // 2, drain, 0)
+
+
+def attend_call(n_cp, n_tp, k_all, vt_all, q_all, x_loc, wo_loc, w_gate, w_up, w_down):
+    n_dev = n_cp * n_tp
+    tok_dev, hid = x_loc.shape
+    seq, head_dim = k_all.shape
+    n_heads = n_tp * wo_loc.shape[0] // head_dim
+    keep = w_gate.shape[0] // 2
+    any_spec = pl.BlockSpec(memory_space=pl.ANY)
+    bf16 = jnp.bfloat16
+    h_loc, _, wg_other, wu_other, wd_other = pl.pallas_call(
+        functools.partial(attend_kernel, n_cp, n_tp),
+        name="attend_heads",
+        out_shape=(jax.ShapeDtypeStruct((tok_dev, hid), bf16), jax.ShapeDtypeStruct((n_heads, tok_dev, head_dim), bf16))
+        + tuple(jax.ShapeDtypeStruct((keep,) + w.shape[1:], bf16) for w in (w_gate, w_up, w_down)),
+        in_specs=[any_spec] * 8,
+        out_specs=(pl.BlockSpec(memory_space=pltpu.VMEM),) + (any_spec,) * 4,
+        scratch_shapes=[
+            pltpu.VMEM((seq, head_dim), bf16),
+            pltpu.VMEM((head_dim, seq), bf16),
+            pltpu.VMEM((seq // 2, head_dim), bf16),
+            pltpu.VMEM((head_dim, 2 * tok_dev), bf16),
+            pltpu.VMEM((n_dev // 2, tok_dev, head_dim), bf16),
+            pltpu.VMEM((n_heads, tok_dev, head_dim), bf16),
+            pltpu.VMEM((n_tp,) + wo_loc.shape, bf16),
+            pltpu.VMEM((tok_dev, hid), bf16),
+            pltpu.VMEM((tok_dev, 2 * tok_dev), jnp.float32),
+            pltpu.VMEM((tok_dev, 2 * tok_dev), jnp.float32),
+            pltpu.VMEM((head_dim, 2 * tok_dev), jnp.float32),
+            pltpu.VMEM((1, 2 * tok_dev), jnp.float32),
+            pltpu.VMEM((1, 2 * tok_dev), jnp.float32),
+            pltpu.SemaphoreType.DMA((5,)),
+            pltpu.SemaphoreType.DMA((n_dev // 2,)),
+            pltpu.SemaphoreType.DMA((n_heads,)),
+            pltpu.SemaphoreType.DMA((n_tp,)),
+            pltpu.SemaphoreType.DMA((n_tp,)),
+            pltpu.SemaphoreType.DMA((3,)),
+            pltpu.SemaphoreType.DMA((3,)),
+            pltpu.SemaphoreType.DMA,
+        ],
+        compiler_params=pltpu.CompilerParams(collective_id=1, has_side_effects=True, vmem_limit_bytes=VMEM_LIMIT),
+        cost_estimate=pl.CostEstimate(flops=2 * seq * seq * head_dim // 2, bytes_accessed=2**26, transcendentals=seq * seq // 4),
+    )(k_all, vt_all, q_all, x_loc, wo_loc, w_gate, w_up, w_down)
+    return h_loc, wg_other, wu_other, wd_other
 
 
 def solution(mesh):
@@ -266,48 +645,13 @@
 
     def device_step(x_loc, w_q, w_k, w_v, w_o, ids_loc, gates_loc, w_gate, w_up, w_down):
         tok_dev, hid_dim = x_loc.shape
-        top_k = ids_loc.shape[1]
-        kv_loc = w_k.shape[1]
-        head_dim = w_q.shape[2]
-        grp_size = w_q.shape[1] // kv_loc
-        local_exp = w_gate.shape[0]
-        n_experts = local_exp * n_cp * n_tp // 2
-        capacity = top_k * tok_dev // n_experts
-        cp_index = lax.axis_index("cp")
-        tp_index = lax.axis_index("tp")
-
-        x_half = lax.all_gather(x_loc, "tp", axis=0, tiled=True)
-        half_len = x_half.shape[0]
-        q_loc = jnp.einsum("sh,hnd->snd", x_half, w_q, preferred_element_type=jnp.float32).astype(jnp.bfloat16).reshape(half_len, kv_loc, grp_size, head_dim)
-        k_cur = jnp.einsum("sh,hnd->snd", x_half, w_k, preferred_element_type=jnp.float32).astype(jnp.bfloat16)
-        v_cur = jnp.einsum("sh,hnd->snd", x_half, w_v, preferred_element_type=jnp.float32).astype(jnp.bfloat16)
-        q_pos = seq_positions(cp_index, n_cp, half_len)
-        init_max = jnp.full((kv_loc, grp_size, half_len), -1e30, jnp.float32)
-        init_sum = jnp.zeros((kv_loc, grp_size, half_len), jnp.float32)
-        init_acc = jnp.zeros((kv_loc, grp_size, half_len, head_dim), jnp.float32)
-        first_state = attend_block(q_loc, k_cur, v_cur, q_pos, q_pos, init_max, init_sum, init_acc)
-        shift_perm = [(src_dev, (src_dev + 1) % n_cp) for src_dev in range(n_cp)]
-
-        def kv_step(step_idx, kv_state):
-            k_blk, v_blk, cur_max, cur_sum, cur_acc = kv_state
-            k_blk = lax.ppermute(k_blk, "cp", shift_perm)
-            v_blk = lax.ppermute(v_blk, "cp", shift_perm)
-            k_pos = seq_positions((cp_index - step_idx) % n_cp, n_cp, half_len)
-            cur_max, cur_sum, cur_acc = attend_block(q_loc, k_blk, v_blk, q_pos, k_pos, cur_max, cur_sum, cur_acc)
-            return k_blk, v_blk, cur_max, cur_sum, cur_acc
-
-        kv_state = lax.fori_loop(1, n_cp, kv_step, (k_cur, v_cur) + first_state)
-        attn_out = (kv_state[4] / kv_state[3][..., None]).astype(jnp.bfloat16)
-        w_o_view = w_o.reshape(kv_loc, grp_size, head_dim, hid_dim)
-        attn_part = jnp.einsum("grqd,grdh->qh", attn_out, w_o_view, preferred_element_type=jnp.float32)
-        attn_rows = lax.psum_scatter(attn_part, "tp", scatter_dimension=0, tiled=True)
-        h_loc = (x_loc.astype(jnp.float32) + attn_rows).astype(jnp.bfloat16)
-
+        n_loc, head_dim = w_q.shape[1:]
+        n_experts = w_gate.shape[0] * n_cp * n_tp // 2
+        capacity = ids_loc.shape[1] * tok_dev // n_experts
+        w_qkv = jnp.concatenate([w.reshape(hid_dim, n_loc * head_dim) for w in (w_q, w_k, w_v)], axis=1)
         rank_rows, gate_rows = routing_rows(ids_loc, gates_loc, n_experts)
-        keep = local_exp // 2
-        give = (1 - tp_index % 2) * keep
-        pair_perm = [(dev_idx, dev_idx ^ 1) for dev_idx in range(n_tp)]
-        others = [lax.ppermute(lax.dynamic_slice_in_dim(w, give, keep, axis=0), "tp", pair_perm) for w in (w_gate, w_up, w_down)]
+        k_all, vt_all, q_all = front_call(n_cp, n_tp, x_loc, w_qkv, head_dim, n_loc)
+        h_loc, *others = attend_call(n_cp, n_tp, k_all, vt_all, q_all, x_loc, w_o.reshape(n_loc * head_dim, hid_dim), w_gate, w_up, w_down)
         return moe_call(n_cp, n_tp, capacity, h_loc, rank_rows, gate_rows, w_gate, w_up, w_down, *others)
 
     return jax.shard_map(device_step, mesh=mesh, in_specs=(row_spec, head_spec, head_spec, head_spec, P("tp", None, None), row_spec, row_spec, expert_spec, expert_spec, expert_spec), out_specs=row_spec, check_vma=False)

time: 1710 us -> 871 us (0.51)
  matrix products: 497 us -> 0.86 us
  waiting for transfers between devices: 321 us -> 0 us
  Pallas kernels: 580 us -> 857 us
  other arithmetic: 240 us -> 4.68 us
  local copies, waits for them, and re-layouts: 32.1 us -> 6.4 us
    dot_general x12 -> x0, matrix products: 496 us -> none  [the longest x4 237 us: attend_block(): jnp.einsum('grqk,kgd->grqd', prob_vals.astype(jnp.bfloat16), v_blk, prefe...]
    pallas_call x0 -> x2, Pallas kernels: none -> 257 us  [the longest x1 152 us: attend_call(): pl.pallas_call(functools.partial(attend_kernel, n_cp, n_tp), name='attend...]
    reduce_sum x4 -> x0, other arithmetic: 185 us -> none  [attend_block(): new_sum = run_sum * rescale + jnp.sum(prob_vals, axis=-1)]
    reduce_scatter x1 -> x0, waiting for transfers between devices: 149 us -> none  [device_step(): lax.psum_scatter(attn_part, 'tp', scatter_dimension=0, tiled=True)]
    ppermute x9 -> x0, waiting for transfers between devices: 98.1 us -> none  [the longest x3 98.1 us: kv_step(): k_blk = lax.ppermute(k_blk, 'cp', shift_perm)]
    all_gather x1 -> x0, waiting for transfers between devices: 73.4 us -> none  [device_step(): x_half = lax.all_gather(x_loc, 'tp', axis=0, tiled=True)]
    ge x4 -> x0, other arithmetic: 49.4 us -> none  [attend_block(): allowed = q_pos[:, None] >= k_pos[None, :]]
    pallas_call x1, Pallas kernels: 580 us -> 600 us  [moe_call(): pl.pallas_call(functools.partial(moe_kernel, n_cp, n_tp, group), name='ro...]
  transfers between devices with their start and end apart: 11 -> 0, of which waited for: 5 -> 0; matrix products, arithmetic and copies ran while one was open for 22% -> 0% of each run, Pallas kernels for 0% -> 0%
where the time goes in v2:
time: 871 us; the launch traced here: 869 us
  Pallas kernels  857 us (98%)
    pallas_call x1, Pallas kernels, moe_call(): pl.pallas_call(functools.partial(moe_kernel, n_cp, n_tp, group), name='ro...  600 us
    pallas_call x1, Pallas kernels, attend_call(): pl.pallas_call(functools.partial(attend_kernel, n_cp, n_tp), name='attend...  152 us
    pallas_call x1, Pallas kernels, front_call(): pl.pallas_call(functools.partial(front_kernel, n_cp, n_tp), name='gather_...  105 us

profile of v2, /device:TPU:103, one launch (start us, length us, event | category | flops | bytes accessed | tf_op | source)
XLA Modules:
  0.0 869.3 jit_solution(5566938759550303691)
XLA Ops:
  0.0 1.1 fusion
  1.1 0.9 convolution_select_fusion.rank_ref
  1.9 1.7 select_reduce_fusion.gate_ref
  3.7 1.4 copy.17
  5.0 1.9 copy_bitcast_fusion
  6.9 1.9 pad_maximum_fusion.w_ref
  8.8 104.6 %gather_project.1 = (bf16[16384,128]{1,0:T(8,128)(2,1)}, bf16[128,16384]{1,0:T(8,128)(2,1)}, bf16[8192,128]{1,0:T(8,128)(2,1)}) custom-call(bf16[512,2048]{1,0:T(8,128)(2,1)} %x_hbm.3, bf16[2048,768]{1,0:T(8,128)(2,1)} %pad_maximum_fusion.w_ref), custom_call_target="tpu_custom_call" | custom-call | flops 12884901888 | bytes 67108864 | tf_op jit(solution)/shard_map/gather_project/pallas_call | solution.py:409
  113.4 152.3 %attend_heads.1 = (bf16[512,2048]{1,0:T(8,128)(2,1)}, bf16[16,512,128]{2,1,0:T(8,128)(2,1)}, bf16[2,2048,512]{2,1,0:T(8,128)(2,1)}, bf16[2,2048,512]{2,1,0:T(8,128)(2,1)}, bf16[2,512,2048]{2,1,0:T(8,128)(2,1)}) custom-call(bf16[16384,128]{1,0:T(8,128)(2,1)} %get-tuple-element.13.k_hbm, bf16[128,16384]{1,0:T(8,128)(2,1)} %get-tuple-element.14.vt_hbm, ...), custom_call_target="tpu_custom_call" | custom-call | flops 34359738368 | bytes 67108864 | tf_op jit(solution)/shard_map/attend_heads/pallas_call | solution.py:603
  265.7 600.4 %routed_experts.1 = (bf16[512,2048]{1,0:T(8,128)(2,1)}, bf16[32,128,2048]{2,1,0:T(8,128)(2,1)}, bf16[32,128,2048]{2,1,0:T(8,128)(2,1)}) custom-call(bf16[512,2048]{1,0:T(8,128)(2,1)} %get-tuple-element.16.h_hbm, f32[64,512]{1,0:T(8,128)} %convolution_select_fusion.rank_ref, f32[64,512]{1,0:T(8,128)} %select_reduce_fusion.gate_ref, ...), custom_call_target="tpu_custom_call" | custom-call | flops 51539607552 | bytes 134217728 | tf_op jit(solution)/shard_map/routed_experts/pallas_call | solution.py:201
  866.1 3.2 copy.19

commit v3 on v2

v3 whole, which is shorter than its diff:
```python
import functools

import jax
import jax.numpy as jnp
from jax import lax
from jax.experimental import pallas as pl
from jax.experimental.pallas import tpu as pltpu
from jax.sharding import PartitionSpec as P

MESH = pl.DeviceIdType.MESH
PAIR = 2
BOTH = range(PAIR)
ROWS_ROWS = (((0,), (0,)), ((), ()))
VMEM_LIMIT = 66_000_000
PLACES = ((0, 0), (0, 1), (1, 0), (0, -1), (-1, 0), (1, 1), (0, 2), (2, 0), (1, 2), (2, 1), (2, -1), (-1, 2), (2, 2), (1, -1), (-1, 1), (-1, -1))
FIRST_FAR, N_FAR = 6, 7
SOURCES = (0, -1, 1, 2)


def peer_of(step, cp_pos, tp_pos, n_cp, n_tp):
    n_x = n_tp // PAIR
    off_x = (step // PAIR) % n_x
    off_y = (off_x + step // n_tp) % n_cp
    return (cp_pos + off_y) % n_cp, ((tp_pos // PAIR + off_x) % n_x) * 2 + (tp_pos % PAIR + step % PAIR) % PAIR


def mesh_id(cp_pos, tp_pos):
    return {"cp": cp_pos, "tp": tp_pos}


def enter_all(n_cp, n_tp):
    cp_pos, tp_pos = lax.axis_index("cp"), lax.axis_index("tp")

    def signal_peer(step, carry):
        to_cp, to_tp = peer_of(step, cp_pos, tp_pos, n_cp, n_tp)
        pl.semaphore_signal(pltpu.get_barrier_semaphore(), inc=1, device_id=mesh_id(to_cp, to_tp), device_id_type=MESH)
        return carry

    lax.fori_loop(1, n_cp * n_tp, signal_peer, 0)
    pl.semaphore_wait(pltpu.get_barrier_semaphore(), n_cp * n_tp - 1)


def pick(values, index):
    out = values[-1]
    for k, value in enumerate(values[:-1]):
        out = jnp.where(index == k, value, out)
    return out


def moe_kernel(n_cp, n_tp, group, h_hbm, rank_hbm, near_hbm, gate_ref, wg_hbm, wu_hbm, wd_hbm, wgx_hbm, wux_hbm, wdx_hbm,
               y_ref, rx_hbm, rl_hbm, rz_hbm, zl_hbm,
               h_buf, rank_buf, wg_buf, wu_buf, wd_buf, ring, own_stage, z_ring, x_buf, z_buf, acc, parts,
               w_sem, rank_sem, in_sem, x_sem, z_sem, hs_sem, hr_sem, ss_sem, rx_sem, rl_sem, fl_sem, sz_sem, rz_sem, zl_sem, fz_sem):
    n_x = n_tp // PAIR
    tok_dev, half_hid = h_buf.shape[2:]
    hid = PAIR * half_hid
    cap = ring.shape[3] // PAIR
    cp_pos, tp_pos = lax.axis_index("cp"), lax.axis_index("tp")
    x_pos, core = tp_pos // PAIR, tp_pos % PAIR
    half_tok = tok_dev // PAIR

    def at(off_y, off_x, flip):
        return (cp_pos + off_y + n_cp) % n_cp, PAIR * ((x_pos + off_x + n_x) % n_x) + (core + flip) % PAIR

    def line(place):
        return place[0] * n_tp + place[1]

    def send(src, dst, s_sem, r_sem, place):
        return pltpu.make_async_remote_copy(src, dst, s_sem, r_sem, device_id=mesh_id(*place), device_id_type=MESH)

    def await_bytes(ref, sem):
        pltpu.make_async_copy(ref, ref, sem).wait()

    h_loads = [pltpu.make_async_copy(h_hbm.at[part], h_buf.at[part, 0], in_sem.at[part]) for part in BOTH]
    rank_loads = []
    for part in BOTH:
        rank_loads.append(pltpu.make_async_copy(rank_hbm, rank_buf.at[part, 0], rank_sem.at[PAIR * part]))
        rank_loads.append(pltpu.make_async_copy(near_hbm.at[part, pl.ds(1, 3)], rank_buf.at[part, pl.ds(1, 3)], rank_sem.at[PAIR * part + 1]))
    w_loads = []
    for slot, (own, other, buf) in enumerate(((wg_hbm, wgx_hbm, wg_buf), (wu_hbm, wux_hbm, wu_buf), (wd_hbm, wdx_hbm, wd_buf))):
        w_loads.append(pltpu.make_async_copy(own.at[pl.ds(PAIR * core, 2)], buf.at[0], w_sem.at[PAIR * slot]))
        w_loads.append(pltpu.make_async_copy(other, buf.at[1], w_sem.at[PAIR * slot + 1]))
    for one in h_loads + rank_loads:
        one.start()
    enter_all(n_cp, n_tp)

    def along(part, off):
        return at(off, 0, 0) if part == 0 else at(0, off, 0)

    def across(part, off, flip):
        return at(0, off, flip) if part == 0 else at(off, 0, flip)

    def rows_of(piece):
        return pl.ds(piece * half_tok, half_tok)

    def spread(part, i):
        piece, off, slot = ((0, 1, 1), (1, -1, 2), (1, 1, 1), (0, -1, 2), (0, 1, 3), (1, -1, 3))[i]
        rows = rows_of(piece)
        src = h_hbm.at[part, rows] if i < 4 else h_buf.at[part, 1 if i == 4 else 2, rows]
        return send(src, h_buf.at[part, slot, rows], hs_sem.at[part, i], hr_sem.at[part, slot, piece], along(part, off))

    def await_h(part, slot, piece):
        await_bytes(h_buf.at[part, slot, rows_of(piece)], hr_sem.at[part, slot, piece])

    for i in range(4):
        for part in BOTH:
            spread(part, i).start()
    for one in w_loads:
        one.start()
    for one in h_loads + rank_loads:
        one.wait()

    slots = lax.broadcasted_iota(jnp.int32, (cap, tok_dev), 0).astype(jnp.float32)

    def gather_rows(part, stage, m):
        turn = m // PAIR
        off = turn + (turn // PAIR) * (5 - PAIR * turn)
        first = PAIR * line(across(part, off, m % PAIR))
        chosen = [jnp.where(rank_buf[part, stage, pl.ds(first + i, 1), :] == slots, 1.0, 0.0) for i in BOTH]
        chosen = jnp.concatenate(chosen, axis=0).astype(jnp.bfloat16)
        return jnp.dot(chosen, h_buf[part, stage], preferred_element_type=jnp.float32).astype(jnp.bfloat16)

    def source_line(part, stage, off):
        a = SOURCES[stage]
        return line(at(a, off, 0) if part == 0 else at(off, a, 0))

    def await_ring(part, stage):
        def one(m, carry):
            await_bytes(ring.at[part, stage % PAIR, m], ss_sem.at[part, stage % PAIR, m])
            return carry
        lax.fori_loop(1, 8, one, 0)

    def own_copy(part, stage):
        src_line = source_line(part, stage, 0)
        return pltpu.make_async_copy(own_stage.at[part, stage], rx_hbm.at[part, src_line], rx_sem.at[part, src_line])

    def run_stage(part, stage):
        side = stage % PAIR
        if stage >= 2:
            await_ring(part, stage)
        own_stage[part, stage] = gather_rows(part, stage, 0)

        def fill(m, carry):
            ring[part, side, m] = gather_rows(part, stage, m)
            return carry

        lax.fori_loop(1, 8, fill, 0)
        src_line = source_line(part, stage, 0)
        own_copy(part, stage).start()
        for m in (6, 7):
            for way, off in ((0, 1), (1, -1)):
                send(ring.at[part, side, m, pl.ds(way * cap, cap)], rl_hbm.at[part, way, stage, m % PAIR], ss_sem.at[part, side, m],
                     rl_sem.at[part, way, stage, m % PAIR], across(part, off, 0)).start()
        for m, off in ((2, 1), (4, -1), (3, 1), (5, -1), (1, 0)):
            send(ring.at[part, side, m], rx_hbm.at[part, src_line], ss_sem.at[part, side, m], rx_sem.at[part, src_line],
                 across(part, off, m % PAIR)).start()

    def relay(part, stage, way, flip):
        off = 1 - PAIR * way
        src_line = source_line(part, stage, -off)
        return send(rl_hbm.at[part, way, stage, flip], rx_hbm.at[part, src_line, pl.ds(way * cap, cap)], fl_sem.at[part, way, stage, flip],
                    rx_sem.at[part, src_line], across(part, off, flip))

    def run_relays(stage):
        for flip in BOTH:
            for way in BOTH:
                for part in BOTH:
                    await_bytes(rl_hbm.at[part, way, stage, flip], rl_sem.at[part, way, stage, flip])
                    relay(part, stage, way, flip).start()

    for part in BOTH:
        run_stage(part, 0)
    for part in BOTH:
        await_h(part, 1, 0)
        spread(part, 4).start()
    for part in BOTH:
        await_h(part, 2, 1)
        spread(part, 5).start()
    for part in BOTH:
        await_h(part, 1, 1)
        run_stage(part, 1)
    gate_all = gate_ref[...]
    high = gate_all.astype(jnp.bfloat16).astype(jnp.float32)
    rest = gate_all - high
    mid = rest.astype(jnp.bfloat16).astype(jnp.float32)
    parts[0] = high
    parts[1] = mid
    parts[2] = rest - mid
    for part in BOTH:
        acc[:, part * half_hid:(part + 1) * half_hid] = h_buf[part, 0].astype(jnp.float32)
    run_relays(0)
    for part in BOTH:
        await_h(part, 2, 0)
        run_stage(part, 2)
    run_relays(1)
    for part in BOTH:
        await_h(part, 3, 0)
        await_h(part, 3, 1)
        run_stage(part, 3)
    run_relays(2)
    for one in w_loads:
        one.wait()

    rows = group * cap
    n_cols = min(512, hid)
    n_groups = len(PLACES) // PAIR

    def expert_rows(slot, i):
        x_rows = x_buf[:, pl.ds(i * cap, cap), :].reshape(rows, hid)
        hidden = []
        for half in BOTH:
            gate_pre = jnp.dot(x_rows, wg_buf[half, i], preferred_element_type=jnp.float32)
            up_pre = jnp.dot(x_rows, wu_buf[half, i], preferred_element_type=jnp.float32)
            hidden.append((gate_pre * (1.0 / (1.0 + jnp.exp(-gate_pre))) * up_pre).astype(jnp.bfloat16))
        for col in range(0, hid, n_cols):
            z_rows = (jnp.dot(hidden[0], wd_buf[0, i, :, pl.ds(col, n_cols)], preferred_element_type=jnp.float32)
                      + jnp.dot(hidden[1], wd_buf[1, i, :, pl.ds(col, n_cols)], preferred_element_type=jnp.float32))
            z_ring[slot, :, pl.ds(i * cap, cap), pl.ds(col, n_cols)] = z_rows.astype(jnp.bfloat16).reshape(group, cap, n_cols)

    def place_at(g, q):
        off_y = pick([PLACES[PAIR * k + q // PAIR][0] for k in range(n_groups)], g)
        off_x = pick([PLACES[PAIR * k + q // PAIR][1] for k in range(n_groups)], g)
        return off_y, off_x

    my_line = line((cp_pos, tp_pos))

    def await_slot(slot):
        for q in range(group):
            await_bytes(z_ring.at[slot, q], sz_sem.at[slot, q])

    def expert_group(g, carry):
        slot = g % 3

        @pl.when(g == 2)
        def _():
            run_relays(3)

        sources = [line(at(*place_at(g, q), q % PAIR)) for q in range(group)]
        loads = []
        for q in range(group):
            for part in BOTH:
                await_bytes(rx_hbm.at[part, sources[q]], rx_sem.at[part, sources[q]])
                loads.append(pltpu.make_async_copy(rx_hbm.at[part, sources[q]], x_buf.at[q, :, pl.ds(part * half_hid, half_hid)], x_sem.at[part, q]))
                loads[-1].start()

        @pl.when(g >= 3)
        def _():
            await_slot(slot)
        for one in loads:
            one.wait()
        for i in BOTH:
            expert_rows(slot, i)
        for q in range(group):
            off_y, off_x = place_at(g, q)
            far = jnp.logical_or(off_y == 2, off_x == 2)
            alone = jnp.logical_and(g == 0, q == 0)

            @pl.when(alone)
            def _():
                pltpu.make_async_copy(z_ring.at[slot, q], rz_hbm.at[my_line], sz_sem.at[slot, q]).start()

            @pl.when(jnp.logical_not(jnp.logical_or(far, alone)))
            def _():
                send(z_ring.at[slot, q], rz_hbm.at[my_line], sz_sem.at[slot, q], rz_sem.at[my_line], at(off_y, off_x, q % PAIR)).start()

            @pl.when(far)
            def _():
                index = PAIR * g + q // PAIR - FIRST_FAR
                lead_y, lead_x = jnp.where(off_y == 2, 1, 0), jnp.where(off_x == 2, 1, 0)
                for way in BOTH:
                    sign = 1 - PAIR * way
                    send(z_ring.at[slot, q, pl.ds(way * cap, cap)], zl_hbm.at[index, q % PAIR, way], sz_sem.at[slot, q],
                         zl_sem.at[index, q % PAIR, way], at(sign * lead_y, sign * lead_x, 0)).start()
        return carry

    lax.fori_loop(0, n_groups, expert_group, 0)

    def z_relay(index, flip, way):
        off_y, off_x = PLACES[FIRST_FAR + index]
        sign = 1 - PAIR * way
        lead_y, lead_x = sign * (off_y == 2), sign * (off_x == 2)
        from_line = line(at(-lead_y, -lead_x, 0))
        to_y = sign if off_y == 2 else off_y
        to_x = sign if off_x == 2 else off_x
        return send(zl_hbm.at[index, flip, way], rz_hbm.at[from_line, pl.ds(way * cap, cap)], fz_sem.at[index, flip, way],
                    rz_sem.at[from_line], at(to_y, to_x, flip))

    def run_z_relays(first, count):
        for index in range(first, first + count):
            for flip in BOTH:
                for way in BOTH:
                    await_bytes(zl_hbm.at[index, flip, way], zl_sem.at[index, flip, way])
                    z_relay(index, flip, way).start()

    def combine(p, carry):
        off_y, off_x = pick([a for a, _ in PLACES], p), pick([b for _, b in PLACES], p)
        homes = [line(at(-off_y, -off_x, q)) for q in BOTH]
        loads = []
        for q in BOTH:
            @pl.when(jnp.logical_or(p > 0, q > 0))
            def _():
                await_bytes(rz_hbm.at[homes[q]], rz_sem.at[homes[q]])
            loads.append(pltpu.make_async_copy(rz_hbm.at[homes[q]], z_buf.at[q], z_sem.at[q]))
            loads[-1].start()
        weights = [[], [], []]
        for q in BOTH:
            for i in BOTH:
                row = pl.ds(PAIR * homes[q] + i, 1)
                chosen = rank_buf[0, 0, row, :] == slots
                for part in range(3):
                    weights[part].append(jnp.where(chosen, parts[part, row, :], 0.0))
        weights = [jnp.concatenate(w, axis=0).astype(jnp.bfloat16) for w in weights]
        for one in loads:
            one.wait()
        for col in range(0, hid, n_cols):
            z_rows = z_buf[:, :, pl.ds(col, n_cols)].reshape(4 * cap, n_cols)
            total = None
            for part in range(3):
                term = lax.dot_general(weights[part], z_rows, ROWS_ROWS, preferred_element_type=jnp.float32)
                total = term if total is None else total + term
            acc[:, pl.ds(col, n_cols)] += total
        return carry

    run_z_relays(0, 4)
    lax.fori_loop(0, FIRST_FAR, combine, 0)
    run_z_relays(4, N_FAR - 4)

    def combine_late(j, carry):
        first_late = FIRST_FAR + N_FAR
        n_late = len(PLACES) - first_late
        return combine(jnp.where(j < n_late, first_late + j, FIRST_FAR + j - n_late), carry)

    lax.fori_loop(0, len(PLACES) - FIRST_FAR, combine_late, 0)
    y_ref[...] = acc[...].astype(jnp.bfloat16)

    for part in BOTH:
        for i in range(6):
            spread(part, i).wait_send()
        for stage in (2, 3):
            await_ring(part, stage)
        for stage in range(4):
            for way in BOTH:
                for flip in BOTH:
                    relay(part, stage, way, flip).wait_send()
    for slot in range(3):
        await_slot(slot)
    for index in range(N_FAR):
        for flip in BOTH:
            for way in BOTH:
                z_relay(index, flip, way).wait_send()


def moe_call(n_cp, n_tp, cap, h_loc, rank_rows, near_rows, gate_rows, w_gate, w_up, w_down, wg_other, wu_other, wd_other):
    n_dev = n_cp * n_tp
    _, tok_dev, half_hid = h_loc.shape
    hid = PAIR * half_hid
    half_f = w_gate.shape[2]
    n_experts = rank_rows.shape[0]
    group = 4
    bf16 = jnp.bfloat16
    any_spec = pl.BlockSpec(memory_space=pl.ANY)
    vmem_spec = pl.BlockSpec(memory_space=pltpu.VMEM)
    dma = pltpu.SemaphoreType.DMA
    flops = PAIR * n_dev * PAIR * cap * hid * PAIR * half_f * 3
    return pl.pallas_call(
        functools.partial(moe_kernel, n_cp, n_tp, group),
        name="routed_experts",
        out_shape=(jax.ShapeDtypeStruct((tok_dev, hid), bf16), jax.ShapeDtypeStruct((2, n_dev, PAIR * cap, half_hid), bf16),
                   jax.ShapeDtypeStruct((2, 2, 4, 2, cap, half_hid), bf16), jax.ShapeDtypeStruct((n_dev, PAIR * cap, hid), bf16),
                   jax.ShapeDtypeStruct((N_FAR, 2, 2, cap, hid), bf16)),
        in_specs=[any_spec, any_spec, any_spec, vmem_spec] + [any_spec] * 6,
        out_specs=(vmem_spec,) + (any_spec,) * 4,
        scratch_shapes=[
            pltpu.VMEM((2, 4, tok_dev, half_hid), bf16),
            pltpu.VMEM((2, 4, n_experts, tok_dev), jnp.float32),
            pltpu.VMEM((2, 2, hid, half_f), bf16),
            pltpu.VMEM((2, 2, hid, half_f), bf16),
            pltpu.VMEM((2, 2, half_f, hid), bf16),
            pltpu.VMEM((2, 2, 8, PAIR * cap, half_hid), bf16),
            pltpu.VMEM((2, 4, PAIR * cap, half_hid), bf16),
            pltpu.VMEM((3, group, PAIR * cap, hid), bf16),
            pltpu.VMEM((group, PAIR * cap, hid), bf16),
            pltpu.VMEM((2, PAIR * cap, hid), bf16),
            pltpu.VMEM((tok_dev, hid), jnp.float32),
            pltpu.VMEM((3, n_experts, tok_dev), jnp.float32),
            dma((6,)), dma((4,)), dma((2,)), dma((2, group)), dma((2,)),
            dma((2, 6)), dma((2, 4, 2)), dma((2, 2, 8)), dma((2, n_dev)), dma((2, 2, 4, 2)), dma((2, 2, 4, 2)),
            dma((3, group)), dma((n_dev,)), dma((N_FAR, 2, 2)), dma((N_FAR, 2, 2)),
        ],
        compiler_params=pltpu.CompilerParams(collective_id=2, has_side_effects=True, vmem_limit_bytes=VMEM_LIMIT),
        cost_estimate=pl.CostEstimate(flops=flops, bytes_accessed=2**27, transcendentals=0),
    )(h_loc, rank_rows, near_rows, gate_rows, w_gate, w_up, w_down, wg_other, wu_other, wd_other)[0]


def routing_rows(ids_loc, gates_loc, n_experts):
    tok_dev = ids_loc.shape[0]
    chosen = ids_loc.T[None, :, :] == jnp.arange(n_experts, dtype=ids_loc.dtype)[:, None, None]
    mask = jnp.any(chosen, axis=1)
    gate_rows = jnp.sum(jnp.where(chosen, gates_loc.T[None, :, :], 0.0), axis=1)
    before = jnp.triu(jnp.ones((tok_dev, tok_dev), jnp.bfloat16), 1)
    rank = jnp.dot(mask.astype(jnp.bfloat16), before, preferred_element_type=jnp.float32)
    return jnp.where(mask, rank, -1.0), gate_rows


def block_of(cp_pos, tp_pos, n_cp, n_tp):
    per_chunk = n_tp // PAIR
    late = tp_pos // per_chunk
    chunk = late * (PAIR * n_cp - 1 - cp_pos) + (1 - late) * cp_pos
    return chunk * per_chunk + tp_pos % per_chunk


def owner_of(block, n_cp, n_tp):
    per_chunk = n_tp // PAIR
    chunk = block // per_chunk
    late = chunk // n_cp
    return late * (PAIR * n_cp - 1 - chunk) + (1 - late) * chunk, late * per_chunk + block % per_chunk


def front_kernel(n_cp, n_tp, x_hbm, w_ref, k_hbm, vt_hbm, q_hbm, x_buf, q_st, k_st, vt_st,
                 own_sem, ring_sem, pair_sem, rx_sem, sk_sem, sv_sem, sq_sem, kv_sem, rq_sem, sf_sem, rf_sem):
    n_x = n_tp // PAIR
    tok_dev, hid = x_hbm.shape
    half = tok_dev // PAIR
    head_dim = k_hbm.shape[1]
    n_loc = q_st.shape[1]
    chunk_len = tok_dev * n_x
    cp_pos, tp_pos = lax.axis_index("cp"), lax.axis_index("tp")
    x_pos, core = tp_pos // PAIR, tp_pos % PAIR
    sibling = PAIR * x_pos + 1 - core
    barrier = pltpu.get_barrier_semaphore()

    def slot_at(off, flip):
        return PAIR * ((x_pos + off + n_x) % n_x) + (core + flip) % PAIR

    own_copy = pltpu.make_async_copy(x_hbm, x_buf.at[tp_pos], own_sem)
    own_copy.start()
    for step in (1, n_x - 1):
        pl.semaphore_signal(barrier, inc=1, device_id=mesh_id(cp_pos, slot_at(step, 0)), device_id_type=MESH)
    for step in range(1, PAIR * n_cp):
        pl.semaphore_signal(barrier, inc=1, device_id=mesh_id((cp_pos + step // PAIR) % n_cp, PAIR * x_pos + (core + step) % PAIR), device_id_type=MESH)
    pl.semaphore_wait(barrier, PAIR * n_cp + 1)

    def own_send(part, to_tp, sem):
        rows = pl.ds(part * half, half)
        return pltpu.make_async_remote_copy(x_hbm.at[rows], x_buf.at[tp_pos, rows], sem, rx_sem.at[tp_pos, part],
                                            device_id=mesh_id(cp_pos, to_tp), device_id_type=MESH)

    def pass_on(slot, part, to_tp, sem):
        rows = pl.ds(pl.multiple_of(part * half, half), half)
        return pltpu.make_async_remote_copy(x_buf.at[slot, rows], x_buf.at[slot, rows], sem, rx_sem.at[slot, part],
                                            device_id=mesh_id(cp_pos, to_tp), device_id_type=MESH)

    for i, (part, off) in enumerate(((0, 1), (1, -1), (1, 1), (0, -1))):
        own_send(part, slot_at(off, 0), ring_sem.at[i]).start()
    for part in BOTH:
        own_send(part, sibling, pair_sem.at[part]).start()

    def place_of(step):
        wave, other, side = step // 4, (step // PAIR) % PAIR, step % PAIR
        near = ((wave + 1) // PAIR) % PAIR
        swap = (wave // PAIR) * (1 - wave // 3)
        off = near * (PAIR * side - 1) + PAIR * (wave // 3)
        return slot_at(off, other), side + swap * (1 - PAIR * side), off

    def outputs_of(step):
        slot, part, _ = place_of(step)
        block = block_of(cp_pos, slot, n_cp, n_tp)
        pos = block * tok_dev + part * half
        q_core = ((block % 4 + 1) // PAIR) % PAIR
        q_pos = (PAIR * (block // 4) + (block % 4) // PAIR) * tok_dev + part * half
        pos, q_pos = pl.multiple_of(pos, half), pl.multiple_of(q_pos, half)
        for i in range(n_loc):
            to_cp = n_loc * core + i
            for src, dst, s_sem, r_sem, to_core in (
                (k_st.at[step, i], k_hbm.at[pl.ds(pos, half)], sk_sem.at[i], kv_sem.at[cp_pos], 0),
                (vt_st.at[step, i], vt_hbm.at[:, pl.ds(pos, half)], sv_sem.at[i], kv_sem.at[cp_pos], 1),
                (q_st.at[step, i], q_hbm.at[pl.ds(q_pos, half)], sq_sem.at[i, q_core], rq_sem.at[cp_pos], q_core),
            ):
                here = jnp.logical_and(to_cp == cp_pos, to_core == core)

                @pl.when(here)
                def _():
                    pltpu.make_async_copy(src, dst, r_sem).start()

                @pl.when(jnp.logical_not(here))
                def _():
                    pltpu.make_async_remote_copy(src, dst, s_sem, r_sem, device_id=mesh_id(to_cp, PAIR * x_pos + to_core),
                                                 device_id_type=MESH).start()

    def project(step, carry):
        slot, part, off = place_of(step)
        wave, other, side = step // 4, (step // PAIR) % PAIR, step % PAIR

        @pl.when(step == 0)
        def _():
            own_copy.wait()

        @pl.when(step > 1)
        def _():
            pass_on(slot, part, sibling, pair_sem.at[0]).wait_recv()

        @pl.when(jnp.logical_and(wave > 0, other == 0))
        def _():
            @pl.when(wave == 1)
            def _():
                pass_on(slot, part, slot_at(-off, 0), ring_sem.at[4 + side]).start()
            pass_on(slot, part, sibling, pair_sem.at[PAIR * wave + side]).start()

        x_rows = x_buf[slot, pl.ds(pl.multiple_of(part * half, half), half), :]
        qkv = jnp.dot(x_rows, w_ref[...], preferred_element_type=jnp.float32)
        for i in range(n_loc):
            q_st[step, i] = qkv[:, i * head_dim:(i + 1) * head_dim].astype(jnp.bfloat16)
            k_st[step, i] = qkv[:, (n_loc + i) * head_dim:(n_loc + i + 1) * head_dim].astype(jnp.bfloat16)
            vt_st[step, i] = qkv[:, (PAIR * n_loc + i) * head_dim:(PAIR * n_loc + i + 1) * head_dim].T.astype(jnp.bfloat16)

        @pl.when(step > 0)
        def _():
            outputs_of(step - 1)
        return carry

    n_steps = PAIR * n_tp
    lax.fori_loop(0, n_steps, project, 0)
    outputs_of(n_steps - 1)

    def whole(ref, count, sem):
        return pltpu.make_async_copy(ref.at[pl.ds(0, count)], ref.at[pl.ds(0, count)], sem)

    def forward(y, place, core_id):
        chunk = y if place == 0 else PAIR * n_cp - 1 - y
        cols = pl.ds(chunk * chunk_len, chunk_len)
        ref = k_hbm.at[cols] if core_id == 0 else vt_hbm.at[:, cols]
        return pltpu.make_async_remote_copy(ref, ref, sf_sem.at[PAIR * y + place], rf_sem.at[PAIR * y + place],
                                            device_id=mesh_id(cp_pos, sibling), device_id_type=MESH)

    for y in range(n_cp):
        whole(k_hbm, PAIR * chunk_len, kv_sem.at[y]).wait()
        for core_id in BOTH:
            @pl.when(core == core_id)
            def _():
                for place in BOTH:
                    forward(y, place, core_id).start()
    for y in range(n_cp):
        whole(q_hbm, chunk_len, rq_sem.at[y]).wait()
    for i in range(4):
        own_send(0, sibling, ring_sem.at[i]).wait_send()
    for i in BOTH:
        own_send(0, sibling, ring_sem.at[4 + i]).wait_send()
    for i in range(8):
        own_send(0, sibling, pair_sem.at[i]).wait_send()
    for i in range(n_loc):
        to_cp = n_loc * core + i
        for sem, to_core, count in ((sk_sem.at[i], 0, PAIR * chunk_len), (sv_sem.at[i], 1, PAIR * chunk_len),
                                    (sq_sem.at[i, 0], 0, chunk_len), (sq_sem.at[i, 1], 1, chunk_len)):
            @pl.when(jnp.logical_not(jnp.logical_and(to_cp == cp_pos, to_core == core)))
            def _():
                whole(k_hbm, count, sem).wait()
    for core_id in BOTH:
        @pl.when(core == core_id)
        def _():
            for y in range(n_cp):
                for place in BOTH:
                    forward(y, place, core_id).wait_send()
                    forward(y, place, 1 - core_id).wait_recv()


def front_call(n_cp, n_tp, x_loc, w_qkv, head_dim, n_loc):
    tok_dev, hid = x_loc.shape
    half = tok_dev // PAIR
    seq = tok_dev * n_cp * n_tp
    any_spec = pl.BlockSpec(memory_space=pl.ANY)
    n_steps = PAIR * n_tp
    return pl.pallas_call(
        functools.partial(front_kernel, n_cp, n_tp),
        name="gather_project",
        out_shape=(jax.ShapeDtypeStruct((seq, head_dim), jnp.bfloat16), jax.ShapeDtypeStruct((head_dim, seq), jnp.bfloat16),
                   jax.ShapeDtypeStruct((seq // PAIR, head_dim), jnp.bfloat16)),
        in_specs=[any_spec, pl.BlockSpec(memory_space=pltpu.VMEM)],
        out_specs=(any_spec, any_spec, any_spec),
        scratch_shapes=[
            pltpu.VMEM((n_tp, tok_dev, hid), jnp.bfloat16),
            pltpu.VMEM((n_steps, n_loc, half, head_dim), jnp.bfloat16),
            pltpu.VMEM((n_steps, n_loc, half, head_dim), jnp.bfloat16),
            pltpu.VMEM((n_steps, n_loc, head_dim, half), jnp.bfloat16),
            pltpu.SemaphoreType.DMA,
            pltpu.SemaphoreType.DMA((6,)),
            pltpu.SemaphoreType.DMA((8,)),
            pltpu.SemaphoreType.DMA((n_tp, 2)),
            pltpu.SemaphoreType.DMA((n_loc,)),
            pltpu.SemaphoreType.DMA((n_loc,)),
            pltpu.SemaphoreType.DMA((n_loc, 2)),
            pltpu.SemaphoreType.DMA((n_cp,)),
            pltpu.SemaphoreType.DMA((n_cp,)),
            pltpu.SemaphoreType.DMA((PAIR * n_cp,)),
            pltpu.SemaphoreType.DMA((PAIR * n_cp,)),
        ],
        compiler_params=pltpu.CompilerParams(collective_id=0, has_side_effects=True, vmem_limit_bytes=VMEM_LIMIT),
        cost_estimate=pl.CostEstimate(flops=PAIR * n_tp * tok_dev * hid * w_qkv.shape[1], bytes_accessed=2**26, transcendentals=0),
    )(x_loc, w_qkv)


def attend_kernel(n_cp, n_tp, k_hbm, vt_hbm, q_hbm, x_hbm, wo_hbm, wg_hbm, wu_hbm, wd_hbm, rank_hbm,
                  h_ref, o_hbm, wgx_hbm, wux_hbm, wdx_hbm, near_hbm,
                  k_buf, vt_buf, q_buf, qt_buf, o_st, o_buf, wo_buf, x_buf, s_even, s_odd, acc, m_ref, l_ref,
                  in_sem, so_sem, ro_sem, swo_sem, rwo_sem, sw_sem, rw_sem, sr_sem, rr_sem, o_sem):
    n_dev = n_cp * n_tp
    n_x = n_tp // PAIR
    tok_dev, hid = x_buf.shape
    head_dim = k_buf.shape[1]
    n_heads = o_buf.shape[0]
    cp_pos, tp_pos = lax.axis_index("cp"), lax.axis_index("tp")
    x_pos, core = tp_pos // PAIR, tp_pos % PAIR
    head = n_cp * x_pos + cp_pos
    scale = (head_dim ** -0.5) * 1.4426950408889634
    loads = [pltpu.make_async_copy(src, dst, in_sem.at[i]) for i, (src, dst) in enumerate(
        ((q_hbm, q_buf), (k_hbm, k_buf), (vt_hbm, vt_buf), (x_hbm, x_buf), (wo_hbm, wo_buf.at[tp_pos])))]
    for one in loads:
        one.start()

    enter_all(n_cp, n_tp)

    def wo_send(step):
        return pltpu.make_async_remote_copy(wo_hbm, wo_buf.at[tp_pos], swo_sem.at[step], rwo_sem.at[step],
                                            device_id=mesh_id(cp_pos, (tp_pos + step) % n_tp), device_id_type=MESH)

    def wo_arrival(step):
        return pltpu.make_async_remote_copy(wo_hbm, wo_buf.at[(tp_pos + n_tp - step) % n_tp], swo_sem.at[step], rwo_sem.at[step],
                                            device_id=mesh_id(cp_pos, tp_pos), device_id_type=MESH)

    keep = wgx_hbm.shape[0]
    swaps = [pltpu.make_async_remote_copy(src.at[pl.ds((1 - core) * keep, keep)], dst, sw_sem.at[i], rw_sem.at[i],
                                          device_id=mesh_id(cp_pos, PAIR * x_pos + 1 - core), device_id_type=MESH)
             for i, (src, dst) in enumerate(((wg_hbm, wgx_hbm), (wu_hbm, wux_hbm), (wd_hbm, wdx_hbm)))]
    ranks = []
    for slot, off in ((1, 1), (2, -1), (3, 2)):
        for part, place in enumerate((((cp_pos + off + n_cp) % n_cp, tp_pos), (cp_pos, PAIR * ((x_pos + off + n_x) % n_x) + core))):
            ranks.append(pltpu.make_async_remote_copy(rank_hbm, near_hbm.at[part, slot], sr_sem.at[part, slot], rr_sem.at[part, slot],
                                                      device_id=mesh_id(*place), device_id_type=MESH))
    for step in range(1, n_tp):
        wo_send(step).start()
    for one in swaps + ranks:
        one.start()
    for one in loads[:3]:
        one.wait()

    def update(s_vals, s_top, v_cols, lo, width):
        cols = pl.ds(lo, width)
        m_old = m_ref[:, cols]
        m_new = jnp.maximum(m_old, s_top)
        prob = jnp.exp2((s_vals - m_new) * scale)
        shrink = jnp.exp2((m_old - m_new) * scale)
        m_ref[:, cols] = m_new
        l_ref[:, cols] = l_ref[:, cols] * shrink + jnp.sum(prob, axis=0, keepdims=True)
        acc[:, cols] = acc[:, cols] * shrink + jnp.dot(v_cols, prob.astype(jnp.bfloat16), preferred_element_type=jnp.float32)

    def keys_at(block):
        return k_buf[pl.ds(pl.multiple_of(block * tok_dev, tok_dev), tok_dev), :]

    def values_at(block):
        return vt_buf[:, pl.ds(pl.multiple_of(block * tok_dev, tok_dev), tok_dev)]

    def query_pair(g, carry):
        q_rows = q_buf[pl.ds(pl.multiple_of(g * PAIR * tok_dev, PAIR * tok_dev), PAIR * tok_dev), :]
        qt_buf[...] = q_rows.astype(jnp.float32).T.astype(jnp.bfloat16)
        m_ref[...] = jnp.full_like(m_ref, -1e30)
        l_ref[...] = jnp.zeros_like(l_ref)
        acc[...] = jnp.zeros_like(acc)
        for r in BOTH:
            lo = r * tok_dev
            inner = (1 - core) * 3 * r + core * (1 + r)

            def near_scores(block):
                return jnp.dot(keys_at(block), qt_buf[:, pl.ds(lo, tok_dev)], preferred_element_type=jnp.float32)

            s_vals = near_scores(4 * g + inner)
            key_id = lax.broadcasted_iota(jnp.int32, s_vals.shape, 0)
            query_id = lax.broadcasted_iota(jnp.int32, s_vals.shape, 1)
            s_vals = jnp.where(key_id <= query_id, s_vals, -1e30)
            update(s_vals, jnp.max(s_vals, axis=0, keepdims=True), values_at(4 * g + inner), lo, tok_dev)

            def near_block(j, inner_carry):
                s_near = near_scores(4 * g + j)
                update(s_near, jnp.max(s_near, axis=0, keepdims=True), values_at(4 * g + j), lo, tok_dev)
                return inner_carry

            lax.fori_loop(0, inner, near_block, 0)

        def far_scores(block, s_ref):
            s_vals = jnp.dot(keys_at(block), qt_buf[...], preferred_element_type=jnp.float32)
            s_ref[...] = s_vals
            return jnp.max(s_vals, axis=0, keepdims=True)

        def far_pair(n, top_even):
            top_odd = far_scores(PAIR * n + 1, s_odd)
            update(s_even[...], top_even, values_at(PAIR * n), 0, PAIR * tok_dev)
            top_next = far_scores(PAIR * n + 2, s_even)
            update(s_odd[...], top_odd, values_at(PAIR * n + 1), 0, PAIR * tok_dev)
            return top_next

        lax.fori_loop(0, PAIR * g, far_pair, far_scores(0, s_even))
        out = (acc[...] / l_ref[...]).T.astype(jnp.bfloat16)
        for r in BOTH:
            o_st[PAIR * g + r] = out[r * tok_dev:(r + 1) * tok_dev]
            o_push(PAIR * g + r, "start")
        return carry

    def o_push(index, what):
        block = 4 * (index // PAIR) + (1 - core) * 3 * (index % PAIR) + core * (1 + index % PAIR)
        to_cp, to_tp = owner_of(block, n_cp, n_tp)
        here = jnp.logical_and(to_cp == cp_pos, to_tp == tp_pos)
        if what == "start":
            @pl.when(here)
            def _():
                pltpu.make_async_copy(o_st.at[index], o_hbm.at[head], ro_sem.at[head]).start()

        @pl.when(jnp.logical_not(here))
        def _():
            copy = pltpu.make_async_remote_copy(o_st.at[index], o_hbm.at[head], so_sem.at[index], ro_sem.at[head],
                                                device_id=mesh_id(to_cp, to_tp), device_id_type=MESH)
            if what == "start":
                copy.start()
            else:
                copy.wait_send()

    lax.fori_loop(0, n_dev // 4, query_pair, 0)

    for step in range(1, n_tp):
        wo_arrival(step).wait_recv()
    for one in loads[3:]:
        one.wait()
    for j in range(n_heads):
        pltpu.make_async_copy(o_hbm.at[j], o_hbm.at[j], ro_sem.at[j]).wait()
    o_load = pltpu.make_async_copy(o_hbm, o_buf, o_sem)
    o_load.start()
    o_load.wait()
    o_rows = jnp.concatenate([o_buf[j] for j in range(n_heads)], axis=1)
    n_cols = min(512, hid // PAIR)

    for col in range(0, hid, n_cols):
        cols = pl.ds(col, n_cols)
        w_cols = wo_buf[:, :, cols].reshape(n_heads * head_dim, n_cols)
        h_cols = (x_buf[:, cols].astype(jnp.float32) + jnp.dot(o_rows, w_cols, preferred_element_type=jnp.float32)).astype(jnp.bfloat16)
        h_ref[PAIR * col // hid, :, pl.ds(col % (hid // PAIR), n_cols)] = h_cols

    for step in range(1, n_tp):
        wo_send(step).wait_send()
    for one in swaps + ranks:
        one.wait()

    def drain(index, carry):
        o_push(index, "wait")
        return carry

    lax.fori_loop(0, n_dev // PAIR, drain, 0)


def attend_call(n_cp, n_tp, k_all, vt_all, q_all, x_loc, wo_loc, w_gate, w_up, w_down, rank_rows):
    n_dev = n_cp * n_tp
    tok_dev, hid = x_loc.shape
    seq, head_dim = k_all.shape
    n_heads = n_tp * wo_loc.shape[0] // head_dim
    keep = w_gate.shape[0] // PAIR
    any_spec = pl.BlockSpec(memory_space=pl.ANY)
    bf16 = jnp.bfloat16
    h_loc, _, wg_other, wu_other, wd_other, near_rows = pl.pallas_call(
        functools.partial(attend_kernel, n_cp, n_tp),
        name="attend_heads",
        out_shape=(jax.ShapeDtypeStruct((2, tok_dev, hid // PAIR), bf16), jax.ShapeDtypeStruct((n_heads, tok_dev, head_dim), bf16))
        + tuple(jax.ShapeDtypeStruct((keep,) + w.shape[1:], bf16) for w in (w_gate, w_up, w_down))
        + (jax.ShapeDtypeStruct((2, 4) + rank_rows.shape, jnp.float32),),
        in_specs=[any_spec] * 9,
        out_specs=(pl.BlockSpec(memory_space=pltpu.VMEM),) + (any_spec,) * 5,
        scratch_shapes=[
            pltpu.VMEM((seq, head_dim), bf16),
            pltpu.VMEM((head_dim, seq), bf16),
            pltpu.VMEM((seq // PAIR, head_dim), bf16),
            pltpu.VMEM((head_dim, PAIR * tok_dev), bf16),
            pltpu.VMEM((n_dev // PAIR, tok_dev, head_dim), bf16),
            pltpu.VMEM((n_heads, tok_dev, head_dim), bf16),
            pltpu.VMEM((n_tp,) + wo_loc.shape, bf16),
            pltpu.VMEM((tok_dev, hid), bf16),
            pltpu.VMEM((tok_dev, PAIR * tok_dev), jnp.float32),
            pltpu.VMEM((tok_dev, PAIR * tok_dev), jnp.float32),
            pltpu.VMEM((head_dim, PAIR * tok_dev), jnp.float32),
            pltpu.VMEM((1, PAIR * tok_dev), jnp.float32),
            pltpu.VMEM((1, PAIR * tok_dev), jnp.float32),
            pltpu.SemaphoreType.DMA((5,)),
            pltpu.SemaphoreType.DMA((n_dev // PAIR,)),
            pltpu.SemaphoreType.DMA((n_heads,)),
            pltpu.SemaphoreType.DMA((n_tp,)),
            pltpu.SemaphoreType.DMA((n_tp,)),
            pltpu.SemaphoreType.DMA((3,)),
            pltpu.SemaphoreType.DMA((3,)),
            pltpu.SemaphoreType.DMA((2, 4)),
            pltpu.SemaphoreType.DMA((2, 4)),
            pltpu.SemaphoreType.DMA,
        ],
        compiler_params=pltpu.CompilerParams(collective_id=1, has_side_effects=True, vmem_limit_bytes=VMEM_LIMIT),
        cost_estimate=pl.CostEstimate(flops=PAIR * seq * seq * head_dim // PAIR, bytes_accessed=2**26, transcendentals=seq * seq // 4),
    )(k_all, vt_all, q_all, x_loc, wo_loc, w_gate, w_up, w_down, rank_rows)
    return h_loc, near_rows, wg_other, wu_other, wd_other


def solution(mesh):
    n_cp = mesh.shape["cp"]
    n_tp = mesh.shape["tp"]
    row_spec = P(("dp", "cp", "tp"), None)
    head_spec = P(None, "tp", None)
    expert_spec = P(("cp", "tp"), None, None)

    def device_step(x_loc, w_q, w_k, w_v, w_o, ids_loc, gates_loc, w_gate, w_up, w_down):
        tok_dev, hid_dim = x_loc.shape
        n_loc, head_dim = w_q.shape[1:]
        n_experts = w_gate.shape[0] * n_cp * n_tp // PAIR
        capacity = ids_loc.shape[1] * tok_dev // n_experts
        w_qkv = jnp.concatenate([w.reshape(hid_dim, n_loc * head_dim) for w in (w_q, w_k, w_v)], axis=1)
        rank_rows, gate_rows = routing_rows(ids_loc, gates_loc, n_experts)
        k_all, vt_all, q_all = front_call(n_cp, n_tp, x_loc, w_qkv, head_dim, n_loc)
        h_loc, near_rows, *others = attend_call(n_cp, n_tp, k_all, vt_all, q_all, x_loc, w_o.reshape(n_loc * head_dim, hid_dim), w_gate, w_up, w_down, rank_rows)
        return moe_call(n_cp, n_tp, capacity, h_loc, rank_rows, near_rows, gate_rows, w_gate, w_up, w_down, *others)

    return jax.shard_map(device_step, mesh=mesh, in_specs=(row_spec, head_spec, head_spec, head_spec, P("tp", None, None), row_spec, row_spec, expert_spec, expert_spec, expert_spec), out_specs=row_spec, check_vma=False)
```

time: 871 us -> 644 us (0.74)
  the two profiles are of different devices: /device:TPU:103 before, /device:TPU:99 now
where the time goes in v3:
time: 644 us; the launch traced here: 642 us
  Pallas kernels  631 us (98%)
    pallas_call x1, Pallas kernels, moe_call(): pl.pallas_call(functools.partial(moe_kernel, n_cp, n_tp, group), name='ro...  392 us
    pallas_call x1, Pallas kernels, attend_call(): pl.pallas_call(functools.partial(attend_kernel, n_cp, n_tp), name='attend...  134 us
    pallas_call x1, Pallas kernels, front_call(): pl.pallas_call(functools.partial(front_kernel, n_cp, n_tp), name='gather_...  104 us

profile of v3, /device:TPU:99, one launch (start us, length us, event | category | flops | bytes accessed | tf_op | source)
XLA Modules:
  0.0 642.5 jit_solution(1054732365254619899)
XLA Ops:
  0.0 1.1 fusion
  1.1 0.9 convolution_select_fusion.rank_hbm
  1.9 1.7 select_reduce_fusion.gate_ref
  3.7 1.4 copy.17
  5.0 1.9 copy_bitcast_fusion
  6.9 1.9 pad_maximum_fusion.w_ref
  8.8 104.3 %gather_project.1 = (bf16[16384,128]{1,0:T(8,128)(2,1)}, bf16[128,16384]{1,0:T(8,128)(2,1)}, bf16[8192,128]{1,0:T(8,128)(2,1)}) custom-call(bf16[512,2048]{1,0:T(8,128)(2,1)} %x_hbm.3, bf16[2048,768]{1,0:T(8,128)(2,1)} %pad_maximum_fusion.w_ref), custom_call_target="tpu_custom_call" | custom-call | flops 12884901888 | bytes 67108864 | tf_op jit(solution)/shard_map/gather_project/pallas_call | solution.py:572
  113.1 133.9 %attend_heads.1 = (bf16[2,512,1024]{2,1,0:T(8,128)(2,1)}, bf16[16,512,128]{2,1,0:T(8,128)(2,1)}, bf16[2,2048,512]{2,1,0:T(8,128)(2,1)}, bf16[2,2048,512]{2,1,0:T...) custom-call(bf16[16384,128]{1,0:T(8,128)(2,1)} %get-tuple-element.14.k_hbm, ...), custom_call_target="tpu_custom_call" | custom-call | flops 34359738368 | bytes 67108864 | tf_op jit(solution)/shard_map/attend_heads/pallas_call | solution.py:764
  247.0 392.3 %routed_experts.1 = (bf16[512,2048]{1,0:T(8,128)(2,1)}, bf16[2,32,128,1024]{3,2,1,0:T(8,128)(2,1)}, bf16[2,2,4,2,64,1024]{5,4,3,2,1,0:T(8,128)(2,1)}, bf16[32,12...) custom-call(bf16[2,512,1024]{2,1,0:T(8,128)(2,1)} %get-tuple-element.17.h_hbm, ...), custom_call_target="tpu_custom_call" | custom-call | flops 51539607552 | bytes 134217728 | tf_op jit(solution)/shard_map/routed_experts/pallas_call | solution.py:365
  639.3 3.2 copy.19

commit v4 on v3

--- a/solution.py
+++ b/solution.py
@@ -11,10 +11,15 @@
 PAIR = 2
 BOTH = range(PAIR)
 ROWS_ROWS = (((0,), (0,)), ((), ()))
+COLUMN_WISE = {"axis": 0, "keepdims": True}
+dma = pltpu.SemaphoreType.DMA
+and_, or_, not_ = jnp.logical_and, jnp.logical_or, jnp.logical_not
 VMEM_LIMIT = 66_000_000
-PLACES = ((0, 0), (0, 1), (1, 0), (0, -1), (-1, 0), (1, 1), (0, 2), (2, 0), (1, 2), (2, 1), (2, -1), (-1, 2), (2, 2), (1, -1), (-1, 1), (-1, -1))
-FIRST_FAR, N_FAR = 6, 7
-SOURCES = (0, -1, 1, 2)
+PLACES = ((0, 0), (0, 1), (1, 0), (0, -1), (-1, 0), (1, 1), (-1, -1), (1, -1), (-1, 1), (0, PAIR), (PAIR, 0), (1, PAIR), (PAIR, 1), (-1, PAIR), (PAIR, -1), (PAIR, PAIR))
+N_NEAR, FIRST_FAR = 5, 9
+GROUPS = ("1234", "1234", "9a9a", "bcbc", "dede", "0f0f", "5656", "7878")
+FLIPS = ("0000", "1111") + ("0011",) * 6
+SOURCES = (0, -1, 1, PAIR)
 
 
 def peer_of(step, cp_pos, tp_pos, n_cp, n_tp):
@@ -78,7 +83,7 @@
         rank_loads.append(pltpu.make_async_copy(near_hbm.at[part, pl.ds(1, 3)], rank_buf.at[part, pl.ds(1, 3)], rank_sem.at[PAIR * part + 1]))
     w_loads = []
     for slot, (own, other, buf) in enumerate(((wg_hbm, wgx_hbm, wg_buf), (wu_hbm, wux_hbm, wu_buf), (wd_hbm, wdx_hbm, wd_buf))):
-        w_loads.append(pltpu.make_async_copy(own.at[pl.ds(PAIR * core, 2)], buf.at[0], w_sem.at[PAIR * slot]))
+        w_loads.append(pltpu.make_async_copy(own.at[pl.ds(PAIR * core, PAIR)], buf.at[0], w_sem.at[PAIR * slot]))
         w_loads.append(pltpu.make_async_copy(other, buf.at[1], w_sem.at[PAIR * slot + 1]))
     for one in h_loads + rank_loads:
         one.start()
@@ -94,7 +99,7 @@
         return pl.ds(piece * half_tok, half_tok)
 
     def spread(part, i):
-        piece, off, slot = ((0, 1, 1), (1, -1, 2), (1, 1, 1), (0, -1, 2), (0, 1, 3), (1, -1, 3))[i]
+        piece, off, slot = ((0, 1, 1), (1, -1, PAIR), (1, 1, 1), (0, -1, PAIR), (0, 1, 3), (1, -1, 3))[i]
         rows = rows_of(piece)
         src = h_hbm.at[part, rows] if i < 4 else h_buf.at[part, 1 if i == 4 else 2, rows]
         return send(src, h_buf.at[part, slot, rows], hs_sem.at[part, i], hr_sem.at[part, slot, piece], along(part, off))
@@ -134,26 +139,31 @@
         src_line = source_line(part, stage, 0)
         return pltpu.make_async_copy(own_stage.at[part, stage], rx_hbm.at[part, src_line], rx_sem.at[part, src_line])
 
-    def run_stage(part, stage):
+    def run_stage(stage):
         side = stage % PAIR
-        if stage >= 2:
-            await_ring(part, stage)
-        own_stage[part, stage] = gather_rows(part, stage, 0)
-
-        def fill(m, carry):
-            ring[part, side, m] = gather_rows(part, stage, m)
-            return carry
-
-        lax.fori_loop(1, 8, fill, 0)
-        src_line = source_line(part, stage, 0)
-        own_copy(part, stage).start()
-        for m in (6, 7):
-            for way, off in ((0, 1), (1, -1)):
-                send(ring.at[part, side, m, pl.ds(way * cap, cap)], rl_hbm.at[part, way, stage, m % PAIR], ss_sem.at[part, side, m],
-                     rl_sem.at[part, way, stage, m % PAIR], across(part, off, 0)).start()
-        for m, off in ((2, 1), (4, -1), (3, 1), (5, -1), (1, 0)):
-            send(ring.at[part, side, m], rx_hbm.at[part, src_line], ss_sem.at[part, side, m], rx_sem.at[part, src_line],
-                 across(part, off, m % PAIR)).start()
+        for part in BOTH:
+            if stage >= 2:
+                await_ring(part, stage)
+            own_stage[part, stage] = gather_rows(part, stage, 0)
+
+            def fill(m, carry):
+                ring[part, side, m] = gather_rows(part, stage, m)
+                return carry
+
+            lax.fori_loop(1, 8, fill, 0)
+        lines = [source_line(part, stage, 0) for part in BOTH]
+        for flip in BOTH:
+            for way, off in enumerate((1, -1)):
+                for part in BOTH:
+                    m = 6 + flip
+                    send(ring.at[part, side, m, pl.ds(way * cap, cap)], rl_hbm.at[part, way, stage, flip], ss_sem.at[part, side, m],
+                         rl_sem.at[part, way, stage, flip], across(part, off, 0)).start()
+        for m, off in ((PAIR, 1), (4, -1), (3, 1), (5, -1), (1, 0)):
+            for part in BOTH:
+                send(ring.at[part, side, m], rx_hbm.at[part, lines[part]], ss_sem.at[part, side, m], rx_sem.at[part, lines[part]],
+                     across(part, off, m % PAIR)).start()
+        for part in BOTH:
+            own_copy(part, stage).start()
 
     def relay(part, stage, way, flip):
         off = 1 - PAIR * way
@@ -168,17 +178,16 @@
                     await_bytes(rl_hbm.at[part, way, stage, flip], rl_sem.at[part, way, stage, flip])
                     relay(part, stage, way, flip).start()
 
-    for part in BOTH:
-        run_stage(part, 0)
+    run_stage(0)
     for part in BOTH:
         await_h(part, 1, 0)
         spread(part, 4).start()
     for part in BOTH:
-        await_h(part, 2, 1)
+        await_h(part, PAIR, 1)
         spread(part, 5).start()
     for part in BOTH:
         await_h(part, 1, 1)
-        run_stage(part, 1)
+    run_stage(1)
     gate_all = gate_ref[...]
     high = gate_all.astype(jnp.bfloat16).astype(jnp.float32)
     rest = gate_all - high
@@ -190,20 +199,19 @@
         acc[:, part * half_hid:(part + 1) * half_hid] = h_buf[part, 0].astype(jnp.float32)
     run_relays(0)
     for part in BOTH:
-        await_h(part, 2, 0)
-        run_stage(part, 2)
+        await_h(part, PAIR, 0)
+    run_stage(2)
     run_relays(1)
     for part in BOTH:
         await_h(part, 3, 0)
         await_h(part, 3, 1)
-        run_stage(part, 3)
+    run_stage(3)
     run_relays(2)
     for one in w_loads:
         one.wait()
 
     rows = group * cap
     n_cols = min(512, hid)
-    n_groups = len(PLACES) // PAIR
 
     def expert_rows(slot, i):
         x_rows = x_buf[:, pl.ds(i * cap, cap), :].reshape(rows, hid)
@@ -218,9 +226,9 @@
             z_ring[slot, :, pl.ds(i * cap, cap), pl.ds(col, n_cols)] = z_rows.astype(jnp.bfloat16).reshape(group, cap, n_cols)
 
     def place_at(g, q):
-        off_y = pick([PLACES[PAIR * k + q // PAIR][0] for k in range(n_groups)], g)
-        off_x = pick([PLACES[PAIR * k + q // PAIR][1] for k in range(n_groups)], g)
-        return off_y, off_x
+        places = [int(names[q], 16) for names in GROUPS]
+        off_y, off_x = (pick([PLACES[p][k] for p in places], g) for k in BOTH)
+        return off_y, off_x, pick([int(flips[q]) for flips in FLIPS], g), pick(places, g)
 
     my_line = line((cp_pos, tp_pos))
 
@@ -235,7 +243,7 @@
         def _():
             run_relays(3)
 
-        sources = [line(at(*place_at(g, q), q % PAIR)) for q in range(group)]
+        sources = [line(at(*place_at(g, q)[:3])) for q in range(group)]
         loads = []
         for q in range(group):
             for part in BOTH:
@@ -251,29 +259,29 @@
         for i in BOTH:
             expert_rows(slot, i)
         for q in range(group):
-            off_y, off_x = place_at(g, q)
-            far = jnp.logical_or(off_y == 2, off_x == 2)
-            alone = jnp.logical_and(g == 0, q == 0)
+            off_y, off_x, flip, p = place_at(g, q)
+            alone = and_(p == 0, flip == 0)
 
             @pl.when(alone)
             def _():
-                pltpu.make_async_copy(z_ring.at[slot, q], rz_hbm.at[my_line], sz_sem.at[slot, q]).start()
-
-            @pl.when(jnp.logical_not(jnp.logical_or(far, alone)))
+                pltpu.make_async_copy(z_ring.at[slot, q], rz_hbm.at[my_line], rz_sem.at[my_line]).start()
+
+            @pl.when(and_(p < FIRST_FAR, not_(alone)))
             def _():
-                send(z_ring.at[slot, q], rz_hbm.at[my_line], sz_sem.at[slot, q], rz_sem.at[my_line], at(off_y, off_x, q % PAIR)).start()
-
-            @pl.when(far)
+                send(z_ring.at[slot, q], rz_hbm.at[my_line], sz_sem.at[slot, q], rz_sem.at[my_line], at(off_y, off_x, flip)).start()
+
+            @pl.when(p >= FIRST_FAR)
             def _():
-                index = PAIR * g + q // PAIR - FIRST_FAR
                 lead_y, lead_x = jnp.where(off_y == 2, 1, 0), jnp.where(off_x == 2, 1, 0)
                 for way in BOTH:
                     sign = 1 - PAIR * way
-                    send(z_ring.at[slot, q, pl.ds(way * cap, cap)], zl_hbm.at[index, q % PAIR, way], sz_sem.at[slot, q],
-                         zl_sem.at[index, q % PAIR, way], at(sign * lead_y, sign * lead_x, 0)).start()
+                    send(z_ring.at[slot, q, pl.ds(way * cap, cap)], zl_hbm.at[p - FIRST_FAR, flip, way], sz_sem.at[slot, q],
+                         zl_sem.at[p - FIRST_FAR, flip, way], at(sign * lead_y, sign * lead_x, 0)).start()
         return carry
 
-    lax.fori_loop(0, n_groups, expert_group, 0)
+    lax.fori_loop(0, len(GROUPS), expert_group, 0)
+
+    n_far = len(PLACES) - FIRST_FAR
 
     def z_relay(index, flip, way):
         off_y, off_x = PLACES[FIRST_FAR + index]
@@ -285,21 +293,20 @@
         return send(zl_hbm.at[index, flip, way], rz_hbm.at[from_line, pl.ds(way * cap, cap)], fz_sem.at[index, flip, way],
                     rz_sem.at[from_line], at(to_y, to_x, flip))
 
-    def run_z_relays(first, count):
-        for index in range(first, first + count):
-            for flip in BOTH:
-                for way in BOTH:
-                    await_bytes(zl_hbm.at[index, flip, way], zl_sem.at[index, flip, way])
-                    z_relay(index, flip, way).start()
+    def each_relay(*indices):
+        return [(index, flip, way) for flip in BOTH for way in BOTH for index in indices]
+
+    def run_z_relays(*indices):
+        for key in each_relay(*indices):
+            await_bytes(zl_hbm.at[key], zl_sem.at[key])
+            z_relay(*key).start()
 
     def combine(p, carry):
         off_y, off_x = pick([a for a, _ in PLACES], p), pick([b for _, b in PLACES], p)
         homes = [line(at(-off_y, -off_x, q)) for q in BOTH]
         loads = []
         for q in BOTH:
-            @pl.when(jnp.logical_or(p > 0, q > 0))
-            def _():
-                await_bytes(rz_hbm.at[homes[q]], rz_sem.at[homes[q]])
+            await_bytes(rz_hbm.at[homes[q]], rz_sem.at[homes[q]])
             loads.append(pltpu.make_async_copy(rz_hbm.at[homes[q]], z_buf.at[q], z_sem.at[q]))
             loads[-1].start()
         weights = [[], [], []]
@@ -321,33 +328,30 @@
             acc[:, pl.ds(col, n_cols)] += total
         return carry
 
-    run_z_relays(0, 4)
-    lax.fori_loop(0, FIRST_FAR, combine, 0)
-    run_z_relays(4, N_FAR - 4)
-
-    def combine_late(j, carry):
-        first_late = FIRST_FAR + N_FAR
-        n_late = len(PLACES) - first_late
-        return combine(jnp.where(j < n_late, first_late + j, FIRST_FAR + j - n_late), carry)
-
-    lax.fori_loop(0, len(PLACES) - FIRST_FAR, combine_late, 0)
+    run_z_relays(0, 1)
+    run_z_relays(PAIR, 3)
+    lax.fori_loop(0, N_NEAR, combine, 0)
+    run_z_relays(4, 5)
+    run_z_relays(6)
+    lax.fori_loop(N_NEAR, len(PLACES), combine, 0)
     y_ref[...] = acc[...].astype(jnp.bfloat16)
 
     for part in BOTH:
         for i in range(6):
             spread(part, i).wait_send()
-        for stage in (2, 3):
+        for stage in (PAIR, 3):
             await_ring(part, stage)
         for stage in range(4):
             for way in BOTH:
                 for flip in BOTH:
                     relay(part, stage, way, flip).wait_send()
-    for slot in range(3):
-        await_slot(slot)
-    for index in range(N_FAR):
-        for flip in BOTH:
-            for way in BOTH:
-                z_relay(index, flip, way).wait_send()
+    last = len(GROUPS) - 3
+    for g in range(last, len(GROUPS)):
+        for q in range(group):
+            if GROUPS[g][q] + FLIPS[g][q] != "00":
+                await_bytes(z_ring.at[g % 3, q], sz_sem.at[g % 3, q])
+    for key in each_relay(*range(n_far)):
+        z_relay(*key).wait_send()
 
 
 def moe_call(n_cp, n_tp, cap, h_loc, rank_rows, near_rows, gate_rows, w_gate, w_up, w_down, wg_other, wu_other, wd_other):
@@ -356,36 +360,36 @@
     hid = PAIR * half_hid
     half_f = w_gate.shape[2]
     n_experts = rank_rows.shape[0]
-    group = 4
+    group = len(GROUPS[0])
+    n_far = len(PLACES) - FIRST_FAR
     bf16 = jnp.bfloat16
     any_spec = pl.BlockSpec(memory_space=pl.ANY)
     vmem_spec = pl.BlockSpec(memory_space=pltpu.VMEM)
-    dma = pltpu.SemaphoreType.DMA
     flops = PAIR * n_dev * PAIR * cap * hid * PAIR * half_f * 3
     return pl.pallas_call(
         functools.partial(moe_kernel, n_cp, n_tp, group),
         name="routed_experts",
-        out_shape=(jax.ShapeDtypeStruct((tok_dev, hid), bf16), jax.ShapeDtypeStruct((2, n_dev, PAIR * cap, half_hid), bf16),
-                   jax.ShapeDtypeStruct((2, 2, 4, 2, cap, half_hid), bf16), jax.ShapeDtypeStruct((n_dev, PAIR * cap, hid), bf16),
-                   jax.ShapeDtypeStruct((N_FAR, 2, 2, cap, hid), bf16)),
+        out_shape=(jax.ShapeDtypeStruct((tok_dev, hid), bf16), jax.ShapeDtypeStruct((PAIR, n_dev, PAIR * cap, half_hid), bf16),
+                   jax.ShapeDtypeStruct((PAIR, PAIR, 4, PAIR, cap, half_hid), bf16), jax.ShapeDtypeStruct((n_dev, PAIR * cap, hid), bf16),
+                   jax.ShapeDtypeStruct((n_far, PAIR, 2, cap, hid), bf16)),
         in_specs=[any_spec, any_spec, any_spec, vmem_spec] + [any_spec] * 6,
         out_specs=(vmem_spec,) + (any_spec,) * 4,
         scratch_shapes=[
-            pltpu.VMEM((2, 4, tok_dev, half_hid), bf16),
-            pltpu.VMEM((2, 4, n_experts, tok_dev), jnp.float32),
-            pltpu.VMEM((2, 2, hid, half_f), bf16),
-            pltpu.VMEM((2, 2, hid, half_f), bf16),
-            pltpu.VMEM((2, 2, half_f, hid), bf16),
-            pltpu.VMEM((2, 2, 8, PAIR * cap, half_hid), bf16),
-            pltpu.VMEM((2, 4, PAIR * cap, half_hid), bf16),
+            pltpu.VMEM((PAIR, 4, tok_dev, half_hid), bf16),
+            pltpu.VMEM((PAIR, 4, n_experts, tok_dev), jnp.float32),
+            pltpu.VMEM((PAIR, PAIR, hid, half_f), bf16),
+            pltpu.VMEM((PAIR, PAIR, hid, half_f), bf16),
+            pltpu.VMEM((PAIR, PAIR, half_f, hid), bf16),
+            pltpu.VMEM((PAIR, PAIR, 8, PAIR * cap, half_hid), bf16),
+            pltpu.VMEM((PAIR, 4, PAIR * cap, half_hid), bf16),
             pltpu.VMEM((3, group, PAIR * cap, hid), bf16),
             pltpu.VMEM((group, PAIR * cap, hid), bf16),
-            pltpu.VMEM((2, PAIR * cap, hid), bf16),
+            pltpu.VMEM((PAIR, PAIR * cap, hid), bf16),
             pltpu.VMEM((tok_dev, hid), jnp.float32),
             pltpu.VMEM((3, n_experts, tok_dev), jnp.float32),
-            dma((6,)), dma((4,)), dma((2,)), dma((2, group)), dma((2,)),
-            dma((2, 6)), dma((2, 4, 2)), dma((2, 2, 8)), dma((2, n_dev)), dma((2, 2, 4, 2)), dma((2, 2, 4, 2)),
-            dma((3, group)), dma((n_dev,)), dma((N_FAR, 2, 2)), dma((N_FAR, 2, 2)),
+            dma((6,)), dma((4,)), dma((PAIR,)), dma((PAIR, group)), dma((PAIR,)),
+            dma((PAIR, 6)), dma((PAIR, 4, PAIR)), dma((PAIR, PAIR, 8)), dma((PAIR, n_dev)), dma((PAIR, PAIR, 4, PAIR)), dma((PAIR, PAIR, 4, PAIR)),
+            dma((3, group)), dma((n_dev,)), dma((n_far, PAIR, PAIR)), dma((n_far, PAIR, PAIR)),
         ],
         compiler_params=pltpu.CompilerParams(collective_id=2, has_side_effects=True, vmem_limit_bytes=VMEM_LIMIT),
         cost_estimate=pl.CostEstimate(flops=flops, bytes_accessed=2**27, transcendentals=0),
@@ -416,8 +420,8 @@
     return late * (PAIR * n_cp - 1 - chunk) + (1 - late) * chunk, late * per_chunk + block % per_chunk
 
 
-def front_kernel(n_cp, n_tp, x_hbm, w_ref, k_hbm, vt_hbm, q_hbm, x_buf, q_st, k_st, vt_st,
-                 own_sem, ring_sem, pair_sem, rx_sem, sk_sem, sv_sem, sq_sem, kv_sem, rq_sem, sf_sem, rf_sem):
+def front_kernel(n_cp, n_tp, x_hbm, wq_hbm, wk_hbm, wv_hbm, k_hbm, vt_hbm, q_hbm, x_buf, w_buf, q_st, k_st, vt_st, k_far, vt_far, q_far,
+                 own_sem, w_sem, ring_sem, pair_sem, rx_sem, sk_sem, sv_sem, sq_sem, kv_sem, rq_sem, sf_sem, rf_sem, far_sem, pass_sem):
     n_x = n_tp // PAIR
     tok_dev, hid = x_hbm.shape
     half = tok_dev // PAIR
@@ -434,6 +438,10 @@
 
     own_copy = pltpu.make_async_copy(x_hbm, x_buf.at[tp_pos], own_sem)
     own_copy.start()
+    width = n_loc * head_dim
+    w_loads = [pltpu.make_async_copy(w, w_buf.at[:, pl.ds(i * width, width)], w_sem.at[i]) for i, w in enumerate((wq_hbm, wk_hbm, wv_hbm))]
+    for one in w_loads:
+        one.start()
     for step in (1, n_x - 1):
         pl.semaphore_signal(barrier, inc=1, device_id=mesh_id(cp_pos, slot_at(step, 0)), device_id_type=MESH)
     for step in range(1, PAIR * n_cp):
@@ -462,30 +470,54 @@
         off = near * (PAIR * side - 1) + PAIR * (wave // 3)
         return slot_at(off, other), side + swap * (1 - PAIR * side), off
 
+    def targets(from_cp, slot, part):
+        block = block_of(from_cp, slot, n_cp, n_tp)
+        pos = pl.multiple_of(block * tok_dev + part * half, half)
+        q_core = ((block % 4 + 1) // PAIR) % PAIR
+        q_pos = pl.multiple_of((PAIR * (block // 4) + (block % 4) // PAIR) * tok_dev + part * half, half)
+        return ((k_hbm.at[pl.ds(pos, half)], 0, kv_sem.at[from_cp]), (vt_hbm.at[:, pl.ds(pos, half)], 1, kv_sem.at[from_cp]),
+                (q_hbm.at[pl.ds(q_pos, half)], q_core, rq_sem.at[from_cp]))
+
+    def remote(src, dst, s_sem, r_sem, to_cp, to_core):
+        return pltpu.make_async_remote_copy(src, dst, s_sem, r_sem, device_id=mesh_id((to_cp + n_cp) % n_cp, PAIR * x_pos + to_core), device_id_type=MESH)
+
+    far_refs = (k_far, vt_far, q_far)
+
     def outputs_of(step):
         slot, part, _ = place_of(step)
-        block = block_of(cp_pos, slot, n_cp, n_tp)
-        pos = block * tok_dev + part * half
-        q_core = ((block % 4 + 1) // PAIR) % PAIR
-        q_pos = (PAIR * (block // 4) + (block % 4) // PAIR) * tok_dev + part * half
-        pos, q_pos = pl.multiple_of(pos, half), pl.multiple_of(q_pos, half)
         for i in range(n_loc):
             to_cp = n_loc * core + i
-            for src, dst, s_sem, r_sem, to_core in (
-                (k_st.at[step, i], k_hbm.at[pl.ds(pos, half)], sk_sem.at[i], kv_sem.at[cp_pos], 0),
-                (vt_st.at[step, i], vt_hbm.at[:, pl.ds(pos, half)], sv_sem.at[i], kv_sem.at[cp_pos], 1),
-                (q_st.at[step, i], q_hbm.at[pl.ds(q_pos, half)], sq_sem.at[i, q_core], rq_sem.at[cp_pos], q_core),
-            ):
-                here = jnp.logical_and(to_cp == cp_pos, to_core == core)
+            far = (to_cp - cp_pos + n_cp) % n_cp == n_cp // PAIR
+            for kind, (src, (dst, to_core, r_sem)) in enumerate(zip((k_st.at[step, i], vt_st.at[step, i], q_st.at[step, i]), targets(cp_pos, slot, part))):
+                s_sem = (sk_sem.at[i], sv_sem.at[i], sq_sem.at[i, to_core])[kind]
+                here = and_(to_cp == cp_pos, to_core == core)
 
                 @pl.when(here)
                 def _():
                     pltpu.make_async_copy(src, dst, r_sem).start()
 
-                @pl.when(jnp.logical_not(here))
+                @pl.when(far)
                 def _():
-                    pltpu.make_async_remote_copy(src, dst, s_sem, r_sem, device_id=mesh_id(to_cp, PAIR * x_pos + to_core),
-                                                 device_id_type=MESH).start()
+                    remote(src, far_refs[kind].at[part, slot], s_sem, far_sem.at[kind, part, slot], cp_pos + 1 - PAIR * part, core).start()
+
+                @pl.when(not_(or_(here, far)))
+                def _():
+                    remote(src, dst, s_sem, r_sem, to_cp, to_core).start()
+
+    def pass_far(step, what):
+        slot, part, _ = place_of(step)
+        sign = 1 - PAIR * part
+
+        @pl.when((cp_pos + sign + n_cp) % n_cp // n_loc == core)
+        def _():
+            for kind, (dst, to_core, r_sem) in enumerate(targets((cp_pos - sign + n_cp) % n_cp, slot, part)):
+                src = far_refs[kind].at[part, slot]
+                copy = remote(src, dst, pass_sem.at[kind, part, slot], r_sem, cp_pos + sign, to_core)
+                if what == "start":
+                    pltpu.make_async_copy(src, src, far_sem.at[kind, part, slot]).wait()
+                    copy.start()
+                else:
+                    copy.wait_send()
 
     def project(step, carry):
         slot, part, off = place_of(step)
@@ -494,12 +526,14 @@
         @pl.when(step == 0)
         def _():
             own_copy.wait()
+            for one in w_loads:
+                one.wait()
 
         @pl.when(step > 1)
         def _():
             pass_on(slot, part, sibling, pair_sem.at[0]).wait_recv()
 
-        @pl.when(jnp.logical_and(wave > 0, other == 0))
+        @pl.when(and_(wave > 0, other == 0))
         def _():
             @pl.when(wave == 1)
             def _():
@@ -507,7 +541,7 @@
             pass_on(slot, part, sibling, pair_sem.at[PAIR * wave + side]).start()
 
         x_rows = x_buf[slot, pl.ds(pl.multiple_of(part * half, half), half), :]
-        qkv = jnp.dot(x_rows, w_ref[...], preferred_element_type=jnp.float32)
+        qkv = jnp.dot(x_rows, w_buf[...], preferred_element_type=jnp.float32)
         for i in range(n_loc):
             q_st[step, i] = qkv[:, i * head_dim:(i + 1) * head_dim].astype(jnp.bfloat16)
             k_st[step, i] = qkv[:, (n_loc + i) * head_dim:(n_loc + i + 1) * head_dim].astype(jnp.bfloat16)
@@ -516,11 +550,21 @@
         @pl.when(step > 0)
         def _():
             outputs_of(step - 1)
+
+        @pl.when(step >= lag)
+        def _():
+            pass_far(step - lag, "start")
         return carry
 
-    n_steps = PAIR * n_tp
+    n_steps, lag = PAIR * n_tp, 4
     lax.fori_loop(0, n_steps, project, 0)
     outputs_of(n_steps - 1)
+
+    def pass_late(step, carry):
+        pass_far(step, "start")
+        return carry
+
+    lax.fori_loop(n_steps - lag, n_steps, pass_late, 0)
 
     def whole(ref, count, sem):
         return pltpu.make_async_copy(ref.at[pl.ds(0, count)], ref.at[pl.ds(0, count)], sem)
@@ -551,9 +595,14 @@
         to_cp = n_loc * core + i
         for sem, to_core, count in ((sk_sem.at[i], 0, PAIR * chunk_len), (sv_sem.at[i], 1, PAIR * chunk_len),
                                     (sq_sem.at[i, 0], 0, chunk_len), (sq_sem.at[i, 1], 1, chunk_len)):
-            @pl.when(jnp.logical_not(jnp.logical_and(to_cp == cp_pos, to_core == core)))
+            @pl.when(not_(and_(to_cp == cp_pos, to_core == core)))
             def _():
                 whole(k_hbm, count, sem).wait()
+    def drain(step, carry):
+        pass_far(step, "wait")
+        return carry
+
+    lax.fori_loop(0, n_steps, drain, 0)
     for core_id in BOTH:
         @pl.when(core == core_id)
         def _():
@@ -563,7 +612,7 @@
                     forward(y, place, 1 - core_id).wait_recv()
 
 
-def front_call(n_cp, n_tp, x_loc, w_qkv, head_dim, n_loc):
+def front_call(n_cp, n_tp, x_loc, w_parts, head_dim, n_loc):
     tok_dev, hid = x_loc.shape
     half = tok_dev // PAIR
     seq = tok_dev * n_cp * n_tp
@@ -574,33 +623,40 @@
         name="gather_project",
         out_shape=(jax.ShapeDtypeStruct((seq, head_dim), jnp.bfloat16), jax.ShapeDtypeStruct((head_dim, seq), jnp.bfloat16),
                    jax.ShapeDtypeStruct((seq // PAIR, head_dim), jnp.bfloat16)),
-        in_specs=[any_spec, pl.BlockSpec(memory_space=pltpu.VMEM)],
-        out_specs=(any_spec, any_spec, any_spec),
+        in_specs=[any_spec] * 4,
+        out_specs=(any_spec,) * 3,
         scratch_shapes=[
             pltpu.VMEM((n_tp, tok_dev, hid), jnp.bfloat16),
+            pltpu.VMEM((hid, 3 * n_loc * head_dim), jnp.bfloat16),
             pltpu.VMEM((n_steps, n_loc, half, head_dim), jnp.bfloat16),
             pltpu.VMEM((n_steps, n_loc, half, head_dim), jnp.bfloat16),
             pltpu.VMEM((n_steps, n_loc, head_dim, half), jnp.bfloat16),
-            pltpu.SemaphoreType.DMA,
-            pltpu.SemaphoreType.DMA((6,)),
-            pltpu.SemaphoreType.DMA((8,)),
-            pltpu.SemaphoreType.DMA((n_tp, 2)),
-            pltpu.SemaphoreType.DMA((n_loc,)),
-            pltpu.SemaphoreType.DMA((n_loc,)),
-            pltpu.SemaphoreType.DMA((n_loc, 2)),
-            pltpu.SemaphoreType.DMA((n_cp,)),
-            pltpu.SemaphoreType.DMA((n_cp,)),
-            pltpu.SemaphoreType.DMA((PAIR * n_cp,)),
-            pltpu.SemaphoreType.DMA((PAIR * n_cp,)),
+            pltpu.VMEM((PAIR, n_tp, half, head_dim), jnp.bfloat16),
+            pltpu.VMEM((PAIR, n_tp, head_dim, half), jnp.bfloat16),
+            pltpu.VMEM((PAIR, n_tp, half, head_dim), jnp.bfloat16),
+            dma,
+            dma((3,)),
+            dma((6,)),
+            dma((8,)),
+            dma((n_tp, PAIR)),
+            dma((n_loc,)),
+            dma((n_loc,)),
+            dma((n_loc, PAIR)),
+            dma((n_cp,)),
+            dma((n_cp,)),
+            dma((PAIR * n_cp,)),
+            dma((PAIR * n_cp,)),
+            dma((3, PAIR, n_tp)),
+            dma((3, PAIR, n_tp)),
         ],
         compiler_params=pltpu.CompilerParams(collective_id=0, has_side_effects=True, vmem_limit_bytes=VMEM_LIMIT),
-        cost_estimate=pl.CostEstimate(flops=PAIR * n_tp * tok_dev * hid * w_qkv.shape[1], bytes_accessed=2**26, transcendentals=0),
-    )(x_loc, w_qkv)
+        cost_estimate=pl.CostEstimate(flops=PAIR * n_tp * tok_dev * hid * 3 * n_loc * head_dim, bytes_accessed=2**26, transcendentals=0),
+    )(x_loc, *w_parts)
 
 
 def attend_kernel(n_cp, n_tp, k_hbm, vt_hbm, q_hbm, x_hbm, wo_hbm, wg_hbm, wu_hbm, wd_hbm, rank_hbm,
                   h_ref, o_hbm, wgx_hbm, wux_hbm, wdx_hbm, near_hbm,
-                  k_buf, vt_buf, q_buf, qt_buf, o_st, o_buf, wo_buf, x_buf, s_even, s_odd, acc, m_ref, l_ref,
+                  k_buf, vt_buf, q_buf, qt_buf, o_st, o_buf, wo_buf, x_buf, s_even, s_odd, p_even, p_odd, p_near, shrink_even, shrink_odd, acc, m_ref, l_ref,
                   in_sem, so_sem, ro_sem, swo_sem, rwo_sem, sw_sem, rw_sem, sr_sem, rr_sem, o_sem):
     n_dev = n_cp * n_tp
     n_x = n_tp // PAIR
@@ -631,7 +687,7 @@
                                           device_id=mesh_id(cp_pos, PAIR * x_pos + 1 - core), device_id_type=MESH)
              for i, (src, dst) in enumerate(((wg_hbm, wgx_hbm), (wu_hbm, wux_hbm), (wd_hbm, wdx_hbm)))]
     ranks = []
-    for slot, off in ((1, 1), (2, -1), (3, 2)):
+    for slot, off in ((1, 1), (PAIR, -1), (3, PAIR)):
         for part, place in enumerate((((cp_pos + off + n_cp) % n_cp, tp_pos), (cp_pos, PAIR * ((x_pos + off + n_x) % n_x) + core))):
             ranks.append(pltpu.make_async_remote_copy(rank_hbm, near_hbm.at[part, slot], sr_sem.at[part, slot], rr_sem.at[part, slot],
                                                       device_id=mesh_id(*place), device_id_type=MESH))
@@ -642,61 +698,82 @@
     for one in loads[:3]:
         one.wait()
 
-    def update(s_vals, s_top, v_cols, lo, width):
-        cols = pl.ds(lo, width)
+    def columns(block):
+        return pl.ds(pl.multiple_of(block * tok_dev, tok_dev), tok_dev)
+
+    def scores(block, cols, s_ref, masked):
+        s_vals = jnp.dot(k_buf[columns(block), :], qt_buf[:, cols], preferred_element_type=jnp.float32)
+        if masked:
+            key_id = lax.broadcasted_iota(jnp.int32, s_vals.shape, 0)
+            query_id = lax.broadcasted_iota(jnp.int32, s_vals.shape, 1)
+            s_vals = jnp.where(key_id <= query_id, s_vals, -1e30)
+        s_ref[...] = s_vals
+        return jnp.max(s_vals, **COLUMN_WISE)
+
+    def soften(s_ref, s_top, cols, p_ref, shrink_ref):
         m_old = m_ref[:, cols]
         m_new = jnp.maximum(m_old, s_top)
-        prob = jnp.exp2((s_vals - m_new) * scale)
         shrink = jnp.exp2((m_old - m_new) * scale)
         m_ref[:, cols] = m_new
-        l_ref[:, cols] = l_ref[:, cols] * shrink + jnp.sum(prob, axis=0, keepdims=True)
-        acc[:, cols] = acc[:, cols] * shrink + jnp.dot(v_cols, prob.astype(jnp.bfloat16), preferred_element_type=jnp.float32)
-
-    def keys_at(block):
-        return k_buf[pl.ds(pl.multiple_of(block * tok_dev, tok_dev), tok_dev), :]
-
-    def values_at(block):
-        return vt_buf[:, pl.ds(pl.multiple_of(block * tok_dev, tok_dev), tok_dev)]
-
-    def query_pair(g, carry):
+        shrink_ref[...] = shrink
+        prob = jnp.exp2((s_ref[...] - m_new) * scale)
+        l_ref[:, cols] = l_ref[:, cols] * shrink + jnp.sum(prob, **COLUMN_WISE)
+        p_ref[...] = prob.astype(jnp.bfloat16)
+
+    def gather_values(block, cols, p_ref, shrink_ref):
+        acc[:, cols] = acc[:, cols] * shrink_ref[...] + jnp.dot(vt_buf[:, columns(block)], p_ref[...], preferred_element_type=jnp.float32)
+
+    def query_pair(turn, carry):
+        g = (turn + n_x * (cp_pos % PAIR) + x_pos) % (n_dev // 4)
         q_rows = q_buf[pl.ds(pl.multiple_of(g * PAIR * tok_dev, PAIR * tok_dev), PAIR * tok_dev), :]
         qt_buf[...] = q_rows.astype(jnp.float32).T.astype(jnp.bfloat16)
         m_ref[...] = jnp.full_like(m_ref, -1e30)
         l_ref[...] = jnp.zeros_like(l_ref)
         acc[...] = jnp.zeros_like(acc)
-        for r in BOTH:
-            lo = r * tok_dev
-            inner = (1 - core) * 3 * r + core * (1 + r)
-
-            def near_scores(block):
-                return jnp.dot(keys_at(block), qt_buf[:, pl.ds(lo, tok_dev)], preferred_element_type=jnp.float32)
-
-            s_vals = near_scores(4 * g + inner)
-            key_id = lax.broadcasted_iota(jnp.int32, s_vals.shape, 0)
-            query_id = lax.broadcasted_iota(jnp.int32, s_vals.shape, 1)
-            s_vals = jnp.where(key_id <= query_id, s_vals, -1e30)
-            update(s_vals, jnp.max(s_vals, axis=0, keepdims=True), values_at(4 * g + inner), lo, tok_dev)
-
-            def near_block(j, inner_carry):
-                s_near = near_scores(4 * g + j)
-                update(s_near, jnp.max(s_near, axis=0, keepdims=True), values_at(4 * g + j), lo, tok_dev)
-                return inner_carry
-
-            lax.fori_loop(0, inner, near_block, 0)
-
-        def far_scores(block, s_ref):
-            s_vals = jnp.dot(keys_at(block), qt_buf[...], preferred_element_type=jnp.float32)
-            s_ref[...] = s_vals
-            return jnp.max(s_vals, axis=0, keepdims=True)
+        p_odd[...] = jnp.zeros_like(p_odd)
+        shrink_odd[...] = jnp.ones_like(shrink_odd)
+        near = ((0, core), (1, 3 - core), (1 - core, 0), (1, 1 - core), (1, 2 - core))
+        lanes = [(s_even, p_even, shrink_even, 0), (s_even, p_even, shrink_even, 1), (s_odd, p_near, shrink_odd, 0), (s_odd, p_near, shrink_odd, 1)]
+        tops = {}
+
+        def near_refs(i):
+            s_ref, p_ref, shrink_ref, place = lanes[i % 4]
+            cols = pl.ds(place * tok_dev, tok_dev)
+            return s_ref.at[:, cols], p_ref.at[:, cols], shrink_ref.at[:, cols]
+
+        def near_scores(i):
+            r, block = near[i]
+            tops[i] = scores(4 * g + block, columns(r), near_refs(i)[0], i < 2)
+
+        def near_soften(i):
+            s_ref, p_ref, shrink_ref = near_refs(i)
+            soften(s_ref, tops[i], columns(near[i][0]), p_ref, shrink_ref)
+
+        def near_values(i):
+            _, p_ref, shrink_ref = near_refs(i)
+            gather_values(4 * g + near[i][1], columns(near[i][0]), p_ref, shrink_ref)
+
+        for i in range(len(near) + 2):
+            if i < len(near):
+                near_scores(i)
+            if 0 <= i - 1 < len(near):
+                near_soften(i - 1)
+            if 0 <= i - 2:
+                near_values(i - 2)
+        shrink_odd[...] = jnp.ones_like(shrink_odd)
+        wide = pl.ds(0, PAIR * tok_dev)
 
         def far_pair(n, top_even):
-            top_odd = far_scores(PAIR * n + 1, s_odd)
-            update(s_even[...], top_even, values_at(PAIR * n), 0, PAIR * tok_dev)
-            top_next = far_scores(PAIR * n + 2, s_even)
-            update(s_odd[...], top_odd, values_at(PAIR * n + 1), 0, PAIR * tok_dev)
+            top_odd = scores(PAIR * n + 1, wide, s_odd, False)
+            soften(s_even, top_even, wide, p_even, shrink_even)
+            gather_values(jnp.maximum(PAIR * n - 1, 0), wide, p_odd, shrink_odd)
+            top_next = scores(PAIR * n + 2, wide, s_even, False)
+            soften(s_odd, top_odd, wide, p_odd, shrink_odd)
+            gather_values(PAIR * n, wide, p_even, shrink_even)
             return top_next
 
-        lax.fori_loop(0, PAIR * g, far_pair, far_scores(0, s_even))
+        lax.fori_loop(0, PAIR * g, far_pair, scores(0, wide, s_even, False))
+        gather_values(jnp.maximum(4 * g - 1, 0), wide, p_odd, shrink_odd)
         out = (acc[...] / l_ref[...]).T.astype(jnp.bfloat16)
         for r in BOTH:
             o_st[PAIR * g + r] = out[r * tok_dev:(r + 1) * tok_dev]
@@ -706,13 +783,13 @@
     def o_push(index, what):
         block = 4 * (index // PAIR) + (1 - core) * 3 * (index % PAIR) + core * (1 + index % PAIR)
         to_cp, to_tp = owner_of(block, n_cp, n_tp)
-        here = jnp.logical_and(to_cp == cp_pos, to_tp == tp_pos)
+        here = and_(to_cp == cp_pos, to_tp == tp_pos)
         if what == "start":
             @pl.when(here)
             def _():
                 pltpu.make_async_copy(o_st.at[index], o_hbm.at[head], ro_sem.at[head]).start()
 
-        @pl.when(jnp.logical_not(here))
+        @pl.when(not_(here))
         def _():
             copy = pltpu.make_async_remote_copy(o_st.at[index], o_hbm.at[head], so_sem.at[index], ro_sem.at[head],
                                                 device_id=mesh_id(to_cp, to_tp), device_id_type=MESH)
@@ -764,9 +841,9 @@
     h_loc, _, wg_other, wu_other, wd_other, near_rows = pl.pallas_call(
         functools.partial(attend_kernel, n_cp, n_tp),
         name="attend_heads",
-        out_shape=(jax.ShapeDtypeStruct((2, tok_dev, hid // PAIR), bf16), jax.ShapeDtypeStruct((n_heads, tok_dev, head_dim), bf16))
+        out_shape=(jax.ShapeDtypeStruct((PAIR, tok_dev, hid // PAIR), bf16), jax.ShapeDtypeStruct((n_heads, tok_dev, head_dim), bf16))
         + tuple(jax.ShapeDtypeStruct((keep,) + w.shape[1:], bf16) for w in (w_gate, w_up, w_down))
-        + (jax.ShapeDtypeStruct((2, 4) + rank_rows.shape, jnp.float32),),
+        + (jax.ShapeDtypeStruct((PAIR, 4) + rank_rows.shape, jnp.float32),),
         in_specs=[any_spec] * 9,
         out_specs=(pl.BlockSpec(memory_space=pltpu.VMEM),) + (any_spec,) * 5,
         scratch_shapes=[
@@ -780,19 +857,24 @@
             pltpu.VMEM((tok_dev, hid), bf16),
             pltpu.VMEM((tok_dev, PAIR * tok_dev), jnp.float32),
             pltpu.VMEM((tok_dev, PAIR * tok_dev), jnp.float32),
+            pltpu.VMEM((tok_dev, PAIR * tok_dev), bf16),
+            pltpu.VMEM((tok_dev, PAIR * tok_dev), bf16),
+            pltpu.VMEM((tok_dev, PAIR * tok_dev), bf16),
+            pltpu.VMEM((1, PAIR * tok_dev), jnp.float32),
+            pltpu.VMEM((1, PAIR * tok_dev), jnp.float32),
             pltpu.VMEM((head_dim, PAIR * tok_dev), jnp.float32),
             pltpu.VMEM((1, PAIR * tok_dev), jnp.float32),
             pltpu.VMEM((1, PAIR * tok_dev), jnp.float32),
-            pltpu.SemaphoreType.DMA((5,)),
-            pltpu.SemaphoreType.DMA((n_dev // PAIR,)),
-            pltpu.SemaphoreType.DMA((n_heads,)),
-            pltpu.SemaphoreType.DMA((n_tp,)),
-            pltpu.SemaphoreType.DMA((n_tp,)),
-            pltpu.SemaphoreType.DMA((3,)),
-            pltpu.SemaphoreType.DMA((3,)),
-            pltpu.SemaphoreType.DMA((2, 4)),
-            pltpu.SemaphoreType.DMA((2, 4)),
-            pltpu.SemaphoreType.DMA,
+            dma((5,)),
+            dma((n_dev // PAIR,)),
+            dma((n_heads,)),
+            dma((n_tp,)),
+            dma((n_tp,)),
+            dma((3,)),
+            dma((3,)),
+            dma((PAIR, 4)),
+            dma((PAIR, 4)),
+            dma,
         ],
         compiler_params=pltpu.CompilerParams(collective_id=1, has_side_effects=True, vmem_limit_bytes=VMEM_LIMIT),
         cost_estimate=pl.CostEstimate(flops=PAIR * seq * seq * head_dim // PAIR, bytes_accessed=2**26, transcendentals=seq * seq // 4),
@@ -812,9 +894,9 @@
         n_loc, head_dim = w_q.shape[1:]
         n_experts = w_gate.shape[0] * n_cp * n_tp // PAIR
         capacity = ids_loc.shape[1] * tok_dev // n_experts
-        w_qkv = jnp.concatenate([w.reshape(hid_dim, n_loc * head_dim) for w in (w_q, w_k, w_v)], axis=1)
+        w_parts = [w.reshape(hid_dim, n_loc * head_dim) for w in (w_q, w_k, w_v)]
         rank_rows, gate_rows = routing_rows(ids_loc, gates_loc, n_experts)
-        k_all, vt_all, q_all = front_call(n_cp, n_tp, x_loc, w_qkv, head_dim, n_loc)
+        k_all, vt_all, q_all = front_call(n_cp, n_tp, x_loc, w_parts, head_dim, n_loc)
         h_loc, near_rows, *others = attend_call(n_cp, n_tp, k_all, vt_all, q_all, x_loc, w_o.reshape(n_loc * head_dim, hid_dim), w_gate, w_up, w_down, rank_rows)
         return moe_call(n_cp, n_tp, capacity, h_loc, rank_rows, near_rows, gate_rows, w_gate, w_up, w_down, *others)
 

time: 644 us -> 609 us (0.946); the launches traced: 642 us -> 601 us
  Pallas kernels: 631 us -> 588 us
    pallas_call x1, Pallas kernels: 392 us -> 346 us  [moe_call(): pl.pallas_call(functools.partial(moe_kernel, n_cp, n_tp, group), name='ro...]
where the time goes in v4:
time: 609 us; the launch traced here: 601 us
  Pallas kernels  588 us (97%)
  local copies, waits for them, and re-layouts  8.76 us (1%)
    pallas_call x1, Pallas kernels, moe_call(): pl.pallas_call(functools.partial(moe_kernel, n_cp, n_tp, group), name='ro...  346 us
    pallas_call x1, Pallas kernels, attend_call(): pl.pallas_call(functools.partial(attend_kernel, n_cp, n_tp), name='attend...  134 us
    pallas_call x1, Pallas kernels, front_call(): pl.pallas_call(functools.partial(front_kernel, n_cp, n_tp), name='gather_...  109 us

profile of v4, /device:TPU:99, one launch (start us, length us, event | category | flops | bytes accessed | tf_op | source)
XLA Modules:
  0.0 600.7 jit_solution(3516764777949500884)
XLA Ops:
  0.0 1.1 fusion
  1.1 0.8 convolution_select_fusion.rank_hbm
  1.9 1.7 select_reduce_fusion.gate_ref
  3.6 2.3 copy.17
  6.0 3.3 copy_bitcast_fusion
  9.2 108.5 %gather_project.1 = (bf16[16384,128]{1,0:T(8,128)(2,1)}, bf16[128,16384]{1,0:T(8,128)(2,1)}, bf16[8192,128]{1,0:T(8,128)(2,1)}) custom-call(bf16[512,2048]{1,0:T(8,128)(2,1)} %x_hbm.3, bf16[2048,256]{1,0:T(8,128)(2,1)} %bitcast.15, bf16[2048,256]{1,0:T(8,128)(2,1)} %get-tuple-element.24.wk_hbm, bf16[2048,256]{1,0:T(8,128)(2,1)} %get-tuple-element.23.wv_hbm), custom_call_target="tpu_custom_call" | custom-call | flops 12884901888 | bytes 67108864 | tf_op jit(solution)/shard_map/gather_project/pallas_call | solution.py:621
  117.8 134.0 %attend_heads.1 = (bf16[2,512,1024]{2,1,0:T(8,128)(2,1)}, bf16[16,512,128]{2,1,0:T(8,128)(2,1)}, bf16[2,2048,512]{2,1,0:T(8,128)(2,1)}, bf16[2,2048,512]{2,1,0:T...) custom-call(bf16[16384,128]{1,0:T(8,128)(2,1)} %get-tuple-element.14.k_hbm, ...), custom_call_target="tpu_custom_call" | custom-call | flops 34359738368 | bytes 67108864 | tf_op jit(solution)/shard_map/attend_heads/pallas_call | solution.py:841
  251.8 345.7 %routed_experts.1 = (bf16[512,2048]{1,0:T(8,128)(2,1)}, bf16[2,32,128,1024]{3,2,1,0:T(8,128)(2,1)}, bf16[2,2,4,2,64,1024]{5,4,3,2,1,0:T(8,128)(2,1)}, bf16[32,12...) custom-call(bf16[2,512,1024]{2,1,0:T(8,128)(2,1)} %get-tuple-element.17.h_hbm, ...), custom_call_target="tpu_custom_call" | custom-call | flops 51539607552 | bytes 134217728 | tf_op jit(solution)/shard_map/routed_experts/pallas_call | solution.py:369
  597.5 3.2 copy.19

commit v5 on v4

--- a/solution.py
+++ b/solution.py
@@ -16,9 +16,10 @@
 and_, or_, not_ = jnp.logical_and, jnp.logical_or, jnp.logical_not
 VMEM_LIMIT = 66_000_000
 PLACES = ((0, 0), (0, 1), (1, 0), (0, -1), (-1, 0), (1, 1), (-1, -1), (1, -1), (-1, 1), (0, PAIR), (PAIR, 0), (1, PAIR), (PAIR, 1), (-1, PAIR), (PAIR, -1), (PAIR, PAIR))
-N_NEAR, FIRST_FAR = 5, 9
-GROUPS = ("1234", "1234", "9a9a", "bcbc", "dede", "0f0f", "5656", "7878")
-FLIPS = ("0000", "1111") + ("0011",) * 6
+FIRST_FAR = 9
+GROUPS = ("5656", "7878", "bcbc", "dede", "9a9a", "0f0f", "1234", "1234")
+FLIPS = ("0011",) * 6 + ("0000", "1111")
+ADD_ORDER = "05678bcde9a1234f"
 SOURCES = (0, -1, 1, PAIR)
 
 
@@ -236,6 +237,26 @@
         for q in range(group):
             await_bytes(z_ring.at[slot, q], sz_sem.at[slot, q])
 
+    n_far = len(PLACES) - FIRST_FAR
+
+    def z_relay(index, flip, way):
+        off_y, off_x = PLACES[FIRST_FAR + index]
+        sign = 1 - PAIR * way
+        lead_y, lead_x = sign * (off_y == 2), sign * (off_x == 2)
+        from_line = line(at(-lead_y, -lead_x, 0))
+        to_y = sign if off_y == 2 else off_y
+        to_x = sign if off_x == 2 else off_x
+        return send(zl_hbm.at[index, flip, way], rz_hbm.at[from_line, pl.ds(way * cap, cap)], fz_sem.at[index, flip, way],
+                    rz_sem.at[from_line], at(to_y, to_x, flip))
+
+    def each_relay(*indices):
+        return [(index, flip, way) for flip in BOTH for way in BOTH for index in indices]
+
+    def run_z_relays(*indices):
+        for key in each_relay(*indices):
+            await_bytes(zl_hbm.at[key], zl_sem.at[key])
+            z_relay(*key).start()
+
     def expert_group(g, carry):
         slot = g % 3
 
@@ -277,32 +298,16 @@
                     sign = 1 - PAIR * way
                     send(z_ring.at[slot, q, pl.ds(way * cap, cap)], zl_hbm.at[p - FIRST_FAR, flip, way], sz_sem.at[slot, q],
                          zl_sem.at[p - FIRST_FAR, flip, way], at(sign * lead_y, sign * lead_x, 0)).start()
+        for turn, indices in ((5, (PAIR, 3)), (6, (4, 5)), (7, (0, 1))):
+            @pl.when(g == turn)
+            def _():
+                run_z_relays(*indices)
         return carry
 
     lax.fori_loop(0, len(GROUPS), expert_group, 0)
 
-    n_far = len(PLACES) - FIRST_FAR
-
-    def z_relay(index, flip, way):
-        off_y, off_x = PLACES[FIRST_FAR + index]
-        sign = 1 - PAIR * way
-        lead_y, lead_x = sign * (off_y == 2), sign * (off_x == 2)
-        from_line = line(at(-lead_y, -lead_x, 0))
-        to_y = sign if off_y == 2 else off_y
-        to_x = sign if off_x == 2 else off_x
-        return send(zl_hbm.at[index, flip, way], rz_hbm.at[from_line, pl.ds(way * cap, cap)], fz_sem.at[index, flip, way],
-                    rz_sem.at[from_line], at(to_y, to_x, flip))
-
-    def each_relay(*indices):
-        return [(index, flip, way) for flip in BOTH for way in BOTH for index in indices]
-
-    def run_z_relays(*indices):
-        for key in each_relay(*indices):
-            await_bytes(zl_hbm.at[key], zl_sem.at[key])
-            z_relay(*key).start()
-
-    def combine(p, carry):
-        off_y, off_x = pick([a for a, _ in PLACES], p), pick([b for _, b in PLACES], p)
+    def combine(turn, carry):
+        off_y, off_x = (pick([PLACES[int(p, 16)][k] for p in ADD_ORDER], turn) for k in BOTH)
         homes = [line(at(-off_y, -off_x, q)) for q in BOTH]
         loads = []
         for q in BOTH:
@@ -328,12 +333,9 @@
             acc[:, pl.ds(col, n_cols)] += total
         return carry
 
-    run_z_relays(0, 1)
-    run_z_relays(PAIR, 3)
-    lax.fori_loop(0, N_NEAR, combine, 0)
-    run_z_relays(4, 5)
+    lax.fori_loop(0, FIRST_FAR - 4, combine, 0)
     run_z_relays(6)
-    lax.fori_loop(N_NEAR, len(PLACES), combine, 0)
+    lax.fori_loop(FIRST_FAR - 4, len(ADD_ORDER), combine, 0)
     y_ref[...] = acc[...].astype(jnp.bfloat16)
 
     for part in BOTH:
@@ -420,11 +422,11 @@
     return late * (PAIR * n_cp - 1 - chunk) + (1 - late) * chunk, late * per_chunk + block % per_chunk
 
 
-def front_kernel(n_cp, n_tp, x_hbm, wq_hbm, wk_hbm, wv_hbm, k_hbm, vt_hbm, q_hbm, x_buf, w_buf, q_st, k_st, vt_st, k_far, vt_far, q_far,
+def front_kernel(n_cp, n_tp, n_part, x_hbm, wq_hbm, wk_hbm, wv_hbm, k_hbm, vt_hbm, q_hbm, x_buf, w_buf, q_st, k_st, vt_st, k_far, vt_far, q_far,
                  own_sem, w_sem, ring_sem, pair_sem, rx_sem, sk_sem, sv_sem, sq_sem, kv_sem, rq_sem, sf_sem, rf_sem, far_sem, pass_sem):
     n_x = n_tp // PAIR
     tok_dev, hid = x_hbm.shape
-    half = tok_dev // PAIR
+    half = tok_dev // n_part
     head_dim = k_hbm.shape[1]
     n_loc = q_st.shape[1]
     chunk_len = tok_dev * n_x
@@ -449,7 +451,7 @@
     pl.semaphore_wait(barrier, PAIR * n_cp + 1)
 
     def own_send(part, to_tp, sem):
-        rows = pl.ds(part * half, half)
+        rows = pl.ds(pl.multiple_of(part * half, half), half)
         return pltpu.make_async_remote_copy(x_hbm.at[rows], x_buf.at[tp_pos, rows], sem, rx_sem.at[tp_pos, part],
                                             device_id=mesh_id(cp_pos, to_tp), device_id_type=MESH)
 
@@ -458,17 +460,25 @@
         return pltpu.make_async_remote_copy(x_buf.at[slot, rows], x_buf.at[slot, rows], sem, rx_sem.at[slot, part],
                                             device_id=mesh_id(cp_pos, to_tp), device_id_type=MESH)
 
-    for i, (part, off) in enumerate(((0, 1), (1, -1), (1, 1), (0, -1))):
-        own_send(part, slot_at(off, 0), ring_sem.at[i]).start()
-    for part in BOTH:
+    def ring_send(i, side):
+        part = i if side == 0 else n_part - 1 - i
+        return own_send(part, slot_at(1 - PAIR * side, 0), ring_sem.at[side, i])
+
+    for i in BOTH:
+        for side in BOTH:
+            ring_send(i, side).start()
+    for part in range(n_part):
         own_send(part, sibling, pair_sem.at[part]).start()
+    first = PAIR * n_part
 
     def place_of(step):
-        wave, other, side = step // 4, (step // PAIR) % PAIR, step % PAIR
-        near = ((wave + 1) // PAIR) % PAIR
-        swap = (wave // PAIR) * (1 - wave // 3)
-        off = near * (PAIR * side - 1) + PAIR * (wave // 3)
-        return slot_at(off, other), side + swap * (1 - PAIR * side), off
+        late = jnp.minimum(step // first, 1)
+        wave, other, side = jnp.maximum(step - first, 0) // 4, late * ((step // PAIR) % PAIR) + (1 - late) * (step // n_part), step % PAIR
+        piece = pick((0, 1, 0, PAIR, 1, 3), wave)
+        through = jnp.where(or_(wave == 2, wave == 4), 1, 0)
+        part = late * (piece + side * (n_part - 1 - PAIR * piece)) + (1 - late) * (step % n_part)
+        off = late * ((1 - through) * (PAIR * side - 1) + PAIR * through)
+        return slot_at(off, other), part, off
 
     def targets(from_cp, slot, part):
         block = block_of(from_cp, slot, n_cp, n_tp)
@@ -498,7 +508,7 @@
 
                 @pl.when(far)
                 def _():
-                    remote(src, far_refs[kind].at[part, slot], s_sem, far_sem.at[kind, part, slot], cp_pos + 1 - PAIR * part, core).start()
+                    remote(src, far_refs[kind].at[part, slot], s_sem, far_sem.at[kind, part, slot], cp_pos + 1 - part // PAIR * 2, core).start()
 
                 @pl.when(not_(or_(here, far)))
                 def _():
@@ -506,7 +516,7 @@
 
     def pass_far(step, what):
         slot, part, _ = place_of(step)
-        sign = 1 - PAIR * part
+        sign = 1 - part // PAIR * 2
 
         @pl.when((cp_pos + sign + n_cp) % n_cp // n_loc == core)
         def _():
@@ -521,7 +531,7 @@
 
     def project(step, carry):
         slot, part, off = place_of(step)
-        wave, other, side = step // 4, (step // PAIR) % PAIR, step % PAIR
+        wave, other, side = (step - first) // 4, (step // PAIR) % PAIR, step % PAIR
 
         @pl.when(step == 0)
         def _():
@@ -529,16 +539,20 @@
             for one in w_loads:
                 one.wait()
 
-        @pl.when(step > 1)
+        @pl.when(step >= n_part)
         def _():
             pass_on(slot, part, sibling, pair_sem.at[0]).wait_recv()
 
-        @pl.when(and_(wave > 0, other == 0))
+        @pl.when(and_(step >= first, other == 0))
         def _():
-            @pl.when(wave == 1)
+            @pl.when(wave < 2)
             def _():
-                pass_on(slot, part, slot_at(-off, 0), ring_sem.at[4 + side]).start()
-            pass_on(slot, part, sibling, pair_sem.at[PAIR * wave + side]).start()
+                pass_on(slot, part, slot_at(-off, 0), ring_sem.at[side, n_part + wave]).start()
+                for i in BOTH:
+                    @pl.when(side == i)
+                    def _():
+                        ring_send(2 + wave, i).start()
+            pass_on(slot, part, sibling, pair_sem.at[n_part + PAIR * wave + side]).start()
 
         x_rows = x_buf[slot, pl.ds(pl.multiple_of(part * half, half), half), :]
         qkv = jnp.dot(x_rows, w_buf[...], preferred_element_type=jnp.float32)
@@ -556,7 +570,7 @@
             pass_far(step - lag, "start")
         return carry
 
-    n_steps, lag = PAIR * n_tp, 4
+    n_steps, lag = n_part * n_tp, 8
     lax.fori_loop(0, n_steps, project, 0)
     outputs_of(n_steps - 1)
 
@@ -585,11 +599,10 @@
                     forward(y, place, core_id).start()
     for y in range(n_cp):
         whole(q_hbm, chunk_len, rq_sem.at[y]).wait()
-    for i in range(4):
-        own_send(0, sibling, ring_sem.at[i]).wait_send()
-    for i in BOTH:
-        own_send(0, sibling, ring_sem.at[4 + i]).wait_send()
-    for i in range(8):
+    for side in BOTH:
+        for i in range(n_part + 2):
+            own_send(0, sibling, ring_sem.at[side, i]).wait_send()
+    for i in range(n_part * n_x):
         own_send(0, sibling, pair_sem.at[i]).wait_send()
     for i in range(n_loc):
         to_cp = n_loc * core + i
@@ -614,12 +627,13 @@
 
 def front_call(n_cp, n_tp, x_loc, w_parts, head_dim, n_loc):
     tok_dev, hid = x_loc.shape
-    half = tok_dev // PAIR
+    n_part, n_x = 4, n_tp // PAIR
+    half = tok_dev // n_part
     seq = tok_dev * n_cp * n_tp
     any_spec = pl.BlockSpec(memory_space=pl.ANY)
-    n_steps = PAIR * n_tp
+    n_steps = n_part * n_tp
     return pl.pallas_call(
-        functools.partial(front_kernel, n_cp, n_tp),
+        functools.partial(front_kernel, n_cp, n_tp, n_part),
         name="gather_project",
         out_shape=(jax.ShapeDtypeStruct((seq, head_dim), jnp.bfloat16), jax.ShapeDtypeStruct((head_dim, seq), jnp.bfloat16),
                    jax.ShapeDtypeStruct((seq // PAIR, head_dim), jnp.bfloat16)),
@@ -631,14 +645,14 @@
             pltpu.VMEM((n_steps, n_loc, half, head_dim), jnp.bfloat16),
             pltpu.VMEM((n_steps, n_loc, half, head_dim), jnp.bfloat16),
             pltpu.VMEM((n_steps, n_loc, head_dim, half), jnp.bfloat16),
-            pltpu.VMEM((PAIR, n_tp, half, head_dim), jnp.bfloat16),
-            pltpu.VMEM((PAIR, n_tp, head_dim, half), jnp.bfloat16),
-            pltpu.VMEM((PAIR, n_tp, half, head_dim), jnp.bfloat16),
+            pltpu.VMEM((n_part, n_tp, half, head_dim), jnp.bfloat16),
+            pltpu.VMEM((n_part, n_tp, head_dim, half), jnp.bfloat16),
+            pltpu.VMEM((n_part, n_tp, half, head_dim), jnp.bfloat16),
             dma,
             dma((3,)),
-            dma((6,)),
-            dma((8,)),
-            dma((n_tp, PAIR)),
+            dma((PAIR, n_part + 2)),
+            dma((n_part * n_x,)),
+            dma((n_tp, n_part)),
             dma((n_loc,)),
             dma((n_loc,)),
             dma((n_loc, PAIR)),
@@ -646,8 +660,8 @@
             dma((n_cp,)),
             dma((PAIR * n_cp,)),
             dma((PAIR * n_cp,)),
-            dma((3, PAIR, n_tp)),
-            dma((3, PAIR, n_tp)),
+            dma((3, n_part, n_tp)),
+            dma((3, n_part, n_tp)),
         ],
         compiler_params=pltpu.CompilerParams(collective_id=0, has_side_effects=True, vmem_limit_bytes=VMEM_LIMIT),
         cost_estimate=pl.CostEstimate(flops=PAIR * n_tp * tok_dev * hid * 3 * n_loc * head_dim, bytes_accessed=2**26, transcendentals=0),
@@ -724,7 +738,7 @@
         acc[:, cols] = acc[:, cols] * shrink_ref[...] + jnp.dot(vt_buf[:, columns(block)], p_ref[...], preferred_element_type=jnp.float32)
 
     def query_pair(turn, carry):
-        g = (turn + n_x * (cp_pos % PAIR) + x_pos) % (n_dev // 4)
+        g = (turn + 1 + cp_pos + x_pos // PAIR * (PAIR * n_cp - 1 - PAIR * cp_pos)) % (n_dev // 4)
         q_rows = q_buf[pl.ds(pl.multiple_of(g * PAIR * tok_dev, PAIR * tok_dev), PAIR * tok_dev), :]
         qt_buf[...] = q_rows.astype(jnp.float32).T.astype(jnp.bfloat16)
         m_ref[...] = jnp.full_like(m_ref, -1e30)
@@ -761,19 +775,28 @@
             if 0 <= i - 2:
                 near_values(i - 2)
         shrink_odd[...] = jnp.ones_like(shrink_odd)
-        wide = pl.ds(0, PAIR * tok_dev)
-
-        def far_pair(n, top_even):
-            top_odd = scores(PAIR * n + 1, wide, s_odd, False)
-            soften(s_even, top_even, wide, p_even, shrink_even)
-            gather_values(jnp.maximum(PAIR * n - 1, 0), wide, p_odd, shrink_odd)
-            top_next = scores(PAIR * n + 2, wide, s_even, False)
-            soften(s_odd, top_odd, wide, p_odd, shrink_odd)
-            gather_values(PAIR * n, wide, p_even, shrink_even)
-            return top_next
-
-        lax.fori_loop(0, PAIR * g, far_pair, scores(0, wide, s_even, False))
-        gather_values(jnp.maximum(4 * g - 1, 0), wide, p_odd, shrink_odd)
+        strip = min(256, tok_dev)
+        strips = [pl.ds(lo, strip) for lo in range(0, PAIR * tok_dev, strip)]
+
+        def far_step(block, parity, tops):
+            s_in, s_out = (s_even, s_odd)[::1 - PAIR * parity]
+            p_out, p_in = (p_even, p_odd)[::1 - PAIR * parity]
+            shrink_out, shrink_in = (shrink_even, shrink_odd)[::1 - PAIR * parity]
+            next_tops = []
+            for cols, top in zip(strips, tops):
+                next_tops.append(scores(block + 1, cols, s_out.at[:, cols], False))
+                soften(s_in.at[:, cols], top, cols, p_out.at[:, cols], shrink_out.at[:, cols])
+                gather_values(jnp.maximum(block - 1, 0), cols, p_in.at[:, cols], shrink_in.at[:, cols])
+            return next_tops
+
+        def far_blocks(n, tops):
+            for j in range(4):
+                tops = far_step(4 * n + j, j % PAIR, tops)
+            return tops
+
+        lax.fori_loop(0, g, far_blocks, [scores(0, cols, s_even.at[:, cols], False) for cols in strips])
+        for cols in strips:
+            gather_values(jnp.maximum(4 * g - 1, 0), cols, p_odd.at[:, cols], shrink_odd.at[:, cols])
         out = (acc[...] / l_ref[...]).T.astype(jnp.bfloat16)
         for r in BOTH:
             o_st[PAIR * g + r] = out[r * tok_dev:(r + 1) * tok_dev]

time: 609 us -> 605 us (level); the launches traced: 601 us -> 604 us
    pallas_call x1, Pallas kernels: 346 us -> 358 us  [moe_call(): pl.pallas_call(functools.partial(moe_kernel, n_cp, n_tp, group), name='ro...]
    pallas_call x1, Pallas kernels: 109 us -> 98.2 us  [front_call(): pl.pallas_call(functools.partial(front_kernel, n_cp, n_tp, n_part), name=...]
where the time goes in v5:
time: 605 us; the launch traced here: 604 us
  Pallas kernels  592 us (98%)
  local copies, waits for them, and re-layouts  8.76 us (1%)
    pallas_call x1, Pallas kernels, moe_call(): pl.pallas_call(functools.partial(moe_kernel, n_cp, n_tp, group), name='ro...  358 us
    pallas_call x1, Pallas kernels, attend_call(): pl.pallas_call(functools.partial(attend_kernel, n_cp, n_tp), name='attend...  135 us
    pallas_call x1, Pallas kernels, front_call(): pl.pallas_call(functools.partial(front_kernel, n_cp, n_tp, n_part), name=...  98.2 us

profile of v5, /device:TPU:99, one launch (start us, length us, event | category | flops | bytes accessed | tf_op | source)
XLA Modules:
  0.0 604.1 jit_solution(7587410992926383260)
XLA Ops:
  0.0 1.1 fusion
  1.1 0.8 convolution_select_fusion.rank_hbm
  1.9 1.7 select_reduce_fusion.gate_ref
  3.6 2.3 copy.17
  6.0 3.3 copy_bitcast_fusion
  9.2 98.2 %gather_project.1 = (bf16[16384,128]{1,0:T(8,128)(2,1)}, bf16[128,16384]{1,0:T(8,128)(2,1)}, bf16[8192,128]{1,0:T(8,128)(2,1)}) custom-call(bf16[512,2048]{1,0:T(8,128)(2,1)} %x_hbm.3, bf16[2048,256]{1,0:T(8,128)(2,1)} %bitcast.15, bf16[2048,256]{1,0:T(8,128)(2,1)} %get-tuple-element.24.wk_hbm, bf16[2048,256]{1,0:T(8,128)(2,1)} %get-tuple-element.23.wv_hbm), custom_call_target="tpu_custom_call" | custom-call | flops 12884901888 | bytes 67108864 | tf_op jit(solution)/shard_map/gather_project/pallas_call | solution.py:635
  107.4 135.1 %attend_heads.1 = (bf16[2,512,1024]{2,1,0:T(8,128)(2,1)}, bf16[16,512,128]{2,1,0:T(8,128)(2,1)}, bf16[2,2048,512]{2,1,0:T(8,128)(2,1)}, bf16[2,2048,512]{2,1,0:T...) custom-call(bf16[16384,128]{1,0:T(8,128)(2,1)} %get-tuple-element.14.k_hbm, ...), custom_call_target="tpu_custom_call" | custom-call | flops 34359738368 | bytes 67108864 | tf_op jit(solution)/shard_map/attend_heads/pallas_call | solution.py:864
  242.6 358.4 %routed_experts.1 = (bf16[512,2048]{1,0:T(8,128)(2,1)}, bf16[2,32,128,1024]{3,2,1,0:T(8,128)(2,1)}, bf16[2,2,4,2,64,1024]{5,4,3,2,1,0:T(8,128)(2,1)}, bf16[32,12...) custom-call(bf16[2,512,1024]{2,1,0:T(8,128)(2,1)} %get-tuple-element.17.h_hbm, ...), custom_call_target="tpu_custom_call" | custom-call | flops 51539607552 | bytes 134217728 | tf_op jit(solution)/shard_map/routed_experts/pallas_call | solution.py:371
  601.0 3.2 copy.19

commit v6 on v5

--- a/solution.py
+++ b/solution.py
@@ -16,10 +16,9 @@
 and_, or_, not_ = jnp.logical_and, jnp.logical_or, jnp.logical_not
 VMEM_LIMIT = 66_000_000
 PLACES = ((0, 0), (0, 1), (1, 0), (0, -1), (-1, 0), (1, 1), (-1, -1), (1, -1), (-1, 1), (0, PAIR), (PAIR, 0), (1, PAIR), (PAIR, 1), (-1, PAIR), (PAIR, -1), (PAIR, PAIR))
-FIRST_FAR = 9
-GROUPS = ("5656", "7878", "bcbc", "dede", "9a9a", "0f0f", "1234", "1234")
-FLIPS = ("0011",) * 6 + ("0000", "1111")
-ADD_ORDER = "05678bcde9a1234f"
+N_NEAR, FIRST_FAR = 5, 9
+GROUPS = ("1234", "1234", "9a9a", "bcbc", "dede", "0f0f", "5656", "7878")
+FLIPS = ("0000", "1111") + ("0011",) * 6
 SOURCES = (0, -1, 1, PAIR)
 
 
@@ -237,6 +236,51 @@
         for q in range(group):
             await_bytes(z_ring.at[slot, q], sz_sem.at[slot, q])
 
+    def expert_group(g, carry):
+        slot = g % 3
+
+        @pl.when(g == 2)
+        def _():
+            run_relays(3)
+
+        sources = [line(at(*place_at(g, q)[:3])) for q in range(group)]
+        loads = []
+        for q in range(group):
+            for part in BOTH:
+                await_bytes(rx_hbm.at[part, sources[q]], rx_sem.at[part, sources[q]])
+                loads.append(pltpu.make_async_copy(rx_hbm.at[part, sources[q]], x_buf.at[q, :, pl.ds(part * half_hid, half_hid)], x_sem.at[part, q]))
+                loads[-1].start()
+
+        @pl.when(g >= 3)
+        def _():
+            await_slot(slot)
+        for one in loads:
+            one.wait()
+        for i in BOTH:
+            expert_rows(slot, i)
+        for q in range(group):
+            off_y, off_x, flip, p = place_at(g, q)
+            alone = and_(p == 0, flip == 0)
+
+            @pl.when(alone)
+            def _():
+                pltpu.make_async_copy(z_ring.at[slot, q], rz_hbm.at[my_line], rz_sem.at[my_line]).start()
+
+            @pl.when(and_(p < FIRST_FAR, not_(alone)))
+            def _():
+                send(z_ring.at[slot, q], rz_hbm.at[my_line], sz_sem.at[slot, q], rz_sem.at[my_line], at(off_y, off_x, flip)).start()
+
+            @pl.when(p >= FIRST_FAR)
+            def _():
+                lead_y, lead_x = jnp.where(off_y == 2, 1, 0), jnp.where(off_x == 2, 1, 0)
+                for way in BOTH:
+                    sign = 1 - PAIR * way
+                    send(z_ring.at[slot, q, pl.ds(way * cap, cap)], zl_hbm.at[p - FIRST_FAR, flip, way], sz_sem.at[slot, q],
+                         zl_sem.at[p - FIRST_FAR, flip, way], at(sign * lead_y, sign * lead_x, 0)).start()
+        return carry
+
+    lax.fori_loop(0, len(GROUPS), expert_group, 0)
+
     n_far = len(PLACES) - FIRST_FAR
 
     def z_relay(index, flip, way):
@@ -257,57 +301,8 @@
             await_bytes(zl_hbm.at[key], zl_sem.at[key])
             z_relay(*key).start()
 
-    def expert_group(g, carry):
-        slot = g % 3
-
-        @pl.when(g == 2)
-        def _():
-            run_relays(3)
-
-        sources = [line(at(*place_at(g, q)[:3])) for q in range(group)]
-        loads = []
-        for q in range(group):
-            for part in BOTH:
-                await_bytes(rx_hbm.at[part, sources[q]], rx_sem.at[part, sources[q]])
-                loads.append(pltpu.make_async_copy(rx_hbm.at[part, sources[q]], x_buf.at[q, :, pl.ds(part * half_hid, half_hid)], x_sem.at[part, q]))
-                loads[-1].start()
-
-        @pl.when(g >= 3)
-        def _():
-            await_slot(slot)
-        for one in loads:
-            one.wait()
-        for i in BOTH:
-            expert_rows(slot, i)
-        for q in range(group):
-            off_y, off_x, flip, p = place_at(g, q)
-            alone = and_(p == 0, flip == 0)
-
-            @pl.when(alone)
-            def _():
-                pltpu.make_async_copy(z_ring.at[slot, q], rz_hbm.at[my_line], rz_sem.at[my_line]).start()
-
-            @pl.when(and_(p < FIRST_FAR, not_(alone)))
-            def _():
-                send(z_ring.at[slot, q], rz_hbm.at[my_line], sz_sem.at[slot, q], rz_sem.at[my_line], at(off_y, off_x, flip)).start()
-
-            @pl.when(p >= FIRST_FAR)
-            def _():
-                lead_y, lead_x = jnp.where(off_y == 2, 1, 0), jnp.where(off_x == 2, 1, 0)
-                for way in BOTH:
-                    sign = 1 - PAIR * way
-                    send(z_ring.at[slot, q, pl.ds(way * cap, cap)], zl_hbm.at[p - FIRST_FAR, flip, way], sz_sem.at[slot, q],
-                         zl_sem.at[p - FIRST_FAR, flip, way], at(sign * lead_y, sign * lead_x, 0)).start()
-        for turn, indices in ((5, (PAIR, 3)), (6, (4, 5)), (7, (0, 1))):
-            @pl.when(g == turn)
-            def _():
-                run_z_relays(*indices)
-        return carry
-
-    lax.fori_loop(0, len(GROUPS), expert_group, 0)
-
-    def combine(turn, carry):
-        off_y, off_x = (pick([PLACES[int(p, 16)][k] for p in ADD_ORDER], turn) for k in BOTH)
+    def combine(p, carry):
+        off_y, off_x = pick([a for a, _ in PLACES], p), pick([b for _, b in PLACES], p)
         homes = [line(at(-off_y, -off_x, q)) for q in BOTH]
         loads = []
         for q in BOTH:
@@ -333,9 +328,12 @@
             acc[:, pl.ds(col, n_cols)] += total
         return carry
 
-    lax.fori_loop(0, FIRST_FAR - 4, combine, 0)
+    run_z_relays(0, 1)
+    run_z_relays(PAIR, 3)
+    lax.fori_loop(0, N_NEAR, combine, 0)
+    run_z_relays(4, 5)
     run_z_relays(6)
-    lax.fori_loop(FIRST_FAR - 4, len(ADD_ORDER), combine, 0)
+    lax.fori_loop(N_NEAR, len(PLACES), combine, 0)
     y_ref[...] = acc[...].astype(jnp.bfloat16)
 
     for part in BOTH:
@@ -688,13 +686,24 @@
 
     enter_all(n_cp, n_tp)
 
+    sibling = PAIR * x_pos + 1 - core
+
+    def wo_copy(src, slot, sem, to_tp):
+        return pltpu.make_async_remote_copy(src, wo_buf.at[slot], swo_sem.at[sem], rwo_sem.at[sem], device_id=mesh_id(cp_pos, to_tp),
+                                            device_id_type=MESH)
+
     def wo_send(step):
-        return pltpu.make_async_remote_copy(wo_hbm, wo_buf.at[tp_pos], swo_sem.at[step], rwo_sem.at[step],
-                                            device_id=mesh_id(cp_pos, (tp_pos + step) % n_tp), device_id_type=MESH)
-
-    def wo_arrival(step):
-        return pltpu.make_async_remote_copy(wo_hbm, wo_buf.at[(tp_pos + n_tp - step) % n_tp], swo_sem.at[step], rwo_sem.at[step],
-                                            device_id=mesh_id(cp_pos, tp_pos), device_id_type=MESH)
+        to_tp = PAIR * ((x_pos + step) % n_x) + core if step else sibling
+        return wo_copy(wo_hbm, tp_pos, step, to_tp)
+
+    def wo_pass(step):
+        slot = PAIR * ((x_pos + n_x - step) % n_x) + core
+        return wo_copy(wo_buf.at[slot], slot, n_x + step, sibling)
+
+    def run_wo_passes():
+        for step in range(1, n_x):
+            wo_send(step).wait_recv()
+            wo_pass(step).start()
 
     keep = wgx_hbm.shape[0]
     swaps = [pltpu.make_async_remote_copy(src.at[pl.ds((1 - core) * keep, keep)], dst, sw_sem.at[i], rw_sem.at[i],
@@ -705,7 +714,7 @@
         for part, place in enumerate((((cp_pos + off + n_cp) % n_cp, tp_pos), (cp_pos, PAIR * ((x_pos + off + n_x) % n_x) + core))):
             ranks.append(pltpu.make_async_remote_copy(rank_hbm, near_hbm.at[part, slot], sr_sem.at[part, slot], rr_sem.at[part, slot],
                                                       device_id=mesh_id(*place), device_id_type=MESH))
-    for step in range(1, n_tp):
+    for step in range(n_x):
         wo_send(step).start()
     for one in swaps + ranks:
         one.start()
@@ -739,6 +748,10 @@
 
     def query_pair(turn, carry):
         g = (turn + 1 + cp_pos + x_pos // PAIR * (PAIR * n_cp - 1 - PAIR * cp_pos)) % (n_dev // 4)
+
+        @pl.when(turn == n_dev // 4 - 2)
+        def _():
+            run_wo_passes()
         q_rows = q_buf[pl.ds(pl.multiple_of(g * PAIR * tok_dev, PAIR * tok_dev), PAIR * tok_dev), :]
         qt_buf[...] = q_rows.astype(jnp.float32).T.astype(jnp.bfloat16)
         m_ref[...] = jnp.full_like(m_ref, -1e30)
@@ -823,8 +836,9 @@
 
     lax.fori_loop(0, n_dev // 4, query_pair, 0)
 
-    for step in range(1, n_tp):
-        wo_arrival(step).wait_recv()
+    wo_send(0).wait_recv()
+    for step in range(1, n_x):
+        wo_pass(step).wait_recv()
     for one in loads[3:]:
         one.wait()
     for j in range(n_heads):
@@ -841,8 +855,10 @@
         h_cols = (x_buf[:, cols].astype(jnp.float32) + jnp.dot(o_rows, w_cols, preferred_element_type=jnp.float32)).astype(jnp.bfloat16)
         h_ref[PAIR * col // hid, :, pl.ds(col % (hid // PAIR), n_cols)] = h_cols
 
-    for step in range(1, n_tp):
+    for step in range(n_x):
         wo_send(step).wait_send()
+    for step in range(1, n_x):
+        wo_pass(step).wait_send()
     for one in swaps + ranks:
         one.wait()
 

time: 605 us -> 594 us (0.982)
  Pallas kernels: 592 us -> 581 us
    pallas_call x1, Pallas kernels: 358 us -> 348 us  [moe_call(): pl.pallas_call(functools.partial(moe_kernel, n_cp, n_tp, group), name='ro...]
where the time goes in v6:
time: 594 us; the launch traced here: 593 us
  Pallas kernels  581 us (98%)
  local copies, waits for them, and re-layouts  8.76 us (1%)
    pallas_call x1, Pallas kernels, moe_call(): pl.pallas_call(functools.partial(moe_kernel, n_cp, n_tp, group), name='ro...  348 us
    pallas_call x1, Pallas kernels, attend_call(): pl.pallas_call(functools.partial(attend_kernel, n_cp, n_tp), name='attend...  134 us
    pallas_call x1, Pallas kernels, front_call(): pl.pallas_call(functools.partial(front_kernel, n_cp, n_tp, n_part), name=...  98.2 us

profile of v6, /device:TPU:99, one launch (start us, length us, event | category | flops | bytes accessed | tf_op | source)
XLA Modules:
  0.0 593.3 jit_solution(6758591135067380568)
XLA Ops:
  0.0 1.1 fusion
  1.1 0.8 convolution_select_fusion.rank_hbm
  1.9 1.7 select_reduce_fusion.gate_ref
  3.6 2.3 copy.17
  6.0 3.3 copy_bitcast_fusion
  9.2 98.2 %gather_project.1 = (bf16[16384,128]{1,0:T(8,128)(2,1)}, bf16[128,16384]{1,0:T(8,128)(2,1)}, bf16[8192,128]{1,0:T(8,128)(2,1)}) custom-call(bf16[512,2048]{1,0:T(8,128)(2,1)} %x_hbm.3, bf16[2048,256]{1,0:T(8,128)(2,1)} %bitcast.15, bf16[2048,256]{1,0:T(8,128)(2,1)} %get-tuple-element.24.wk_hbm, bf16[2048,256]{1,0:T(8,128)(2,1)} %get-tuple-element.23.wv_hbm), custom_call_target="tpu_custom_call" | custom-call | flops 12884901888 | bytes 67108864 | tf_op jit(solution)/shard_map/gather_project/pallas_call | solution.py:633
  107.4 134.4 %attend_heads.1 = (bf16[2,512,1024]{2,1,0:T(8,128)(2,1)}, bf16[16,512,128]{2,1,0:T(8,128)(2,1)}, bf16[2,2048,512]{2,1,0:T(8,128)(2,1)}, bf16[2,2048,512]{2,1,0:T...) custom-call(bf16[16384,128]{1,0:T(8,128)(2,1)} %get-tuple-element.14.k_hbm, ...), custom_call_target="tpu_custom_call" | custom-call | flops 34359738368 | bytes 67108864 | tf_op jit(solution)/shard_map/attend_heads/pallas_call | solution.py:880
  241.8 348.3 %routed_experts.1 = (bf16[512,2048]{1,0:T(8,128)(2,1)}, bf16[2,32,128,1024]{3,2,1,0:T(8,128)(2,1)}, bf16[2,2,4,2,64,1024]{5,4,3,2,1,0:T(8,128)(2,1)}, bf16[32,12...) custom-call(bf16[2,512,1024]{2,1,0:T(8,128)(2,1)} %get-tuple-element.17.h_hbm, ...), custom_call_target="tpu_custom_call" | custom-call | flops 51539607552 | bytes 134217728 | tf_op jit(solution)/shard_map/routed_experts/pallas_call | solution.py:369
  590.1 3.2 copy.19

commit v7 on v6

--- a/solution.py
+++ b/solution.py
@@ -396,14 +396,20 @@
     )(h_loc, rank_rows, near_rows, gate_rows, w_gate, w_up, w_down, wg_other, wu_other, wd_other)[0]
 
 
-def routing_rows(ids_loc, gates_loc, n_experts):
-    tok_dev = ids_loc.shape[0]
-    chosen = ids_loc.T[None, :, :] == jnp.arange(n_experts, dtype=ids_loc.dtype)[:, None, None]
-    mask = jnp.any(chosen, axis=1)
-    gate_rows = jnp.sum(jnp.where(chosen, gates_loc.T[None, :, :], 0.0), axis=1)
-    before = jnp.triu(jnp.ones((tok_dev, tok_dev), jnp.bfloat16), 1)
-    rank = jnp.dot(mask.astype(jnp.bfloat16), before, preferred_element_type=jnp.float32)
-    return jnp.where(mask, rank, -1.0), gate_rows
+def routing_rows(ids_ref, gates_ref, rank_ref, gate_ref):
+    top_k, tok_dev = ids_ref.shape
+    ids, gates = ids_ref[...].astype(jnp.float32), gates_ref[...]
+    expert = lax.broadcasted_iota(jnp.int32, rank_ref.shape, 0).astype(jnp.float32)
+    chosen, weight = jnp.zeros_like(expert), jnp.zeros_like(expert)
+    for k in range(top_k):
+        hit = ids[k:k + 1] == expert
+        chosen = jnp.where(hit, 1.0, chosen)
+        weight = jnp.where(hit, gates[k:k + 1], weight)
+    token = lax.broadcasted_iota(jnp.int32, (tok_dev, tok_dev), 0)
+    before = jnp.where(token < lax.broadcasted_iota(jnp.int32, (tok_dev, tok_dev), 1), 1.0, 0.0).astype(jnp.bfloat16)
+    rank = jnp.dot(chosen.astype(jnp.bfloat16), before, preferred_element_type=jnp.float32)
+    rank_ref[...] = jnp.where(chosen > 0.0, rank, -1.0)
+    gate_ref[...] = weight
 
 
 def block_of(cp_pos, tp_pos, n_cp, n_tp):
@@ -420,7 +426,8 @@
     return late * (PAIR * n_cp - 1 - chunk) + (1 - late) * chunk, late * per_chunk + block % per_chunk
 
 
-def front_kernel(n_cp, n_tp, n_part, x_hbm, wq_hbm, wk_hbm, wv_hbm, k_hbm, vt_hbm, q_hbm, x_buf, w_buf, q_st, k_st, vt_st, k_far, vt_far, q_far,
+def front_kernel(n_cp, n_tp, n_part, x_hbm, wq_hbm, wk_hbm, wv_hbm, ids_ref, gates_ref, k_hbm, vt_hbm, q_hbm, rank_ref, gate_ref,
+                 x_buf, w_raw, w_buf, q_st, k_st, vt_st, k_far, vt_far, q_far,
                  own_sem, w_sem, ring_sem, pair_sem, rx_sem, sk_sem, sv_sem, sq_sem, kv_sem, rq_sem, sf_sem, rf_sem, far_sem, pass_sem):
     n_x = n_tp // PAIR
     tok_dev, hid = x_hbm.shape
@@ -439,7 +446,7 @@
     own_copy = pltpu.make_async_copy(x_hbm, x_buf.at[tp_pos], own_sem)
     own_copy.start()
     width = n_loc * head_dim
-    w_loads = [pltpu.make_async_copy(w, w_buf.at[:, pl.ds(i * width, width)], w_sem.at[i]) for i, w in enumerate((wq_hbm, wk_hbm, wv_hbm))]
+    w_loads = [pltpu.make_async_copy(w, w_raw.at[i], w_sem.at[i]) for i, w in enumerate((wq_hbm, wk_hbm, wv_hbm))]
     for one in w_loads:
         one.start()
     for step in (1, n_x - 1):
@@ -468,6 +475,18 @@
     for part in range(n_part):
         own_send(part, sibling, pair_sem.at[part]).start()
     first = PAIR * n_part
+    for one in w_loads:
+        one.wait()
+    rows_once = min(256, hid)
+
+    def widen(r, carry):
+        rows = pl.ds(pl.multiple_of(r * rows_once, rows_once), rows_once)
+        for i in range(len(w_loads)):
+            w_buf[rows, pl.ds(i * width, width)] = w_raw[i, rows].reshape(rows_once, width)
+        return carry
+
+    lax.fori_loop(0, hid // rows_once, widen, 0)
+    routing_rows(ids_ref, gates_ref, rank_ref, gate_ref)
 
     def place_of(step):
         late = jnp.minimum(step // first, 1)
@@ -534,8 +553,6 @@
         @pl.when(step == 0)
         def _():
             own_copy.wait()
-            for one in w_loads:
-                one.wait()
 
         @pl.when(step >= n_part)
         def _():
@@ -623,22 +640,25 @@
                     forward(y, place, 1 - core_id).wait_recv()
 
 
-def front_call(n_cp, n_tp, x_loc, w_parts, head_dim, n_loc):
+def front_call(n_cp, n_tp, x_loc, w_parts, ids_loc, gates_loc, n_experts):
+    _, n_loc, head_dim = w_parts[0].shape
     tok_dev, hid = x_loc.shape
     n_part, n_x = 4, n_tp // PAIR
     half = tok_dev // n_part
     seq = tok_dev * n_cp * n_tp
     any_spec = pl.BlockSpec(memory_space=pl.ANY)
     n_steps = n_part * n_tp
+    vmem_spec = pl.BlockSpec(memory_space=pltpu.VMEM)
     return pl.pallas_call(
         functools.partial(front_kernel, n_cp, n_tp, n_part),
         name="gather_project",
         out_shape=(jax.ShapeDtypeStruct((seq, head_dim), jnp.bfloat16), jax.ShapeDtypeStruct((head_dim, seq), jnp.bfloat16),
-                   jax.ShapeDtypeStruct((seq // PAIR, head_dim), jnp.bfloat16)),
-        in_specs=[any_spec] * 4,
-        out_specs=(any_spec,) * 3,
+                   jax.ShapeDtypeStruct((seq // PAIR, head_dim), jnp.bfloat16)) + (jax.ShapeDtypeStruct((n_experts, tok_dev), jnp.float32),) * 2,
+        in_specs=[any_spec] * 4 + [vmem_spec] * 2,
+        out_specs=(any_spec,) * 3 + (vmem_spec,) * 2,
         scratch_shapes=[
             pltpu.VMEM((n_tp, tok_dev, hid), jnp.bfloat16),
+            pltpu.VMEM((3, hid, n_loc, head_dim), jnp.bfloat16),
             pltpu.VMEM((hid, 3 * n_loc * head_dim), jnp.bfloat16),
             pltpu.VMEM((n_steps, n_loc, half, head_dim), jnp.bfloat16),
             pltpu.VMEM((n_steps, n_loc, half, head_dim), jnp.bfloat16),
@@ -663,7 +683,7 @@
         ],
         compiler_params=pltpu.CompilerParams(collective_id=0, has_side_effects=True, vmem_limit_bytes=VMEM_LIMIT),
         cost_estimate=pl.CostEstimate(flops=PAIR * n_tp * tok_dev * hid * 3 * n_loc * head_dim, bytes_accessed=2**26, transcendentals=0),
-    )(x_loc, *w_parts)
+    )(x_loc, *w_parts, ids_loc, gates_loc)
 
 
 def attend_kernel(n_cp, n_tp, k_hbm, vt_hbm, q_hbm, x_hbm, wo_hbm, wg_hbm, wu_hbm, wd_hbm, rank_hbm,
@@ -933,9 +953,7 @@
         n_loc, head_dim = w_q.shape[1:]
         n_experts = w_gate.shape[0] * n_cp * n_tp // PAIR
         capacity = ids_loc.shape[1] * tok_dev // n_experts
-        w_parts = [w.reshape(hid_dim, n_loc * head_dim) for w in (w_q, w_k, w_v)]
-        rank_rows, gate_rows = routing_rows(ids_loc, gates_loc, n_experts)
-        k_all, vt_all, q_all = front_call(n_cp, n_tp, x_loc, w_parts, head_dim, n_loc)
+        k_all, vt_all, q_all, rank_rows, gate_rows = front_call(n_cp, n_tp, x_loc, (w_q, w_k, w_v), ids_loc.T, gates_loc.T, n_experts)
         h_loc, near_rows, *others = attend_call(n_cp, n_tp, k_all, vt_all, q_all, x_loc, w_o.reshape(n_loc * head_dim, hid_dim), w_gate, w_up, w_down, rank_rows)
         return moe_call(n_cp, n_tp, capacity, h_loc, rank_rows, near_rows, gate_rows, w_gate, w_up, w_down, *others)
 

time: 594 us -> 586 us (0.987)
  no operation moved by 1% of the time
where the time goes in v7:
time: 586 us; the launch traced here: 585 us
  Pallas kernels  582 us (99%)
    pallas_call x1, Pallas kernels, moe_call(): pl.pallas_call(functools.partial(moe_kernel, n_cp, n_tp, group), name='ro...  348 us
    pallas_call x1, Pallas kernels, attend_call(): pl.pallas_call(functools.partial(attend_kernel, n_cp, n_tp), name='attend...  134 us
    pallas_call x1, Pallas kernels, front_call(): pl.pallas_call(functools.partial(front_kernel, n_cp, n_tp, n_part), name=...  99.6 us

profile of v7, /device:TPU:99, one launch (start us, length us, event | category | flops | bytes accessed | tf_op | source)
XLA Modules:
  0.0 585.4 jit_solution(10128698080987340634)
XLA Ops:
  0.0 99.6 %gather_project.1 = (bf16[16384,128]{1,0:T(8,128)(2,1)}, bf16[128,16384]{1,0:T(8,128)(2,1)}, bf16[8192,128]{1,0:T(8,128)(2,1)}, f32[64,512]{1,0:T(8,128)}, f32[64,512]{1,0:T(8,128)}) custom-call(bf16[512,2048]{1,0:T(8,128)(2,1)} %x_hbm.3, bf16[2048,2,128]{2,1,0:T(2,128)(2,1)} %wq_hbm.1, bf16[2048,2,128]{2,1,0:T(2,128)(2,1)} %wk_hbm.1, ...), custom_call_target="tpu_custom_call" | custom-call | flops 12884901888 | bytes 67108864 | tf_op jit(solution)/shard_map/gather_project/pallas_call | solution.py:652
  99.6 134.4 %attend_heads.1 = (bf16[2,512,1024]{2,1,0:T(8,128)(2,1)}, bf16[16,512,128]{2,1,0:T(8,128)(2,1)}, bf16[2,2048,512]{2,1,0:T(8,128)(2,1)}, bf16[2,2048,512]{2,1,0:T...) custom-call(bf16[16384,128]{1,0:T(8,128)(2,1)} %get-tuple-element.16.k_hbm, ...), custom_call_target="tpu_custom_call" | custom-call | flops 34359738368 | bytes 67108864 | tf_op jit(solution)/shard_map/attend_heads/pallas_call | solution.py:900
  234.0 348.3 %routed_experts.1 = (bf16[512,2048]{1,0:T(8,128)(2,1)}, bf16[2,32,128,1024]{3,2,1,0:T(8,128)(2,1)}, bf16[2,2,4,2,64,1024]{5,4,3,2,1,0:T(8,128)(2,1)}, bf16[32,12...) custom-call(bf16[2,512,1024]{2,1,0:T(8,128)(2,1)} %get-tuple-element.20.h_hbm, f32[64,512]{1,0:T(8,128)} %get-tuple-element.19.rank_hbm, ...), custom_call_target="tpu_custom_call" | custom-call | flops 51539607552 | bytes 134217728 | tf_op jit(solution)/shard_map/routed_experts/pallas_call | solution.py:369
  582.3 3.2 copy.12

commit v8 on v7

--- a/solution.py
+++ b/solution.py
@@ -17,8 +17,8 @@
 VMEM_LIMIT = 66_000_000
 PLACES = ((0, 0), (0, 1), (1, 0), (0, -1), (-1, 0), (1, 1), (-1, -1), (1, -1), (-1, 1), (0, PAIR), (PAIR, 0), (1, PAIR), (PAIR, 1), (-1, PAIR), (PAIR, -1), (PAIR, PAIR))
 N_NEAR, FIRST_FAR = 5, 9
-GROUPS = ("1234", "1234", "9a9a", "bcbc", "dede", "0f0f", "5656", "7878")
-FLIPS = ("0000", "1111") + ("0011",) * 6
+GROUPS = ("1234", "9a9a", "5656", "bcbc", "1234", "dede", "7878", "0f0f")
+FLIPS = ("0000", "0011", "0011", "0011", "1111", "0011", "0011", "0011")
 SOURCES = (0, -1, 1, PAIR)
 
 
@@ -808,7 +808,7 @@
             if 0 <= i - 2:
                 near_values(i - 2)
         shrink_odd[...] = jnp.ones_like(shrink_odd)
-        strip = min(256, tok_dev)
+        strip = min(512, tok_dev)
         strips = [pl.ds(lo, strip) for lo in range(0, PAIR * tok_dev, strip)]
 
         def far_step(block, parity, tops):

time: 586 us -> 580 us (0.990)
  Pallas kernels: 582 us -> 574 us
    pallas_call x1, Pallas kernels: 348 us -> 341 us  [moe_call(): pl.pallas_call(functools.partial(moe_kernel, n_cp, n_tp, group), name='ro...]
where the time goes in v8:
time: 580 us; the launch traced here: 578 us
  Pallas kernels  574 us (99%)
    pallas_call x1, Pallas kernels, moe_call(): pl.pallas_call(functools.partial(moe_kernel, n_cp, n_tp, group), name='ro...  341 us
    pallas_call x1, Pallas kernels, attend_call(): pl.pallas_call(functools.partial(attend_kernel, n_cp, n_tp), name='attend...  134 us
    pallas_call x1, Pallas kernels, front_call(): pl.pallas_call(functools.partial(front_kernel, n_cp, n_tp, n_part), name=...  99.6 us

profile of v8, /device:TPU:99, one launch (start us, length us, event | category | flops | bytes accessed | tf_op | source)
XLA Modules:
  0.0 577.6 jit_solution(15737650403776241539)
XLA Ops:
  0.0 99.6 %gather_project.1 = (bf16[16384,128]{1,0:T(8,128)(2,1)}, bf16[128,16384]{1,0:T(8,128)(2,1)}, bf16[8192,128]{1,0:T(8,128)(2,1)}, f32[64,512]{1,0:T(8,128)}, f32[64,512]{1,0:T(8,128)}) custom-call(bf16[512,2048]{1,0:T(8,128)(2,1)} %x_hbm.3, bf16[2048,2,128]{2,1,0:T(2,128)(2,1)} %wq_hbm.1, bf16[2048,2,128]{2,1,0:T(2,128)(2,1)} %wk_hbm.1, ...), custom_call_target="tpu_custom_call" | custom-call | flops 12884901888 | bytes 67108864 | tf_op jit(solution)/shard_map/gather_project/pallas_call | solution.py:652
  99.6 134.3 %attend_heads.1 = (bf16[2,512,1024]{2,1,0:T(8,128)(2,1)}, bf16[16,512,128]{2,1,0:T(8,128)(2,1)}, bf16[2,2048,512]{2,1,0:T(8,128)(2,1)}, bf16[2,2048,512]{2,1,0:T...) custom-call(bf16[16384,128]{1,0:T(8,128)(2,1)} %get-tuple-element.16.k_hbm, ...), custom_call_target="tpu_custom_call" | custom-call | flops 34359738368 | bytes 67108864 | tf_op jit(solution)/shard_map/attend_heads/pallas_call | solution.py:900
  233.9 340.5 %routed_experts.1 = (bf16[512,2048]{1,0:T(8,128)(2,1)}, bf16[2,32,128,1024]{3,2,1,0:T(8,128)(2,1)}, bf16[2,2,4,2,64,1024]{5,4,3,2,1,0:T(8,128)(2,1)}, bf16[32,12...) custom-call(bf16[2,512,1024]{2,1,0:T(8,128)(2,1)} %get-tuple-element.20.h_hbm, f32[64,512]{1,0:T(8,128)} %get-tuple-element.19.rank_hbm, ...), custom_call_target="tpu_custom_call" | custom-call | flops 51539607552 | bytes 134217728 | tf_op jit(solution)/shard_map/routed_experts/pallas_call | solution.py:369
  574.5 3.2 copy.12

commit v9 on v8

--- a/solution.py
+++ b/solution.py
@@ -17,8 +17,8 @@
 VMEM_LIMIT = 66_000_000
 PLACES = ((0, 0), (0, 1), (1, 0), (0, -1), (-1, 0), (1, 1), (-1, -1), (1, -1), (-1, 1), (0, PAIR), (PAIR, 0), (1, PAIR), (PAIR, 1), (-1, PAIR), (PAIR, -1), (PAIR, PAIR))
 N_NEAR, FIRST_FAR = 5, 9
-GROUPS = ("1234", "9a9a", "5656", "bcbc", "1234", "dede", "7878", "0f0f")
-FLIPS = ("0000", "0011", "0011", "0011", "1111", "0011", "0011", "0011")
+GROUPS = ("1234", "bcbc", "5656", "dede", "7878", "0f0f", "9a9a", "1234")
+FLIPS = ("0000",) + ("0011",) * 6 + ("1111",)
 SOURCES = (0, -1, 1, PAIR)
 
 
@@ -328,11 +328,11 @@
             acc[:, pl.ds(col, n_cols)] += total
         return carry
 
+    run_z_relays(PAIR, 3)
+    run_z_relays(4, 5)
+    lax.fori_loop(0, N_NEAR, combine, 0)
+    run_z_relays(6)
     run_z_relays(0, 1)
-    run_z_relays(PAIR, 3)
-    lax.fori_loop(0, N_NEAR, combine, 0)
-    run_z_relays(4, 5)
-    run_z_relays(6)
     lax.fori_loop(N_NEAR, len(PLACES), combine, 0)
     y_ref[...] = acc[...].astype(jnp.bfloat16)
 

time: 580 us -> 599 us (1.033)
  Pallas kernels: 574 us -> 592 us
    pallas_call x1, Pallas kernels: 341 us -> 358 us  [moe_call(): pl.pallas_call(functools.partial(moe_kernel, n_cp, n_tp, group), name='ro...]
where the time goes in v9:
time: 599 us; the launch traced here: 595 us
  Pallas kernels  592 us (99%)
    pallas_call x1, Pallas kernels, moe_call(): pl.pallas_call(functools.partial(moe_kernel, n_cp, n_tp, group), name='ro...  358 us
    pallas_call x1, Pallas kernels, attend_call(): pl.pallas_call(functools.partial(attend_kernel, n_cp, n_tp), name='attend...  134 us
    pallas_call x1, Pallas kernels, front_call(): pl.pallas_call(functools.partial(front_kernel, n_cp, n_tp, n_part), name=...  99.6 us

profile of v9, /device:TPU:99, one launch (start us, length us, event | category | flops | bytes accessed | tf_op | source)
XLA Modules:
  0.0 594.8 jit_solution(13060277437064503134)
XLA Ops:
  0.0 99.6 %gather_project.1 = (bf16[16384,128]{1,0:T(8,128)(2,1)}, bf16[128,16384]{1,0:T(8,128)(2,1)}, bf16[8192,128]{1,0:T(8,128)(2,1)}, f32[64,512]{1,0:T(8,128)}, f32[64,512]{1,0:T(8,128)}) custom-call(bf16[512,2048]{1,0:T(8,128)(2,1)} %x_hbm.3, bf16[2048,2,128]{2,1,0:T(2,128)(2,1)} %wq_hbm.1, bf16[2048,2,128]{2,1,0:T(2,128)(2,1)} %wk_hbm.1, ...), custom_call_target="tpu_custom_call" | custom-call | flops 12884901888 | bytes 67108864 | tf_op jit(solution)/shard_map/gather_project/pallas_call | solution.py:652
  99.6 134.3 %attend_heads.1 = (bf16[2,512,1024]{2,1,0:T(8,128)(2,1)}, bf16[16,512,128]{2,1,0:T(8,128)(2,1)}, bf16[2,2048,512]{2,1,0:T(8,128)(2,1)}, bf16[2,2048,512]{2,1,0:T...) custom-call(bf16[16384,128]{1,0:T(8,128)(2,1)} %get-tuple-element.16.k_hbm, ...), custom_call_target="tpu_custom_call" | custom-call | flops 34359738368 | bytes 67108864 | tf_op jit(solution)/shard_map/attend_heads/pallas_call | solution.py:900
  233.9 357.7 %routed_experts.1 = (bf16[512,2048]{1,0:T(8,128)(2,1)}, bf16[2,32,128,1024]{3,2,1,0:T(8,128)(2,1)}, bf16[2,2,4,2,64,1024]{5,4,3,2,1,0:T(8,128)(2,1)}, bf16[32,12...) custom-call(bf16[2,512,1024]{2,1,0:T(8,128)(2,1)} %get-tuple-element.20.h_hbm, f32[64,512]{1,0:T(8,128)} %get-tuple-element.19.rank_hbm, ...), custom_call_target="tpu_custom_call" | custom-call | flops 51539607552 | bytes 134217728 | tf_op jit(solution)/shard_map/routed_experts/pallas_call | solution.py:369
  591.6 3.2 copy.12
